TPU v7x, 128 devices: a whole 4x4x4 slice. The times are simulated.
128 devices in a mesh: section: 4 (over x), dp: 32 (over y, z, core).
Axes of the slice: x: 4, y: 4, z: 4, core: 2. Of those that a mesh axis runs over, the one named last changes fastest.
Arguments:
- clip_pool: bfloat16 [1024, 256, 512], P('dp'), may hold values from -8 to 8
- clip_index: int32 [8, 128], P(None, 'dp'), may hold values from 0 to 31, as said below
- batch_order: int32 [8], replicated, may hold values from 0 to 7, each once
- tap_weights: bfloat16 [4, 3, 512, 512], P('section'), may hold values from -0.15625 to 0.15625
- out_weights: bfloat16 [4, 512, 512], P('section'), may hold values from -0.25 to 0.25
- norm_gains: bfloat16 [4, 512], P('section'), may hold values from 0.099609375 to 1.8984375
- quant_weight: bfloat16 [512, 18], replicated, may hold values from -0.25 to 0.25
- quant_bias: float32 [18], replicated, may hold values from -3 to 3
- post_weight: bfloat16 [18, 512], replicated, may hold values from -1.5 to 1.5
Outputs:
- row_error: float32 [8, 128, 256], P('section', 'dp')
- entropy_loss: float32 [8], replicated
Inputs may be any that keep to these rules, and one draw needn't show every extreme that they name: `clip_index`: entries index the clips of the replica that holds the column; over all 8 micro-batches, the 4 columns of one replica name each of its 32 clips exactly once. `batch_order`: each micro-batch number 0 to 7 once.
All inputs are finite; a program needn't handle non-finite values.
Results may differ from a plain program's by a relative error of at most 0.0015.
Values may be sent and summed in bfloat16 or wider, within the bound.
No kernel may reach another device: no remote copies, remote signals or barrier semaphores. Data moves between devices by JAX's collectives and lax.ppermute only.
A program may use at most 128 MiB of HBM per device.

v0:
```python
import functools

import jax
import jax.numpy as jnp
from jax import lax
from jax.experimental import pallas as pl
from jax.experimental.pallas import tpu as pltpu
from jax.sharding import Mesh
from jax.sharding import PartitionSpec as P


DP = ("dp_0", "dp_1", "dp_2")
EPS = 1e-06
C = 512
BITS = 18
FRAME = 64
ROWS = 256
CLIPS = 4
FRAMES = ROWS // FRAME
CHUNKS = ((4, 0, 1, 6, 7), (None, 2, 3, 5, None), (4, 2, 3, 5, None), (None, 0, 1, 6, 7))
STEPS = len(CHUNKS[0])
CODE_ROWS = 24
HALF = 1024
PIECE = HALF + 16
VM = pl.BlockSpec(memory_space=pltpu.VMEM)
SM = pl.BlockSpec(memory_space=pltpu.SMEM)
HB = pl.BlockSpec(memory_space=pltpu.HBM)
ANY = pl.BlockSpec(memory_space=pl.ANY)


def call(body, ins, outs, scratch=(), limit=24, aliases={}, blocks=0):
    return pl.pallas_call(
        body,
        in_specs=list(ins),
        out_specs=[VM] * len(outs),
        out_shape=[jax.ShapeDtypeStruct(shape, kind) for shape, kind in outs],
        scratch_shapes=list(scratch),
        compiler_params=pltpu.CompilerParams(vmem_limit_bytes=limit * 2**20),
        input_output_aliases=aliases,
        cost_estimate=pl.CostEstimate(
            flops=blocks * CLIPS * ROWS * C * C * 8, transcendentals=0, bytes_accessed=0
        ),
    )


def run_block(src, dst, taps, out_weight, half_gain):
    frames = [
        src[:, f * FRAME : (f + 1) * FRAME, :].reshape(CLIPS * FRAME, C) for f in range(FRAMES)
    ]
    normed = []
    for v in frames:
        w = v.astype(jnp.float32)
        mean = jnp.mean(w * w, axis=-1, keepdims=True)
        normed.append((w * lax.rsqrt(mean + EPS) * half_gain).astype(jnp.bfloat16))
    first = jnp.dot(normed[0], taps(C), preferred_element_type=jnp.float32)
    second = jnp.dot(
        jnp.concatenate([normed[1], normed[0]], axis=1),
        taps(2 * C),
        preferred_element_type=jnp.float32,
    )
    rest = jnp.concatenate(
        [
            jnp.concatenate([normed[f], normed[f - 1], normed[f - 2]], axis=1)
            for f in range(2, FRAMES)
        ],
        axis=0,
    )
    third = jnp.dot(rest, taps(3 * C), preferred_element_type=jnp.float32)
    h = jnp.concatenate([first, second, third], axis=0)
    activated = (h + h * jnp.tanh(h)).astype(jnp.bfloat16)
    update = jnp.dot(activated, out_weight(), preferred_element_type=jnp.float32)
    for f in range(FRAMES):
        part = update[f * CLIPS * FRAME : (f + 1) * CLIPS * FRAME]
        dst[:, f * FRAME : (f + 1) * FRAME, :] = (
            (frames[f].astype(jnp.float32) + part)
            .astype(jnp.bfloat16)
            .reshape(CLIPS, FRAME, C)
        )


def prep_body(taps, out_weight, gain_hbm, piece, gain, sems):
    colour = lax.rem(lax.axis_index("dp_0") + 2 * lax.axis_index("dp_1"), 4)
    at = pl.ds(pl.multiple_of(colour * 128, 128), 128)
    core = lax.axis_index("dp_2")
    gain_copy = pltpu.make_async_copy(gain_hbm, gain, sems.at[5])
    gain_copy.start()

    @pl.when(core == 0)
    def _():
        copy = pltpu.make_async_copy(
            taps.at[pl.ds(0, HALF), at], piece.at[pl.ds(0, HALF)], sems.at[0]
        )
        copy.start()
        copy.wait()

    @pl.when(core == 1)
    def _():
        copies = [
            pltpu.make_async_copy(
                taps.at[pl.ds(HALF, 512), at], piece.at[pl.ds(0, 512)], sems.at[0]
            )
        ]
        for j in range(4):
            copies.append(
                pltpu.make_async_copy(
                    out_weight.at[at, pl.ds(128 * j, 128)],
                    piece.at[pl.ds(512 + 128 * j, 128)],
                    sems.at[1 + j],
                )
            )
        for copy in copies:
            copy.start()
        for copy in copies:
            copy.wait()

    gain_copy.wait()
    wide = gain[...].astype(jnp.float32)
    rows = [wide[:, 128 * j : 128 * (j + 1)] for j in range(4)]
    rows.append(jnp.zeros((12, 128), jnp.float32))
    piece[HALF:, :] = jnp.concatenate(rows, axis=0).astype(jnp.bfloat16)


def batch_of(t):
    section = lax.axis_index("section")
    batch = jnp.int32(0)
    for k in range(4):
        if CHUNKS[k][t] is not None:
            batch = jnp.where(section == k, CHUNKS[k][t], batch)
    return batch


def has_chunk(t, sections):
    section = lax.axis_index("section")
    found = [section == k for k in sections if CHUNKS[k][t] is not None]
    return functools.reduce(jnp.logical_or, found)


def start_body(
    steps, pool, index_hbm, taps, out_weight, gain_hbm, qwt_hbm, qbias_hbm, postw_hbm,
    v, all_taps, all_out, all_gain, qw, qb, post,
    index, gain, qwt, qbias, postw, sems,
):
    own = lax.rem(lax.axis_index("section"), 2)
    pairs = [
        (index_hbm, index),
        (taps, all_taps.at[own]),
        (out_weight, all_out.at[own]),
        (gain_hbm, gain),
        (qwt_hbm, qwt),
        (qbias_hbm, qbias),
        (postw_hbm, postw),
    ]
    small = [pltpu.make_async_copy(a, b, sems.at[k]) for k, (a, b) in enumerate(pairs)]
    for copy in small:
        copy.start()
    small[0].wait()
    copies = []
    for t in range(STEPS):
        batch = batch_of(t)
        for c in range(CLIPS):
            copy = pltpu.make_async_copy(
                pool.at[index[c, batch]], v.at[t, c], sems.at[len(pairs) + t * CLIPS + c]
            )
            copy.start()
            copies.append(copy)
    for copy in small[1:]:
        copy.wait()
    all_gain[own] = jnp.broadcast_to(0.5 * gain[...].astype(jnp.float32), (8, C))
    wide = jnp.concatenate(
        [qwt[...].astype(jnp.float32), jnp.zeros((128 - BITS, C), jnp.float32)], axis=0
    )
    qw[...] = wide.T.astype(jnp.bfloat16)
    qb[...] = jnp.zeros((8, 128), jnp.float32)
    qb[0:1, 0:BITS] = qbias[...]
    post[...] = jnp.zeros((CODE_ROWS, C), jnp.bfloat16)
    post[0:BITS, :] = postw[...]
    for copy in copies[: steps * CLIPS]:
        copy.wait()
    first_block(0, steps, v, all_taps, all_out, all_gain)
    for copy in copies[steps * CLIPS :]:
        copy.wait()


def first_block(begin, end, v, all_taps, all_out, all_gain):
    @pl.when(lax.axis_index("section") == 0)
    def _():
        def step(t, _):
            block_at(0, v.at[t], all_taps, all_out, all_gain)
            return 0

        lax.fori_loop(begin, end, step, 0)


def more_body(begin, end, before, all_taps, all_out, all_gain, v):
    first_block(begin, end, v, all_taps, all_out, all_gain)


def join_body(*refs):
    pieces, (all_taps, all_out, all_gain), sems = refs[:8], refs[11:14], refs[14]
    section = lax.axis_index("section")
    core = lax.axis_index("dp_2")
    other = 1 - lax.rem(section, 2)

    def place(lower, upper):
        copies = []
        for j in range(4):
            lanes = pl.ds(128 * j, 128)
            copies.append(
                pltpu.make_async_copy(
                    lower[j].at[pl.ds(0, HALF)],
                    all_taps.at[other, pl.ds(0, HALF), lanes],
                    sems.at[j],
                )
            )
            copies.append(
                pltpu.make_async_copy(
                    upper[j].at[pl.ds(0, 512)],
                    all_taps.at[other, pl.ds(HALF, 512), lanes],
                    sems.at[4 + j],
                )
            )
            for k in range(4):
                copies.append(
                    pltpu.make_async_copy(
                        upper[j].at[pl.ds(512 + 128 * k, 128)],
                        all_out.at[other, pl.ds(128 * j, 128), pl.ds(128 * k, 128)],
                        sems.at[8 + 4 * j + k],
                    )
                )
        for copy in copies:
            copy.start()
        for copy in copies:
            copy.wait()

    @pl.when(core == 0)
    def _():
        place(pieces[:4], pieces[4:])

    @pl.when(core == 1)
    def _():
        place(pieces[4:], pieces[:4])

    rows = pieces[0][HALF:, :].astype(jnp.float32)
    row = jnp.concatenate([rows[k : k + 1, :] for k in range(4)], axis=1)
    all_gain[other] = jnp.broadcast_to(0.5 * row, (8, C))


def block_at(b, buf, all_taps, all_out, all_gain):
    run_block(
        buf,
        buf,
        lambda k: all_taps[b, :k, :],
        lambda: all_out[b],
        all_gain[b, 0:1, :],
    )


def encode_body(steps, last, v, all_taps, all_out, all_gain, qw, qb, *rest):
    section = lax.axis_index("section")
    codes, stats, buf, sums = rest[-4:]
    sums[...] = rest[0][...] if len(rest) > 4 else jnp.zeros_like(sums)
    row = lax.broadcasted_iota(jnp.int32, (CODE_ROWS, CLIPS * ROWS), 0)
    top = lax.broadcasted_iota(jnp.int32, (CODE_ROWS, 128), 0)
    lane = lax.broadcasted_iota(jnp.int32, (CODE_ROWS, 128), 1)

    def chunk(i, t):
        buf[...] = v[t]

        def step(b, _):
            block_at(b, buf, all_taps, all_out, all_gain)
            return 0

        lax.fori_loop(1 - section, 2, step, 0)
        logits = jnp.dot(
            buf[...].reshape(CLIPS * ROWS, C), qw[...], preferred_element_type=jnp.float32
        )
        z = (4.0 * (logits + qb[0:1, :])).T[:CODE_ROWS]
        size = jnp.abs(z)
        e = jnp.exp(-size)
        r = 1.0 / (1.0 + e)
        p = jnp.where(z >= 0, r, e * r)
        entropy = jnp.log1p(e) + size * (e * r)
        valid = row < BITS
        codes[i] = jnp.where(valid, 2.0 * p - 1.0, 0.0).astype(jnp.bfloat16)
        bit_sums = jnp.sum(jnp.where(valid, p, 0.0), axis=1, keepdims=True)
        total = jnp.sum(
            jnp.sum(jnp.where(valid, entropy, 0.0), axis=1, keepdims=True), axis=0, keepdims=True
        )
        column = jnp.where(top == BITS, total, bit_sums)
        sums[...] += jnp.where(lane == batch_of(t), column, 0.0)

    for i, t in enumerate(steps):
        pl.when(has_chunk(t, (0, 1)))(functools.partial(chunk, i, t))

    if last:
        full = jnp.concatenate([sums[...], jnp.zeros((128 - CODE_ROWS, 128), jnp.float32)], axis=0)
        stats[...] = full.T[:8]
    else:
        stats[...] = sums[...]


def decode_body(steps, v, all_taps, all_out, all_gain, post, codes, errors, buf):
    def chunk(i, t):
        quantized = lax.dot_general(
            codes[i], post[...], (((0,), (0,)), ((), ())), preferred_element_type=jnp.float32
        )
        buf[...] = quantized.astype(jnp.bfloat16).reshape(CLIPS, ROWS, C)

        def step(b, _):
            block_at(b, buf, all_taps, all_out, all_gain)
            return 0

        lax.fori_loop(0, 2, step, 0)
        for c in range(CLIPS):
            differ = buf[c].astype(jnp.float32) - v[t, c].astype(jnp.float32)
            square = differ * differ
            part = (
                square[:, :128] + square[:, 128:256] + square[:, 256:384] + square[:, 384:]
            )
            mean = jnp.sum(part.T, axis=0, keepdims=True) * (1.0 / C)
            errors[i, 2 * c : 2 * c + 1, :] = mean[:, :128]
            errors[i, 2 * c + 1 : 2 * c + 2, :] = mean[:, 128:]

    for i, t in enumerate(steps):
        pl.when(has_chunk(t, (2, 3)))(functools.partial(chunk, i, t))


def unpack(target, source):
    for c in range(CLIPS):
        row = source[2 * c : 2 * c + 2, :]
        target[c : c + 1, :] = jnp.concatenate([row[0:1], row[1:2]], axis=1)


def final_body(rows_total, order, mine, next_, cross, far, e0, e34, error, loss):
    section = lax.axis_index("section")
    a, b, c, d = mine[0:8], next_[0:8], cross[0:8], far[0:8]
    sums = (jnp.where(section <= 1, a + b, c + d)) * (1.0 / rows_total)
    row = lax.broadcasted_iota(jnp.int32, sums.shape, 0)
    lane = lax.broadcasted_iota(jnp.int32, sums.shape, 1)
    averaged = jnp.zeros_like(sums)
    running = None
    for t in range(8):
        here = row == order[t]
        marginal = jnp.sum(jnp.where(here, sums, 0.0), axis=0, keepdims=True)
        running = marginal if t == 0 else 0.5 * running + 0.5 * marginal
        averaged = jnp.where(here, running, averaged)
    smoothed = jnp.where(lane < BITS, 0.05 + 0.9 * averaged, 0.5)
    term = smoothed * jnp.log(smoothed) + (1.0 - smoothed) * jnp.log(1.0 - smoothed)
    term = jnp.where(lane < BITS, term, jnp.where(lane == BITS, sums, 0.0))
    result = jnp.sum(term, axis=1, keepdims=True)
    loss[...] = jnp.sum(jnp.where(row == lane, result, 0.0), axis=0, keepdims=True)

    @pl.when(section <= 1)
    def _():
        unpack(error.at[0], cross.at[pl.ds(8, 8)])
        unpack(error.at[1], cross.at[pl.ds(16, 8)])

    @pl.when(section == 2)
    def _():
        unpack(error.at[0], e0.at[0])
        unpack(error.at[1], e34.at[0])

    @pl.when(section == 3)
    def _():
        unpack(error.at[0], e34.at[0])
        unpack(error.at[1], e34.at[1])


PAIR = ((0, 1), (1, 0), (2, 3), (3, 2))
CROSS = ((0, 3), (3, 0), (1, 2), (2, 1))
FAR = ((0, 2), (2, 0), (1, 3), (3, 1))


def shifted(x, axis, by):
    n = lax.axis_size(axis)
    return lax.ppermute(x, axis, [(i, (i + by) % n) for i in range(n)])


def split_shift(x, axis):
    n = lax.axis_size(axis)
    pairs = []
    for i in range(n):
        pairs.append((2 * i, 2 * ((i + 1) % n)))
        pairs.append((2 * i + 1, 2 * ((i - 1) % n) + 1))
    return lax.ppermute(x, (axis, "dp_2"), pairs)


def plane_sum(x):
    n = lax.axis_size(DP)
    return jnp.sum(lax.all_to_all(jnp.broadcast_to(x[None], (n, *x.shape)), DP, 0, 0), axis=0)


def on_device(pool, index, order, taps, out_weight, gain, quant_weight, quant_bias, post_weight):
    bf16, f32 = jnp.bfloat16, jnp.float32
    taps = taps.reshape(3 * C, C)
    out_weight = out_weight.reshape(C, C)
    dma = pltpu.SemaphoreType.DMA
    index = index.T
    encoder = (lax.axis_index("section") <= 1).astype(jnp.int32)
    gain, encoder = lax.optimization_barrier((gain, encoder))
    chunk = (CLIPS, ROWS, C)
    kinds = [((2, 3 * C, C), bf16), ((2, C, C), bf16), ((2, 8, C), f32)]

    pool, taps, out_weight = (
        pltpu.with_memory_space_constraint(x, pltpu.HBM) for x in (pool, taps, out_weight)
    )
    gain, qwt, post_weight, index = (
        pltpu.with_memory_space_constraint(x, pltpu.HBM)
        for x in (gain, quant_weight.T, post_weight, index)
    )
    qbias = pltpu.with_memory_space_constraint(quant_bias.reshape(1, BITS), pltpu.HBM)
    (piece,) = call(
        prep_body, [HB] * 3, [((PIECE, 128), bf16)], [pltpu.VMEM((1, C), bf16), dma((6,))]
    )(taps, out_weight, gain)
    mine = lax.ppermute(piece, "section", PAIR)
    v_kind = ((STEPS, *chunk), bf16)
    v, *weights, qw, qb, post = call(
        functools.partial(start_body, 2),
        [HB] * 8,
        [v_kind, *kinds, ((C, 128), bf16), ((8, 128), f32), ((CODE_ROWS, C), bf16)],
        [
            pltpu.SMEM(index.shape, jnp.int32),
            pltpu.VMEM((1, C), bf16),
            pltpu.VMEM((BITS, C), bf16),
            pltpu.VMEM((1, BITS), f32),
            pltpu.VMEM((BITS, C), bf16),
            dma((7 + STEPS * CLIPS,)),
        ],
        blocks=2,
    )(pool, index, taps, out_weight, gain, qwt, qbias, post_weight)
    mine, v = lax.optimization_barrier((mine, v))
    up = shifted(mine, "dp_0", 1)
    down = shifted(mine, "dp_0", -1)
    side = split_shift(mine, "dp_1")
    mine_s = shifted(mine, "dp_2", 1)
    (v,) = call(
        functools.partial(more_body, 2, STEPS), [VM] * 4, [v_kind], blocks=3, aliases={0: 0}
    )(v, *weights)
    up, down, side, mine_s, v = lax.optimization_barrier((up, down, side, mine_s, v))
    swapped = [mine_s] + [shifted(x, "dp_2", 1) for x in (up, down, side)]
    weights = call(
        join_body, [VM] + [ANY] * 7 + [VM] * 3, kinds, [dma((24,))], aliases={8: 0, 9: 1, 10: 2}
    )(mine, up, down, side, *swapped, *weights)

    def encode(steps, before, last):
        n = len(steps)
        return call(
            functools.partial(encode_body, steps, last),
            [VM] * (6 + len(before)),
            [((n, CODE_ROWS, CLIPS * ROWS), bf16), ((8 if last else CODE_ROWS, 128), f32)],
            [pltpu.VMEM(chunk, bf16), pltpu.VMEM((CODE_ROWS, 128), f32)],
            blocks=2 * n,
        )(v, *weights, qw, qb, *before)

    def decode(steps, codes):
        n = len(steps)
        return call(
            functools.partial(decode_body, steps),
            [VM] * 6,
            [((n, 8, 128), f32)],
            [pltpu.VMEM(chunk, bf16)],
            blocks=2 * n,
        )(v, *weights, post, codes)[0]

    to_cross = ((0, 3), (1, 2))
    codes, stats = encode((0,), (), False)
    codes_a = lax.ppermute(codes, "section", ((0, 2),))
    codes, stats = encode((1, 2), (stats,), False)
    codes_b = lax.ppermute(codes, "section", to_cross)
    codes, stats = encode((3, 4), (stats,), True)
    codes_c = lax.ppermute(codes, "section", to_cross)
    codes_a, stats = lax.optimization_barrier((codes_a, stats))
    e0 = decode((0,), codes_a)
    codes_b, e0 = lax.optimization_barrier((codes_b, e0))
    e12 = decode((1, 2), codes_b)
    codes_c, e12 = lax.optimization_barrier((codes_c, e12))
    e34 = decode((3, 4), codes_c)
    stats, e12, e34, encoder = lax.optimization_barrier((stats, e12, e34, encoder))
    total = lax.cond(encoder == 1, plane_sum, lambda x: 0.0 * x, stats)
    packed = jnp.concatenate([total, e12[0], e12[1]], axis=0)
    near, cross, far = (lax.ppermute(packed, "section", pairs) for pairs in (PAIR, CROSS, FAR))
    rows_total = float(CLIPS * lax.axis_size(DP) * ROWS)
    error, loss = call(
        functools.partial(final_body, rows_total),
        [SM] + [VM] * 6,
        [((2, CLIPS, ROWS), f32), ((1, 128), f32)],
    )(order, packed, near, cross, far, e0, e34)
    return error, loss[0, : order.shape[0]]


def solution(mesh):
    torus = Mesh(
        mesh.devices.reshape(mesh.shape["section"], 4, 4, 2), ("section", "dp_0", "dp_1", "dp_2")
    )
    return jax.shard_map(
        on_device,
        mesh=torus,
        in_specs=(
            P(DP, None, None),
            P(None, DP),
            P(),
            P("section", None, None, None),
            P("section", None, None),
            P("section", None),
            P(),
            P(),
            P(),
        ),
        out_specs=(P("section", DP, None), P()),
        check_vma=False,
    )
```

profile of v0, /device:TPU:1, one launch (start us, length us, event | category | flops | bytes accessed | tf_op | source)
XLA Modules:
  0.0 78.4 jit_solution(5237535560379405873)
XLA Ops:
  0.6 1.0 %shard_map.104 = bf16[1040,128]{1,0:T(8,128)(2,1)S(1)} custom-call(bf16[1536,512]{1,0:T(8,128)(2,1)} %bitcast.11, bf16[512,512]{1,0:T(8,128)(2,1)} %bitcast.13, bf16[1,512]{1,0:T(2,128)(2,1)} %gain_hbm.1), custom_call_target="tpu_custom_call" | custom-call | tf_op jit(solution)/shard_map/pallas_call | solution.py:412
  1.6 2.1 %collective-permute-start = (bf16[1040,128]{1,0:T(8,128)(2,1)S(1)}, bf16[1040,128]{1,0:T(8,128)(2,1)S(1)}, u32[]{:S(2)}, u32[]{:S(2)}) collective-permute-start(bf16[1040,128]{1,0:T(8,128)(2,1)S(1)} %shard_map.104), channel_id=1, source_target_pairs={{0,32},{32,0},{64,96},{96,64},{1,33},{33,1},{65,97},{97,65},{2,34}... | collective-permute-start | bytes 798728 | tf_op jit(solution)/shard_map/ppermute | solution.py:415
  3.7 6.7 %shard_map.105 = (bf16[5,4,256,512]{3,2,1,0:T(8,128)(2,1)S(1)}, bf16[2,1536,512]{2,1,0:T(8,128)(2,1)S(1)}, bf16[2,512,512]{2,1,0:T(8,128)(2,1)S(1)}, f32[2,8,512...) custom-call(bf16[32,256,512]{2,1,0:T(8,128)(2,1)} %pool.1, ...), custom_call_target="tpu_custom_call" | custom-call | flops 4294967296 | tf_op jit(solution)/shard_map/pallas_call | solution.py:417
  10.5 0.0 collective-permute-done.refs_0_
  10.5 1.1 %collective-permute-start.4 = (bf16[1040,128]{1,0:T(8,128)(2,1)S(1)}, bf16[1040,128]{1,0:T(8,128)(2,1)S(1)}, u32[]{:S(2)}, u32[]{:S(2)}) collective-permute-start(bf16[1040,128]{1,0:T(8,128)(2,1)S(1)} %collective-permute-done.refs_0_), channel_id=1, source_target_pairs={{0,1},{1,0},{2,3},{3,2},{4,5},{5,4},{6,7},{7,6},{8,9},{9,8},{10,11... | collective-permute-start | bytes 798728 | tf_op jit(solution)/shard_map/ppermute | solution.py:376
  11.6 3.7 %collective-permute-start.3 = (bf16[1040,128]{1,0:T(8,128)(2,1)S(1)}, bf16[1040,128]{1,0:T(8,128)(2,1)S(1)}, u32[]{:S(2)}, u32[]{:S(2)}) collective-permute-start(bf16[1040,128]{1,0:T(8,128)(2,1)S(1)} %collective-permute-done.refs_0_), channel_id=1, source_target_pairs={{0,2},{1,7},{2,4},{3,1},{4,6},{5,3},{6,0},{7,5},{8,10},{9,15},{10,... | collective-permute-start | bytes 798728 | tf_op jit(solution)/shard_map/ppermute | solution.py:385
  15.3 2.7 %collective-permute-start.2 = (bf16[1040,128]{1,0:T(8,128)(2,1)S(1)}, bf16[1040,128]{1,0:T(8,128)(2,1)S(1)}, u32[]{:S(2)}, u32[]{:S(2)}) collective-permute-start(bf16[1040,128]{1,0:T(8,128)(2,1)S(1)} %collective-permute-done.refs_0_), channel_id=1, source_target_pairs={{0,24},{8,0},{16,8},{24,16},{1,25},{9,1},{17,9},{25,17},{2,26},{10... | collective-permute-start | bytes 798728 | tf_op jit(solution)/shard_map/ppermute | solution.py:376
  18.0 0.0 collective-permute-start.1
  18.0 6.2 %shard_map.106.v = bf16[5,4,256,512]{3,2,1,0:T(8,128)(2,1)S(1)} custom-call(bf16[5,4,256,512]{3,2,1,0:T(8,128)(2,1)S(1)} %get-tuple-element.47.before, bf16[2,1536,512]{2,1,0:T(8,128)(2,1)S(1)} %get-tuple-element.48.all_taps.refs_8_, bf16[2,512,512]{2,1,0:T(8,128)(2,1)S(1)} %get-tuple-element.49.all_out.refs_9_, ...), custom_call_target="tpu_custom_call", output_to_operand_aliasing={{}: (0, {})} | custom-call | flops 6442450944 | tf_op jit(solution)/shard_map/pallas_call | solution.py:436
  24.3 0.0 collective-permute-done.4.refs_4_
  24.3 0.0 collective-permute-done.3.refs_3_
  24.3 0.0 collective-permute-done.2.refs_2_
  24.3 2.0 %collective-permute-done.1.refs_1_ = bf16[1040,128]{1,0:T(8,128)(2,1)S(1)} collective-permute-done((bf16[1040,128]{1,0:T(8,128)(2,1)S(1)}, bf16[1040,128]{1,0:T(8,128)(2,1)S(1)}, u32[]{:S(2)}, u32[]{:S(2)}) %collective-permute-start.1) | collective-permute-done | bytes 266272 | tf_op jit(solution)/shard_map/ppermute | solution.py:376
  26.3 0.0 collective-permute-start.5
  26.3 0.5 collective-permute-start.6
  26.9 0.0 collective-permute-start.7
  26.9 1.0 %collective-permute-done.5.refs_5_ = bf16[1040,128]{1,0:T(8,128)(2,1)S(1)} collective-permute-done((bf16[1040,128]{1,0:T(8,128)(2,1)S(1)}, bf16[1040,128]{1,0:T(8,128)(2,1)S(1)}, u32[]{:S(2)}, u32[]{:S(2)}) %collective-permute-start.5) | collective-permute-done | bytes 266272 | tf_op jit(solution)/shard_map/ppermute | solution.py:376
  27.9 0.4 collective-permute-done.6.refs_6_
  28.3 0.4 collective-permute-done.7.refs_7_
  28.6 0.6 shard_map.107
  29.3 2.7 %shard_map.108 = (bf16[1,24,1024]{2,1,0:T(8,128)(2,1)S(1)}, f32[24,128]{1,0:T(8,128)S(1)}) custom-call(bf16[5,4,256,512]{3,2,1,0:T(8,128)(2,1)S(1)} %shard_map.106.v, bf16[2,1536,512]{2,1,0:T(8,128)(2,1)S(1)} %get-tuple-element.56.all_taps, bf16[2,512,512]{2,1,0:T(8,128)(2,1)S(1)} %get-tuple-element.57.all_out, f32[2,8,512]{2,1,0:T(8,128)S(1)} %get-tuple-element.58.all_gain, ...), custom_call_target="tpu_custom_call" | custom-call | flops 4294967296 | tf_op jit(solution)/shard_map/pallas_call | solution.py:447
  32.0 1.6 %collective-permute-start.8 = (bf16[1,24,1024]{2,1,0:T(8,128)(2,1)S(1)}, bf16[1,24,1024]{2,1,0:T(8,128)(2,1)S(1)}, u32[]{:S(2)}, u32[]{:S(2)}) collective-permute-start(bf16[1,24,1024]{2,1,0:T(8,128)(2,1)S(1)} %get-tuple-element.61), channel_id=1, source_target_pairs={{0,64},{1,65},{2,66},{3,67},{4,68},{5,69},{6,70},{7,71},{8,72},{9,... | collective-permute-start | bytes 147464 | tf_op jit(solution)/shard_map/ppermute | solution.py:467
  33.7 5.6 %shard_map.109 = (bf16[2,24,1024]{2,1,0:T(8,128)(2,1)S(1)}, f32[24,128]{1,0:T(8,128)S(1)}) custom-call(bf16[5,4,256,512]{3,2,1,0:T(8,128)(2,1)S(1)} %shard_map.106.v, bf16[2,1536,512]{2,1,0:T(8,128)(2,1)S(1)} %get-tuple-element.56.all_taps, bf16[2,512,512]{2,1,0:T(8,128)(2,1)S(1)} %get-tuple-element.57.all_out, f32[2,8,512]{2,1,0:T(8,128)S(1)} %get-tuple-element.58.all_gain, ...), custom_call_target="tpu_custom_call" | custom-call | flops 8589934592 | tf_op jit(solution)/shard_map/pallas_call | solution.py:447
  39.3 5.5 %shard_map.110 = (bf16[2,24,1024]{2,1,0:T(8,128)(2,1)S(1)}, f32[8,128]{1,0:T(8,128)S(1)}) custom-call(bf16[5,4,256,512]{3,2,1,0:T(8,128)(2,1)S(1)} %shard_map.106.v, bf16[2,1536,512]{2,1,0:T(8,128)(2,1)S(1)} %get-tuple-element.56.all_taps, bf16[2,512,512]{2,1,0:T(8,128)(2,1)S(1)} %get-tuple-element.57.all_out, f32[2,8,512]{2,1,0:T(8,128)S(1)} %get-tuple-element.58.all_gain, ...), custom_call_target="tpu_custom_call" | custom-call | flops 8589934592 | tf_op jit(solution)/shard_map/pallas_call | solution.py:447
  44.9 1.3 %collective-permute-start.9 = (bf16[2,24,1024]{2,1,0:T(8,128)(2,1)S(1)}, bf16[2,24,1024]{2,1,0:T(8,128)(2,1)S(1)}, u32[]{:S(2)}, u32[]{:S(2)}) collective-permute-start(bf16[2,24,1024]{2,1,0:T(8,128)(2,1)S(1)} %get-tuple-element.66), channel_id=1, source_target_pairs={{0,96},{32,64},{1,97},{33,65},{2,98},{34,66},{3,99},{35,67},{4,100... | collective-permute-start | bytes 294920 | tf_op jit(solution)/shard_map/ppermute | solution.py:471
  46.2 1.3 %collective-permute-start.10 = (bf16[2,24,1024]{2,1,0:T(8,128)(2,1)S(1)}, bf16[2,24,1024]{2,1,0:T(8,128)(2,1)S(1)}, u32[]{:S(2)}, u32[]{:S(2)}) collective-permute-start(bf16[2,24,1024]{2,1,0:T(8,128)(2,1)S(1)} %get-tuple-element.68), channel_id=1, source_target_pairs={{0,96},{32,64},{1,97},{33,65},{2,98},{34,66},{3,99},{35,67},{4,100... | collective-permute-start | bytes 294920 | tf_op jit(solution)/shard_map/ppermute | solution.py:469
  47.5 0.0 collective-permute-done.8.codes
  47.5 2.8 %collective-permute-done.10.codes = bf16[2,24,1024]{2,1,0:T(8,128)(2,1)S(1)} collective-permute-done((bf16[2,24,1024]{2,1,0:T(8,128)(2,1)S(1)}, bf16[2,24,1024]{2,1,0:T(8,128)(2,1)S(1)}, u32[]{:S(2)}, u32[]{:S(2)}) %collective-permute-start.10) | collective-permute-done | bytes 98336 | tf_op jit(solution)/shard_map/ppermute | solution.py:469
  50.3 0.0 copy-start
  50.3 0.0 collective-permute-done.9.codes
  50.3 12.1 %conditional.1 = (f32[8,128]{1,0:T(8,128)S(1)}) conditional(s32[]{:T(128)} %convert_element_type.7, f32[8,128]{1,0:T(8,128)S(1)} %get-tuple-element.75, f32[8,128]{1,0:T(8,128)S(1)} %get-tuple-element.75), branch_computations={%region_0.0_spmd, %region_1.0_spmd} | conditional | flops 31744 | bytes 532492 | solution.py:479
  50.3 12.0 %all_to_all.4 = f32[32,8,128]{2,1,0:T(8,128)S(1)} all-to-all(f32[32,8,128]{2,1,0:T(8,128)S(1)} %broadcast_in_dim.0), channel_id=1, replica_groups=mesh['section'=4,'dp_0'=4,'dp_1'=4,'dp_2'=2] {'dp_0','dp_1','dp_2'}, dimensions={0} | all-to-all | bytes 262144 | tf_op jit(solution)/shard_map/cond/branch_1_fun/all_to_all | solution.py:390
  62.4 6.7 %collective-permute-start.13 = (f32[24,128]{1,0:T(8,128)S(1)}, f32[24,128]{1,0:T(8,128)S(1)}, u32[]{:S(2)}, u32[]{:S(2)}) collective-permute-start(f32[24,128]{1,0:T(8,128)S(1)} %pad_maximum_fusion.mine), channel_id=1, source_target_pairs={{0,64},{64,0},{32,96},{96,32},{1,65},{65,1},{33,97},{97,33},{2,66}... | collective-permute-start | bytes 36872 | tf_op jit(solution)/shard_map/ppermute | solution.py:481
  69.0 5.0 %collective-permute-start.12 = (f32[24,128]{1,0:T(8,128)S(1)}, f32[24,128]{1,0:T(8,128)S(1)}, u32[]{:S(2)}, u32[]{:S(2)}) collective-permute-start(f32[24,128]{1,0:T(8,128)S(1)} %pad_maximum_fusion.mine), channel_id=1, source_target_pairs={{0,96},{96,0},{32,64},{64,32},{1,97},{97,1},{33,65},{65,33},{2,98}... | collective-permute-start | bytes 36872 | tf_op jit(solution)/shard_map/ppermute | solution.py:481
  74.0 0.5 collective-permute-start.11
  74.5 0.0 collective-permute-done.13.far
  74.5 0.6 collective-permute-done.12.cross
  75.1 1.5 %collective-permute-done.11.next_ = f32[24,128]{1,0:T(8,128)S(1)} collective-permute-done((f32[24,128]{1,0:T(8,128)S(1)}, f32[24,128]{1,0:T(8,128)S(1)}, u32[]{:S(2)}, u32[]{:S(2)}) %collective-permute-start.11) | collective-permute-done | bytes 12320 | tf_op jit(solution)/shard_map/ppermute | solution.py:481
  76.6 0.0 copy-done
  76.6 1.3 %shard_map.114 = (f32[2,4,256]{2,1,0:T(4,128)}, f32[1,128]{1,0:T(1,128)S(1)}) custom-call(s32[8]{0:T(128)S(1)} %copy-done, f32[24,128]{1,0:T(8,128)S(1)} %pad_maximum_fusion.mine, f32[24,128]{1,0:T(8,128)S(1)} %collective-permute-done.11.next_, f32[24,128]{1,0:T(8,128)S(1)} %collective-permute-done.12.cross, f32[24,128]{1,0:T(8,128)S(1)} %collective-permute-done.13.far, ...), custom_call_target="tpu_custom_call" | custom-call | tf_op jit(solution)/shard_map/pallas_call | solution.py:483
  77.9 0.5 slice_bitcast_fusion.2
  (7 shorter events, 0.1 us)
Async XLA Ops:
  1.6 8.8 %collective-permute-start = (bf16[1040,128]{1,0:T(8,128)(2,1)S(1)}, bf16[1040,128]{1,0:T(8,128)(2,1)S(1)}, u32[]{:S(2)}, u32[]{:S(2)}) collective-permute-start(bf16[1040,128]{1,0:T(8,128)(2,1)S(1)} %shard_map.104), channel_id=1, source_target_pairs={{0,32},{32,0},{64,96},{96,64},{1,33},{33,1},{65,97},{97,65},{2,34}... | collective-permute-start | bytes 798728 | tf_op jit(solution)/shard_map/ppermute | solution.py:415
  10.5 13.8 %collective-permute-start.4 = (bf16[1040,128]{1,0:T(8,128)(2,1)S(1)}, bf16[1040,128]{1,0:T(8,128)(2,1)S(1)}, u32[]{:S(2)}, u32[]{:S(2)}) collective-permute-start(bf16[1040,128]{1,0:T(8,128)(2,1)S(1)} %collective-permute-done.refs_0_), channel_id=1, source_target_pairs={{0,1},{1,0},{2,3},{3,2},{4,5},{5,4},{6,7},{7,6},{8,9},{9,8},{10,11... | collective-permute-start | bytes 798728 | tf_op jit(solution)/shard_map/ppermute | solution.py:376
  11.6 12.7 %collective-permute-start.3 = (bf16[1040,128]{1,0:T(8,128)(2,1)S(1)}, bf16[1040,128]{1,0:T(8,128)(2,1)S(1)}, u32[]{:S(2)}, u32[]{:S(2)}) collective-permute-start(bf16[1040,128]{1,0:T(8,128)(2,1)S(1)} %collective-permute-done.refs_0_), channel_id=1, source_target_pairs={{0,2},{1,7},{2,4},{3,1},{4,6},{5,3},{6,0},{7,5},{8,10},{9,15},{10,... | collective-permute-start | bytes 798728 | tf_op jit(solution)/shard_map/ppermute | solution.py:385
  15.3 9.0 %collective-permute-start.2 = (bf16[1040,128]{1,0:T(8,128)(2,1)S(1)}, bf16[1040,128]{1,0:T(8,128)(2,1)S(1)}, u32[]{:S(2)}, u32[]{:S(2)}) collective-permute-start(bf16[1040,128]{1,0:T(8,128)(2,1)S(1)} %collective-permute-done.refs_0_), channel_id=1, source_target_pairs={{0,24},{8,0},{16,8},{24,16},{1,25},{9,1},{17,9},{25,17},{2,26},{10... | collective-permute-start | bytes 798728 | tf_op jit(solution)/shard_map/ppermute | solution.py:376
  18.0 8.3 %collective-permute-start.1 = (bf16[1040,128]{1,0:T(8,128)(2,1)S(1)}, bf16[1040,128]{1,0:T(8,128)(2,1)S(1)}, u32[]{:S(2)}, u32[]{:S(2)}) collective-permute-start(bf16[1040,128]{1,0:T(8,128)(2,1)S(1)} %collective-permute-done.refs_0_), channel_id=1, source_target_pairs={{0,8},{8,16},{16,24},{24,0},{1,9},{9,17},{17,25},{25,1},{2,10},{10... | collective-permute-start | bytes 798728 | tf_op jit(solution)/shard_map/ppermute | solution.py:376
  26.3 1.5 %collective-permute-start.5 = (bf16[1040,128]{1,0:T(8,128)(2,1)S(1)}, bf16[1040,128]{1,0:T(8,128)(2,1)S(1)}, u32[]{:S(2)}, u32[]{:S(2)}) collective-permute-start(bf16[1040,128]{1,0:T(8,128)(2,1)S(1)} %collective-permute-done.1.refs_1_), channel_id=1, source_target_pairs={{0,1},{1,0},{2,3},{3,2},{4,5},{5,4},{6,7},{7,6},{8,9},{9,8},{10,11... | collective-permute-start | bytes 798728 | tf_op jit(solution)/shard_map/ppermute | solution.py:376
  26.3 1.9 %collective-permute-start.6 = (bf16[1040,128]{1,0:T(8,128)(2,1)S(1)}, bf16[1040,128]{1,0:T(8,128)(2,1)S(1)}, u32[]{:S(2)}, u32[]{:S(2)}) collective-permute-start(bf16[1040,128]{1,0:T(8,128)(2,1)S(1)} %collective-permute-done.2.refs_2_), channel_id=1, source_target_pairs={{0,1},{1,0},{2,3},{3,2},{4,5},{5,4},{6,7},{7,6},{8,9},{9,8},{10,11... | collective-permute-start | bytes 798728 | tf_op jit(solution)/shard_map/ppermute | solution.py:376
  26.9 1.8 %collective-permute-start.7 = (bf16[1040,128]{1,0:T(8,128)(2,1)S(1)}, bf16[1040,128]{1,0:T(8,128)(2,1)S(1)}, u32[]{:S(2)}, u32[]{:S(2)}) collective-permute-start(bf16[1040,128]{1,0:T(8,128)(2,1)S(1)} %collective-permute-done.3.refs_3_), channel_id=1, source_target_pairs={{0,1},{1,0},{2,3},{3,2},{4,5},{5,4},{6,7},{7,6},{8,9},{9,8},{10,11... | collective-permute-start | bytes 798728 | tf_op jit(solution)/shard_map/ppermute | solution.py:376
  32.0 15.4 %collective-permute-start.8 = (bf16[1,24,1024]{2,1,0:T(8,128)(2,1)S(1)}, bf16[1,24,1024]{2,1,0:T(8,128)(2,1)S(1)}, u32[]{:S(2)}, u32[]{:S(2)}) collective-permute-start(bf16[1,24,1024]{2,1,0:T(8,128)(2,1)S(1)} %get-tuple-element.61), channel_id=1, source_target_pairs={{0,64},{1,65},{2,66},{3,67},{4,68},{5,69},{6,70},{7,71},{8,72},{9,... | collective-permute-start | bytes 147464 | tf_op jit(solution)/shard_map/ppermute | solution.py:467
  44.9 5.4 %collective-permute-start.9 = (bf16[2,24,1024]{2,1,0:T(8,128)(2,1)S(1)}, bf16[2,24,1024]{2,1,0:T(8,128)(2,1)S(1)}, u32[]{:S(2)}, u32[]{:S(2)}) collective-permute-start(bf16[2,24,1024]{2,1,0:T(8,128)(2,1)S(1)} %get-tuple-element.66), channel_id=1, source_target_pairs={{0,96},{32,64},{1,97},{33,65},{2,98},{34,66},{3,99},{35,67},{4,100... | collective-permute-start | bytes 294920 | tf_op jit(solution)/shard_map/ppermute | solution.py:471
  46.2 4.1 %collective-permute-start.10 = (bf16[2,24,1024]{2,1,0:T(8,128)(2,1)S(1)}, bf16[2,24,1024]{2,1,0:T(8,128)(2,1)S(1)}, u32[]{:S(2)}, u32[]{:S(2)}) collective-permute-start(bf16[2,24,1024]{2,1,0:T(8,128)(2,1)S(1)} %get-tuple-element.68), channel_id=1, source_target_pairs={{0,96},{32,64},{1,97},{33,65},{2,98},{34,66},{3,99},{35,67},{4,100... | collective-permute-start | bytes 294920 | tf_op jit(solution)/shard_map/ppermute | solution.py:469
  50.3 26.3 %copy-start = (s32[8]{0:T(128)S(1)}, s32[8]{0:T(128)}, u32[]{:S(2)}) copy-start(s32[8]{0:T(128)} %order.1) | copy-start | bytes 100
  62.4 12.1 %collective-permute-start.13 = (f32[24,128]{1,0:T(8,128)S(1)}, f32[24,128]{1,0:T(8,128)S(1)}, u32[]{:S(2)}, u32[]{:S(2)}) collective-permute-start(f32[24,128]{1,0:T(8,128)S(1)} %pad_maximum_fusion.mine), channel_id=1, source_target_pairs={{0,64},{64,0},{32,96},{96,32},{1,65},{65,1},{33,97},{97,33},{2,66}... | collective-permute-start | bytes 36872 | tf_op jit(solution)/shard_map/ppermute | solution.py:481
  69.0 6.1 %collective-permute-start.12 = (f32[24,128]{1,0:T(8,128)S(1)}, f32[24,128]{1,0:T(8,128)S(1)}, u32[]{:S(2)}, u32[]{:S(2)}) collective-permute-start(f32[24,128]{1,0:T(8,128)S(1)} %pad_maximum_fusion.mine), channel_id=1, source_target_pairs={{0,96},{96,0},{32,64},{64,32},{1,97},{97,1},{33,65},{65,33},{2,98}... | collective-permute-start | bytes 36872 | tf_op jit(solution)/shard_map/ppermute | solution.py:481
  74.0 2.6 %collective-permute-start.11 = (f32[24,128]{1,0:T(8,128)S(1)}, f32[24,128]{1,0:T(8,128)S(1)}, u32[]{:S(2)}, u32[]{:S(2)}) collective-permute-start(f32[24,128]{1,0:T(8,128)S(1)} %pad_maximum_fusion.mine), channel_id=1, source_target_pairs={{0,32},{32,0},{64,96},{96,64},{1,33},{33,1},{65,97},{97,65},{2,34}... | collective-permute-start | bytes 36872 | tf_op jit(solution)/shard_map/ppermute | solution.py:481
where the time goes:
time: 79.6 us; the launch traced here: 78.4 us
  Pallas kernels  29.8 us (37%)
  starting transfers between devices  26.6 us (33%)
  blocking collectives  12 us (15%)
  waiting for transfers between devices  8.67 us (11%)
    pallas_call x3, Pallas kernels, encode(): call(functools.partial(encode_body, steps, last), [VM] * (6 + len(before)...  13.9 us
    ppermute x3, starting transfers between devices, on_device(): lax.ppermute(packed, 'section', pairs)  12.1 us
    all_to_all x1, blocking collectives, plane_sum(): lax.all_to_all(jnp.broadcast_to(x[None], (n, *x.shape)), DP, 0, 0)  12 us
    pallas_call x1, Pallas kernels, on_device(): call(functools.partial(start_body, 2), [HB] * 8, [v_kind, *kinds, ((C, 12...  6.71 us
    pallas_call x1, Pallas kernels, on_device(): call(functools.partial(more_body, 2, STEPS), [VM] * 4, [v_kind], blocks=3...  6.21 us
    ppermute x6, starting transfers between devices, shifted(): return lax.ppermute(x, axis, [(i, (i + by) % n) for i in range(n)])  4.34 us
    ppermute x6, waiting for transfers between devices, shifted(): return lax.ppermute(x, axis, [(i, (i + by) % n) for i in range(n)])  3.83 us
    ppermute x1, starting transfers between devices, split_shift(): return lax.ppermute(x, (axis, 'dp_2'), pairs)  3.75 us
  transfers between devices with their start and end apart: 14, of which 7 were waited for; matrix products, arithmetic and copies ran while one was open for 0% of the time, Pallas kernels for 31%

commit v1 on v0

--- a/solution.py
+++ b/solution.py
@@ -78,40 +78,44 @@
         )
 
 
-def prep_body(taps, out_weight, gain_hbm, piece, gain, sems):
-    colour = lax.rem(lax.axis_index("dp_0") + 2 * lax.axis_index("dp_1"), 4)
-    at = pl.ds(pl.multiple_of(colour * 128, 128), 128)
+def prep_body(taps, out_weight, gain_hbm, piece, second, gain, sems):
     core = lax.axis_index("dp_2")
-    gain_copy = pltpu.make_async_copy(gain_hbm, gain, sems.at[5])
+    gain_copy = pltpu.make_async_copy(gain_hbm, gain, sems.at[10])
     gain_copy.start()
 
-    @pl.when(core == 0)
-    def _():
-        copy = pltpu.make_async_copy(
-            taps.at[pl.ds(0, HALF), at], piece.at[pl.ds(0, HALF)], sems.at[0]
-        )
-        copy.start()
-        copy.wait()
-
-    @pl.when(core == 1)
-    def _():
-        copies = [
+    def copies(target, on, at):
+        colour = lax.rem(lax.axis_index("dp_0") + 2 * lax.axis_index("dp_1") + on, 4)
+        lanes = pl.ds(pl.multiple_of(colour * 128, 128), 128)
+        lower = [
             pltpu.make_async_copy(
-                taps.at[pl.ds(HALF, 512), at], piece.at[pl.ds(0, 512)], sems.at[0]
+                taps.at[pl.ds(0, HALF), lanes], target.at[pl.ds(0, HALF)], sems.at[at]
+            )
+        ]
+        upper = [
+            pltpu.make_async_copy(
+                taps.at[pl.ds(HALF, 512), lanes], target.at[pl.ds(0, 512)], sems.at[at]
             )
         ]
         for j in range(4):
-            copies.append(
+            upper.append(
                 pltpu.make_async_copy(
-                    out_weight.at[at, pl.ds(128 * j, 128)],
-                    piece.at[pl.ds(512 + 128 * j, 128)],
-                    sems.at[1 + j],
+                    out_weight.at[lanes, pl.ds(128 * j, 128)],
+                    target.at[pl.ds(512 + 128 * j, 128)],
+                    sems.at[at + 1 + j],
                 )
             )
-        for copy in copies:
-            copy.start()
-        for copy in copies:
-            copy.wait()
+        return lower, upper
+
+    sets = [copies(piece, 0, 0), copies(second, 2, 5)]
+    for side in range(2):
+
+        @pl.when(core == side)
+        def _(side=side):
+            chosen = sets[0][side] + sets[1][side]
+            for copy in chosen:
+                copy.start()
+            for copy in chosen:
+                copy.wait()
 
     gain_copy.wait()
     wide = gain[...].astype(jnp.float32)
@@ -348,7 +352,8 @@
     term = smoothed * jnp.log(smoothed) + (1.0 - smoothed) * jnp.log(1.0 - smoothed)
     term = jnp.where(lane < BITS, term, jnp.where(lane == BITS, sums, 0.0))
     result = jnp.sum(term, axis=1, keepdims=True)
-    loss[...] = jnp.sum(jnp.where(row == lane, result, 0.0), axis=0, keepdims=True)
+    flat = jnp.sum(jnp.where(row == lane, result, 0.0), axis=0)
+    loss[...] = flat[:8]
 
     @pl.when(section <= 1)
     def _():
@@ -374,15 +379,6 @@
 def shifted(x, axis, by):
     n = lax.axis_size(axis)
     return lax.ppermute(x, axis, [(i, (i + by) % n) for i in range(n)])
-
-
-def split_shift(x, axis):
-    n = lax.axis_size(axis)
-    pairs = []
-    for i in range(n):
-        pairs.append((2 * i, 2 * ((i + 1) % n)))
-        pairs.append((2 * i + 1, 2 * ((i - 1) % n) + 1))
-    return lax.ppermute(x, (axis, "dp_2"), pairs)
 
 
 def plane_sum(x):
@@ -409,10 +405,14 @@
         for x in (gain, quant_weight.T, post_weight, index)
     )
     qbias = pltpu.with_memory_space_constraint(quant_bias.reshape(1, BITS), pltpu.HBM)
-    (piece,) = call(
-        prep_body, [HB] * 3, [((PIECE, 128), bf16)], [pltpu.VMEM((1, C), bf16), dma((6,))]
+    piece, second = call(
+        prep_body,
+        [HB] * 3,
+        [((PIECE, 128), bf16), ((HALF, 128), bf16)],
+        [pltpu.VMEM((1, C), bf16), dma((11,))],
     )(taps, out_weight, gain)
     mine = lax.ppermute(piece, "section", PAIR)
+    second = lax.ppermute(second, "section", PAIR)
     v_kind = ((STEPS, *chunk), bf16)
     v, *weights, qw, qb, post = call(
         functools.partial(start_body, 2),
@@ -431,16 +431,15 @@
     mine, v = lax.optimization_barrier((mine, v))
     up = shifted(mine, "dp_0", 1)
     down = shifted(mine, "dp_0", -1)
-    side = split_shift(mine, "dp_1")
     mine_s = shifted(mine, "dp_2", 1)
     (v,) = call(
         functools.partial(more_body, 2, STEPS), [VM] * 4, [v_kind], blocks=3, aliases={0: 0}
     )(v, *weights)
-    up, down, side, mine_s, v = lax.optimization_barrier((up, down, side, mine_s, v))
-    swapped = [mine_s] + [shifted(x, "dp_2", 1) for x in (up, down, side)]
+    up, down, second, mine_s, v = lax.optimization_barrier((up, down, second, mine_s, v))
+    swapped = [mine_s] + [shifted(x, "dp_2", 1) for x in (second, up, down)]
     weights = call(
         join_body, [VM] + [ANY] * 7 + [VM] * 3, kinds, [dma((24,))], aliases={8: 0, 9: 1, 10: 2}
-    )(mine, up, down, side, *swapped, *weights)
+    )(mine, second, up, down, *swapped, *weights)
 
     def encode(steps, before, last):
         n = len(steps)
@@ -483,9 +482,9 @@
     error, loss = call(
         functools.partial(final_body, rows_total),
         [SM] + [VM] * 6,
-        [((2, CLIPS, ROWS), f32), ((1, 128), f32)],
+        [((2, CLIPS, ROWS), f32), ((8,), f32)],
     )(order, packed, near, cross, far, e0, e34)
-    return error, loss[0, : order.shape[0]]
+    return error, loss
 
 
 def solution(mesh):

time: 79.6 us -> 82.6 us (1.038)
  waiting for transfers between devices: 8.67 us -> 13.4 us
  starting transfers between devices: 26.6 us -> 23 us
  blocking collectives: 12 us -> 14.1 us
    ppermute x1, waiting for transfers between devices: 0.01 us -> 4.51 us  [on_device(): mine = lax.ppermute(piece, 'section', PAIR)]
    ppermute x3, starting transfers between devices: 12.1 us -> 9.98 us  [on_device(): lax.ppermute(packed, 'section', pairs)]
    all_to_all x1, blocking collectives: 12 us -> 14.1 us  [plane_sum(): lax.all_to_all(jnp.broadcast_to(x[None], (n, *x.shape)), DP, 0, 0)]
    ppermute x1, starting transfers between devices: 2.11 us -> 0.09 us  [on_device(): mine = lax.ppermute(piece, 'section', PAIR)]
    ppermute x6, starting transfers between devices: 4.34 us -> 6.29 us  [shifted(): return lax.ppermute(x, axis, [(i, (i + by) % n) for i in range(n)])]
    ppermute x1, starting transfers between devices: 3.75 us -> 2.11 us  [on_device(): second = lax.ppermute(second, 'section', PAIR)]
  transfers between devices with their start and end apart: 14 -> 14, of which waited for: 7 -> 6; matrix products, arithmetic and copies ran while one was open for 0% -> 0% of each run, Pallas kernels for 31% -> 30%
where the time goes in v1:
time: 82.6 us; the launch traced here: 81.3 us
  Pallas kernels  29.9 us (36%)
  starting transfers between devices  23 us (28%)
  blocking collectives  14.1 us (17%)
  waiting for transfers between devices  13.4 us (16%)
    all_to_all x1, blocking collectives, plane_sum(): lax.all_to_all(jnp.broadcast_to(x[None], (n, *x.shape)), DP, 0, 0)  14.1 us
    pallas_call x3, Pallas kernels, encode(): call(functools.partial(encode_body, steps, last), [VM] * (6 + len(before)...  13.9 us
    ppermute x3, starting transfers between devices, on_device(): lax.ppermute(packed, 'section', pairs)  9.98 us
    pallas_call x1, Pallas kernels, on_device(): call(functools.partial(start_body, 2), [HB] * 8, [v_kind, *kinds, ((C, 12...  6.71 us
    ppermute x6, starting transfers between devices, shifted(): return lax.ppermute(x, axis, [(i, (i + by) % n) for i in range(n)])  6.29 us
    pallas_call x1, Pallas kernels, on_device(): call(functools.partial(more_body, 2, STEPS), [VM] * 4, [v_kind], blocks=3...  6.2 us
    ppermute x1, waiting for transfers between devices, on_device(): mine = lax.ppermute(piece, 'section', PAIR)  4.51 us
    ppermute x6, waiting for transfers between devices, shifted(): return lax.ppermute(x, axis, [(i, (i + by) % n) for i in range(n)])  4.06 us
  transfers between devices with their start and end apart: 14, of which 6 were waited for; matrix products, arithmetic and copies ran while one was open for 0% of the time, Pallas kernels for 30%

profile of v1, /device:TPU:1, one launch (start us, length us, event | category | flops | bytes accessed | tf_op | source)
XLA Modules:
  0.0 81.3 jit_solution(1562587819086572609)
XLA Ops:
  0.6 1.2 %shard_map.104 = (bf16[1040,128]{1,0:T(8,128)(2,1)S(1)}, bf16[1024,128]{1,0:T(8,128)(2,1)S(1)}) custom-call(bf16[1536,512]{1,0:T(8,128)(2,1)} %bitcast.9, bf16[512,512]{1,0:T(8,128)(2,1)} %bitcast.11, bf16[1,512]{1,0:T(2,128)(2,1)} %gain_hbm.1), custom_call_target="tpu_custom_call" | custom-call | tf_op jit(solution)/shard_map/pallas_call | solution.py:408
  1.8 2.1 %collective-permute-start.3 = (bf16[1024,128]{1,0:T(8,128)(2,1)S(1)}, bf16[1024,128]{1,0:T(8,128)(2,1)S(1)}, u32[]{:S(2)}, u32[]{:S(2)}) collective-permute-start(bf16[1024,128]{1,0:T(8,128)(2,1)S(1)} %get-tuple-element.48), channel_id=1, source_target_pairs={{0,32},{32,0},{64,96},{96,64},{1,33},{33,1},{65,97},{97,65},{2,34}... | collective-permute-start | bytes 786440 | tf_op jit(solution)/shard_map/ppermute | solution.py:415
  3.9 0.1 collective-permute-start
  4.0 6.7 %shard_map.105 = (bf16[5,4,256,512]{3,2,1,0:T(8,128)(2,1)S(1)}, bf16[2,1536,512]{2,1,0:T(8,128)(2,1)S(1)}, bf16[2,512,512]{2,1,0:T(8,128)(2,1)S(1)}, f32[2,8,512...) custom-call(bf16[32,256,512]{2,1,0:T(8,128)(2,1)} %pool.1, ...), custom_call_target="tpu_custom_call" | custom-call | flops 4294967296 | tf_op jit(solution)/shard_map/pallas_call | solution.py:417
  10.7 4.5 %collective-permute-done.refs_0_ = bf16[1040,128]{1,0:T(8,128)(2,1)S(1)} collective-permute-done((bf16[1040,128]{1,0:T(8,128)(2,1)S(1)}, bf16[1040,128]{1,0:T(8,128)(2,1)S(1)}, u32[]{:S(2)}, u32[]{:S(2)}) %collective-permute-start) | collective-permute-done | bytes 266272 | tf_op jit(solution)/shard_map/ppermute | solution.py:414
  15.2 1.7 %collective-permute-start.4 = (bf16[1040,128]{1,0:T(8,128)(2,1)S(1)}, bf16[1040,128]{1,0:T(8,128)(2,1)S(1)}, u32[]{:S(2)}, u32[]{:S(2)}) collective-permute-start(bf16[1040,128]{1,0:T(8,128)(2,1)S(1)} %collective-permute-done.refs_0_), channel_id=1, source_target_pairs={{0,1},{1,0},{2,3},{3,2},{4,5},{5,4},{6,7},{7,6},{8,9},{9,8},{10,11... | collective-permute-start | bytes 798728 | tf_op jit(solution)/shard_map/ppermute | solution.py:381
  16.9 3.0 %collective-permute-start.2 = (bf16[1040,128]{1,0:T(8,128)(2,1)S(1)}, bf16[1040,128]{1,0:T(8,128)(2,1)S(1)}, u32[]{:S(2)}, u32[]{:S(2)}) collective-permute-start(bf16[1040,128]{1,0:T(8,128)(2,1)S(1)} %collective-permute-done.refs_0_), channel_id=1, source_target_pairs={{0,24},{8,0},{16,8},{24,16},{1,25},{9,1},{17,9},{25,17},{2,26},{10... | collective-permute-start | bytes 798728 | tf_op jit(solution)/shard_map/ppermute | solution.py:381
  19.9 0.0 collective-permute-start.1
  19.9 6.2 %shard_map.106.v = bf16[5,4,256,512]{3,2,1,0:T(8,128)(2,1)S(1)} custom-call(bf16[5,4,256,512]{3,2,1,0:T(8,128)(2,1)S(1)} %get-tuple-element.49.before, bf16[2,1536,512]{2,1,0:T(8,128)(2,1)S(1)} %get-tuple-element.50.all_taps.refs_8_, bf16[2,512,512]{2,1,0:T(8,128)(2,1)S(1)} %get-tuple-element.51.all_out.refs_9_, ...), custom_call_target="tpu_custom_call", output_to_operand_aliasing={{}: (0, {})} | custom-call | flops 6442450944 | tf_op jit(solution)/shard_map/pallas_call | solution.py:435
  26.1 0.0 collective-permute-done.3.refs_1_
  26.1 0.0 collective-permute-done.4.refs_4_
  26.1 0.0 collective-permute-done.2.refs_3_
  26.1 2.6 %collective-permute-done.1.refs_2_ = bf16[1040,128]{1,0:T(8,128)(2,1)S(1)} collective-permute-done((bf16[1040,128]{1,0:T(8,128)(2,1)S(1)}, bf16[1040,128]{1,0:T(8,128)(2,1)S(1)}, u32[]{:S(2)}, u32[]{:S(2)}) %collective-permute-start.1) | collective-permute-done | bytes 266272 | tf_op jit(solution)/shard_map/ppermute | solution.py:381
  28.8 1.1 %collective-permute-start.6 = (bf16[1040,128]{1,0:T(8,128)(2,1)S(1)}, bf16[1040,128]{1,0:T(8,128)(2,1)S(1)}, u32[]{:S(2)}, u32[]{:S(2)}) collective-permute-start(bf16[1040,128]{1,0:T(8,128)(2,1)S(1)} %collective-permute-done.1.refs_2_), channel_id=1, source_target_pairs={{0,1},{1,0},{2,3},{3,2},{4,5},{5,4},{6,7},{7,6},{8,9},{9,8},{10,11... | collective-permute-start | bytes 798728 | tf_op jit(solution)/shard_map/ppermute | solution.py:381
  29.9 0.0 collective-permute-start.7
  29.9 0.5 collective-permute-start.5
  30.4 1.4 %collective-permute-done.5.refs_5_ = bf16[1024,128]{1,0:T(8,128)(2,1)S(1)} collective-permute-done((bf16[1024,128]{1,0:T(8,128)(2,1)S(1)}, bf16[1024,128]{1,0:T(8,128)(2,1)S(1)}, u32[]{:S(2)}, u32[]{:S(2)}) %collective-permute-start.5) | collective-permute-done | bytes 262176 | tf_op jit(solution)/shard_map/ppermute | solution.py:381
  31.8 0.0 collective-permute-done.6.refs_6_
  31.8 0.0 collective-permute-done.7.refs_7_
  31.8 0.6 shard_map.107
  32.5 2.7 %shard_map.108 = (bf16[1,24,1024]{2,1,0:T(8,128)(2,1)S(1)}, f32[24,128]{1,0:T(8,128)S(1)}) custom-call(bf16[5,4,256,512]{3,2,1,0:T(8,128)(2,1)S(1)} %shard_map.106.v, bf16[2,1536,512]{2,1,0:T(8,128)(2,1)S(1)} %get-tuple-element.58.all_taps, bf16[2,512,512]{2,1,0:T(8,128)(2,1)S(1)} %get-tuple-element.59.all_out, f32[2,8,512]{2,1,0:T(8,128)S(1)} %get-tuple-element.60.all_gain, ...), custom_call_target="tpu_custom_call" | custom-call | flops 4294967296 | tf_op jit(solution)/shard_map/pallas_call | solution.py:446
  35.2 1.9 %collective-permute-start.8 = (bf16[1,24,1024]{2,1,0:T(8,128)(2,1)S(1)}, bf16[1,24,1024]{2,1,0:T(8,128)(2,1)S(1)}, u32[]{:S(2)}, u32[]{:S(2)}) collective-permute-start(bf16[1,24,1024]{2,1,0:T(8,128)(2,1)S(1)} %get-tuple-element.63), channel_id=1, source_target_pairs={{0,64},{1,65},{2,66},{3,67},{4,68},{5,69},{6,70},{7,71},{8,72},{9,... | collective-permute-start | bytes 147464 | tf_op jit(solution)/shard_map/ppermute | solution.py:466
  37.2 5.6 %shard_map.109 = (bf16[2,24,1024]{2,1,0:T(8,128)(2,1)S(1)}, f32[24,128]{1,0:T(8,128)S(1)}) custom-call(bf16[5,4,256,512]{3,2,1,0:T(8,128)(2,1)S(1)} %shard_map.106.v, bf16[2,1536,512]{2,1,0:T(8,128)(2,1)S(1)} %get-tuple-element.58.all_taps, bf16[2,512,512]{2,1,0:T(8,128)(2,1)S(1)} %get-tuple-element.59.all_out, f32[2,8,512]{2,1,0:T(8,128)S(1)} %get-tuple-element.60.all_gain, ...), custom_call_target="tpu_custom_call" | custom-call | flops 8589934592 | tf_op jit(solution)/shard_map/pallas_call | solution.py:446
  42.8 5.5 %shard_map.110 = (bf16[2,24,1024]{2,1,0:T(8,128)(2,1)S(1)}, f32[8,128]{1,0:T(8,128)S(1)}) custom-call(bf16[5,4,256,512]{3,2,1,0:T(8,128)(2,1)S(1)} %shard_map.106.v, bf16[2,1536,512]{2,1,0:T(8,128)(2,1)S(1)} %get-tuple-element.58.all_taps, bf16[2,512,512]{2,1,0:T(8,128)(2,1)S(1)} %get-tuple-element.59.all_out, f32[2,8,512]{2,1,0:T(8,128)S(1)} %get-tuple-element.60.all_gain, ...), custom_call_target="tpu_custom_call" | custom-call | flops 8589934592 | tf_op jit(solution)/shard_map/pallas_call | solution.py:446
  48.3 1.3 %collective-permute-start.9 = (bf16[2,24,1024]{2,1,0:T(8,128)(2,1)S(1)}, bf16[2,24,1024]{2,1,0:T(8,128)(2,1)S(1)}, u32[]{:S(2)}, u32[]{:S(2)}) collective-permute-start(bf16[2,24,1024]{2,1,0:T(8,128)(2,1)S(1)} %get-tuple-element.68), channel_id=1, source_target_pairs={{0,96},{32,64},{1,97},{33,65},{2,98},{34,66},{3,99},{35,67},{4,100... | collective-permute-start | bytes 294920 | tf_op jit(solution)/shard_map/ppermute | solution.py:470
  49.6 1.3 %collective-permute-start.10 = (bf16[2,24,1024]{2,1,0:T(8,128)(2,1)S(1)}, bf16[2,24,1024]{2,1,0:T(8,128)(2,1)S(1)}, u32[]{:S(2)}, u32[]{:S(2)}) collective-permute-start(bf16[2,24,1024]{2,1,0:T(8,128)(2,1)S(1)} %get-tuple-element.70), channel_id=1, source_target_pairs={{0,96},{32,64},{1,97},{33,65},{2,98},{34,66},{3,99},{35,67},{4,100... | collective-permute-start | bytes 294920 | tf_op jit(solution)/shard_map/ppermute | solution.py:468
  50.9 0.0 collective-permute-done.8.codes
  51.0 2.6 %collective-permute-done.10.codes = bf16[2,24,1024]{2,1,0:T(8,128)(2,1)S(1)} collective-permute-done((bf16[2,24,1024]{2,1,0:T(8,128)(2,1)S(1)}, bf16[2,24,1024]{2,1,0:T(8,128)(2,1)S(1)}, u32[]{:S(2)}, u32[]{:S(2)}) %collective-permute-start.10) | collective-permute-done | bytes 98336 | tf_op jit(solution)/shard_map/ppermute | solution.py:468
  53.5 0.0 copy-start
  53.5 0.0 collective-permute-done.9.codes
  53.5 14.2 %conditional.1 = (f32[8,128]{1,0:T(8,128)S(1)}) conditional(s32[]{:T(128)} %convert_element_type.7, f32[8,128]{1,0:T(8,128)S(1)} %get-tuple-element.77, f32[8,128]{1,0:T(8,128)S(1)} %get-tuple-element.77), branch_computations={%region_0.0_spmd, %region_1.0_spmd} | conditional | flops 31744 | bytes 532492 | solution.py:478
  53.6 14.1 %all_to_all.4 = f32[32,8,128]{2,1,0:T(8,128)S(1)} all-to-all(f32[32,8,128]{2,1,0:T(8,128)S(1)} %broadcast_in_dim.0), channel_id=1, replica_groups=mesh['section'=4,'dp_0'=4,'dp_1'=4,'dp_2'=2] {'dp_0','dp_1','dp_2'}, dimensions={0} | all-to-all | bytes 262144 | tf_op jit(solution)/shard_map/cond/branch_1_fun/all_to_all | solution.py:386
  67.8 4.5 %collective-permute-start.13 = (f32[24,128]{1,0:T(8,128)S(1)}, f32[24,128]{1,0:T(8,128)S(1)}, u32[]{:S(2)}, u32[]{:S(2)}) collective-permute-start(f32[24,128]{1,0:T(8,128)S(1)} %pad_maximum_fusion.mine), channel_id=1, source_target_pairs={{0,64},{64,0},{32,96},{96,32},{1,65},{65,1},{33,97},{97,33},{2,66}... | collective-permute-start | bytes 36872 | tf_op jit(solution)/shard_map/ppermute | solution.py:480
  72.3 5.0 %collective-permute-start.12 = (f32[24,128]{1,0:T(8,128)S(1)}, f32[24,128]{1,0:T(8,128)S(1)}, u32[]{:S(2)}, u32[]{:S(2)}) collective-permute-start(f32[24,128]{1,0:T(8,128)S(1)} %pad_maximum_fusion.mine), channel_id=1, source_target_pairs={{0,96},{96,0},{32,64},{64,32},{1,97},{97,1},{33,65},{65,33},{2,98}... | collective-permute-start | bytes 36872 | tf_op jit(solution)/shard_map/ppermute | solution.py:480
  77.3 0.5 collective-permute-start.11
  77.7 0.0 collective-permute-done.13.far
  77.8 0.6 collective-permute-done.12.cross
  78.3 1.7 %collective-permute-done.11.next_ = f32[24,128]{1,0:T(8,128)S(1)} collective-permute-done((f32[24,128]{1,0:T(8,128)S(1)}, f32[24,128]{1,0:T(8,128)S(1)}, u32[]{:S(2)}, u32[]{:S(2)}) %collective-permute-start.11) | collective-permute-done | bytes 12320 | tf_op jit(solution)/shard_map/ppermute | solution.py:480
  80.0 0.0 copy-done
  80.0 1.3 %shard_map.114 = (f32[2,4,256]{2,1,0:T(4,128)}, f32[8]{0:T(128)}) custom-call(s32[8]{0:T(128)S(1)} %copy-done, f32[24,128]{1,0:T(8,128)S(1)} %pad_maximum_fusion.mine, f32[24,128]{1,0:T(8,128)S(1)} %collective-permute-done.11.next_, f32[24,128]{1,0:T(8,128)S(1)} %collective-permute-done.12.cross, f32[24,128]{1,0:T(8,128)S(1)} %collective-permute-done.13.far, ...), custom_call_target="tpu_custom_call" | custom-call | tf_op jit(solution)/shard_map/pallas_call | solution.py:482
  (7 shorter events, 0.1 us)
Async XLA Ops:
  1.8 24.3 %collective-permute-start.3 = (bf16[1024,128]{1,0:T(8,128)(2,1)S(1)}, bf16[1024,128]{1,0:T(8,128)(2,1)S(1)}, u32[]{:S(2)}, u32[]{:S(2)}) collective-permute-start(bf16[1024,128]{1,0:T(8,128)(2,1)S(1)} %get-tuple-element.48), channel_id=1, source_target_pairs={{0,32},{32,0},{64,96},{96,64},{1,33},{33,1},{65,97},{97,65},{2,34}... | collective-permute-start | bytes 786440 | tf_op jit(solution)/shard_map/ppermute | solution.py:415
  3.9 11.3 %collective-permute-start = (bf16[1040,128]{1,0:T(8,128)(2,1)S(1)}, bf16[1040,128]{1,0:T(8,128)(2,1)S(1)}, u32[]{:S(2)}, u32[]{:S(2)}) collective-permute-start(bf16[1040,128]{1,0:T(8,128)(2,1)S(1)} %get-tuple-element.45), channel_id=1, source_target_pairs={{0,32},{32,0},{64,96},{96,64},{1,33},{33,1},{65,97},{97,65},{2,34}... | collective-permute-start | bytes 798728 | tf_op jit(solution)/shard_map/ppermute | solution.py:414
  15.2 10.9 %collective-permute-start.4 = (bf16[1040,128]{1,0:T(8,128)(2,1)S(1)}, bf16[1040,128]{1,0:T(8,128)(2,1)S(1)}, u32[]{:S(2)}, u32[]{:S(2)}) collective-permute-start(bf16[1040,128]{1,0:T(8,128)(2,1)S(1)} %collective-permute-done.refs_0_), channel_id=1, source_target_pairs={{0,1},{1,0},{2,3},{3,2},{4,5},{5,4},{6,7},{7,6},{8,9},{9,8},{10,11... | collective-permute-start | bytes 798728 | tf_op jit(solution)/shard_map/ppermute | solution.py:381
  16.9 9.2 %collective-permute-start.2 = (bf16[1040,128]{1,0:T(8,128)(2,1)S(1)}, bf16[1040,128]{1,0:T(8,128)(2,1)S(1)}, u32[]{:S(2)}, u32[]{:S(2)}) collective-permute-start(bf16[1040,128]{1,0:T(8,128)(2,1)S(1)} %collective-permute-done.refs_0_), channel_id=1, source_target_pairs={{0,24},{8,0},{16,8},{24,16},{1,25},{9,1},{17,9},{25,17},{2,26},{10... | collective-permute-start | bytes 798728 | tf_op jit(solution)/shard_map/ppermute | solution.py:381
  19.9 8.9 %collective-permute-start.1 = (bf16[1040,128]{1,0:T(8,128)(2,1)S(1)}, bf16[1040,128]{1,0:T(8,128)(2,1)S(1)}, u32[]{:S(2)}, u32[]{:S(2)}) collective-permute-start(bf16[1040,128]{1,0:T(8,128)(2,1)S(1)} %collective-permute-done.refs_0_), channel_id=1, source_target_pairs={{0,8},{8,16},{16,24},{24,0},{1,9},{9,17},{17,25},{25,1},{2,10},{10... | collective-permute-start | bytes 798728 | tf_op jit(solution)/shard_map/ppermute | solution.py:381
  28.8 3.1 %collective-permute-start.6 = (bf16[1040,128]{1,0:T(8,128)(2,1)S(1)}, bf16[1040,128]{1,0:T(8,128)(2,1)S(1)}, u32[]{:S(2)}, u32[]{:S(2)}) collective-permute-start(bf16[1040,128]{1,0:T(8,128)(2,1)S(1)} %collective-permute-done.1.refs_2_), channel_id=1, source_target_pairs={{0,1},{1,0},{2,3},{3,2},{4,5},{5,4},{6,7},{7,6},{8,9},{9,8},{10,11... | collective-permute-start | bytes 798728 | tf_op jit(solution)/shard_map/ppermute | solution.py:381
  29.9 1.9 %collective-permute-start.7 = (bf16[1040,128]{1,0:T(8,128)(2,1)S(1)}, bf16[1040,128]{1,0:T(8,128)(2,1)S(1)}, u32[]{:S(2)}, u32[]{:S(2)}) collective-permute-start(bf16[1040,128]{1,0:T(8,128)(2,1)S(1)} %collective-permute-done.2.refs_3_), channel_id=1, source_target_pairs={{0,1},{1,0},{2,3},{3,2},{4,5},{5,4},{6,7},{7,6},{8,9},{9,8},{10,11... | collective-permute-start | bytes 798728 | tf_op jit(solution)/shard_map/ppermute | solution.py:381
  29.9 1.9 %collective-permute-start.5 = (bf16[1024,128]{1,0:T(8,128)(2,1)S(1)}, bf16[1024,128]{1,0:T(8,128)(2,1)S(1)}, u32[]{:S(2)}, u32[]{:S(2)}) collective-permute-start(bf16[1024,128]{1,0:T(8,128)(2,1)S(1)} %collective-permute-done.3.refs_1_), channel_id=1, source_target_pairs={{0,1},{1,0},{2,3},{3,2},{4,5},{5,4},{6,7},{7,6},{8,9},{9,8},{10,11... | collective-permute-start | bytes 786440 | tf_op jit(solution)/shard_map/ppermute | solution.py:381
  35.2 15.7 %collective-permute-start.8 = (bf16[1,24,1024]{2,1,0:T(8,128)(2,1)S(1)}, bf16[1,24,1024]{2,1,0:T(8,128)(2,1)S(1)}, u32[]{:S(2)}, u32[]{:S(2)}) collective-permute-start(bf16[1,24,1024]{2,1,0:T(8,128)(2,1)S(1)} %get-tuple-element.63), channel_id=1, source_target_pairs={{0,64},{1,65},{2,66},{3,67},{4,68},{5,69},{6,70},{7,71},{8,72},{9,... | collective-permute-start | bytes 147464 | tf_op jit(solution)/shard_map/ppermute | solution.py:466
  48.3 5.2 %collective-permute-start.9 = (bf16[2,24,1024]{2,1,0:T(8,128)(2,1)S(1)}, bf16[2,24,1024]{2,1,0:T(8,128)(2,1)S(1)}, u32[]{:S(2)}, u32[]{:S(2)}) collective-permute-start(bf16[2,24,1024]{2,1,0:T(8,128)(2,1)S(1)} %get-tuple-element.68), channel_id=1, source_target_pairs={{0,96},{32,64},{1,97},{33,65},{2,98},{34,66},{3,99},{35,67},{4,100... | collective-permute-start | bytes 294920 | tf_op jit(solution)/shard_map/ppermute | solution.py:470
  49.6 3.9 %collective-permute-start.10 = (bf16[2,24,1024]{2,1,0:T(8,128)(2,1)S(1)}, bf16[2,24,1024]{2,1,0:T(8,128)(2,1)S(1)}, u32[]{:S(2)}, u32[]{:S(2)}) collective-permute-start(bf16[2,24,1024]{2,1,0:T(8,128)(2,1)S(1)} %get-tuple-element.70), channel_id=1, source_target_pairs={{0,96},{32,64},{1,97},{33,65},{2,98},{34,66},{3,99},{35,67},{4,100... | collective-permute-start | bytes 294920 | tf_op jit(solution)/shard_map/ppermute | solution.py:468
  53.5 26.5 %copy-start = (s32[8]{0:T(128)S(1)}, s32[8]{0:T(128)}, u32[]{:S(2)}) copy-start(s32[8]{0:T(128)} %order.1) | copy-start | bytes 100
  67.8 10.0 %collective-permute-start.13 = (f32[24,128]{1,0:T(8,128)S(1)}, f32[24,128]{1,0:T(8,128)S(1)}, u32[]{:S(2)}, u32[]{:S(2)}) collective-permute-start(f32[24,128]{1,0:T(8,128)S(1)} %pad_maximum_fusion.mine), channel_id=1, source_target_pairs={{0,64},{64,0},{32,96},{96,32},{1,65},{65,1},{33,97},{97,33},{2,66}... | collective-permute-start | bytes 36872 | tf_op jit(solution)/shard_map/ppermute | solution.py:480
  72.3 6.1 %collective-permute-start.12 = (f32[24,128]{1,0:T(8,128)S(1)}, f32[24,128]{1,0:T(8,128)S(1)}, u32[]{:S(2)}, u32[]{:S(2)}) collective-permute-start(f32[24,128]{1,0:T(8,128)S(1)} %pad_maximum_fusion.mine), channel_id=1, source_target_pairs={{0,96},{96,0},{32,64},{64,32},{1,97},{97,1},{33,65},{65,33},{2,98}... | collective-permute-start | bytes 36872 | tf_op jit(solution)/shard_map/ppermute | solution.py:480
  77.3 2.8 %collective-permute-start.11 = (f32[24,128]{1,0:T(8,128)S(1)}, f32[24,128]{1,0:T(8,128)S(1)}, u32[]{:S(2)}, u32[]{:S(2)}) collective-permute-start(f32[24,128]{1,0:T(8,128)S(1)} %pad_maximum_fusion.mine), channel_id=1, source_target_pairs={{0,32},{32,0},{64,96},{96,64},{1,33},{33,1},{65,97},{97,65},{2,34}... | collective-permute-start | bytes 36872 | tf_op jit(solution)/shard_map/ppermute | solution.py:480

commit v2 on v1

--- a/solution.py
+++ b/solution.py
@@ -84,7 +84,7 @@
     gain_copy.start()
 
     def copies(target, on, at):
-        colour = lax.rem(lax.axis_index("dp_0") + 2 * lax.axis_index("dp_1") + on, 4)
+        colour = lax.rem(lax.axis_index("dp_0") + lax.axis_index("dp_1") + on, 4)
         lanes = pl.ds(pl.multiple_of(colour * 128, 128), 128)
         lower = [
             pltpu.make_async_copy(
@@ -381,6 +381,19 @@
     return lax.ppermute(x, axis, [(i, (i + by) % n) for i in range(n)])
 
 
+def around(x, by):
+    n, m = lax.axis_size("dp_0"), lax.axis_size("dp_1")
+    pairs = []
+    for i in range(n):
+        for j in range(m):
+            along_0 = (((i + by) % n) * m + j) * 2
+            along_1 = (i * m + (j + by) % m) * 2
+            targets = (along_0, along_1) if by == 1 else (along_1, along_0)
+            pairs.append(((i * m + j) * 2, targets[0]))
+            pairs.append(((i * m + j) * 2 + 1, targets[1] + 1))
+    return lax.ppermute(x, DP, pairs)
+
+
 def plane_sum(x):
     n = lax.axis_size(DP)
     return jnp.sum(lax.all_to_all(jnp.broadcast_to(x[None], (n, *x.shape)), DP, 0, 0), axis=0)
@@ -429,8 +442,8 @@
         blocks=2,
     )(pool, index, taps, out_weight, gain, qwt, qbias, post_weight)
     mine, v = lax.optimization_barrier((mine, v))
-    up = shifted(mine, "dp_0", 1)
-    down = shifted(mine, "dp_0", -1)
+    up = around(mine, 1)
+    down = around(mine, -1)
     mine_s = shifted(mine, "dp_2", 1)
     (v,) = call(
         functools.partial(more_body, 2, STEPS), [VM] * 4, [v_kind], blocks=3, aliases={0: 0}
@@ -461,13 +474,12 @@
             blocks=2 * n,
         )(v, *weights, post, codes)[0]
 
-    to_cross = ((0, 3), (1, 2))
     codes, stats = encode((0,), (), False)
-    codes_a = lax.ppermute(codes, "section", ((0, 2),))
+    codes_a = lax.ppermute(codes, "section", FAR)
     codes, stats = encode((1, 2), (stats,), False)
-    codes_b = lax.ppermute(codes, "section", to_cross)
+    codes_b = lax.ppermute(codes, "section", CROSS)
     codes, stats = encode((3, 4), (stats,), True)
-    codes_c = lax.ppermute(codes, "section", to_cross)
+    codes_c = lax.ppermute(codes, "section", ((0, 3), (1, 2)))
     codes_a, stats = lax.optimization_barrier((codes_a, stats))
     e0 = decode((0,), codes_a)
     codes_b, e0 = lax.optimization_barrier((codes_b, e0))

time: 82.6 us -> 79.9 us (0.967)
  starting transfers between devices: 23 us -> 21.7 us
  blocking collectives: 14.1 us -> 13 us
    ppermute x6 -> x4, starting transfers between devices: 6.29 us -> 3.49 us  [shifted(): return lax.ppermute(x, axis, [(i, (i + by) % n) for i in range(n)])]
    ppermute x6 -> x4, waiting for transfers between devices: 4.06 us -> 1.42 us  [shifted(): return lax.ppermute(x, axis, [(i, (i + by) % n) for i in range(n)])]
    ppermute x3 -> x5, waiting for transfers between devices: 2.56 us -> 5.16 us  [the longest x1 5.15 us: on_device(): codes_b = lax.ppermute(codes, 'section', CROSS)]
    ppermute x3 -> x5, starting transfers between devices: 4.52 us -> 6.08 us  [the longest x2 4.62 us: around(): return lax.ppermute(x, DP, pairs)]
    all_to_all x1, blocking collectives: 14.1 us -> 13 us  [plane_sum(): lax.all_to_all(jnp.broadcast_to(x[None], (n, *x.shape)), DP, 0, 0)]
  transfers between devices with their start and end apart: 14 -> 14, of which waited for: 6 -> 5; matrix products, arithmetic and copies ran while one was open for 0% -> 0% of each run, Pallas kernels for 30% -> 31%
where the time goes in v2:
time: 79.9 us; the launch traced here: 78.7 us
  Pallas kernels  29.9 us (37%)
  starting transfers between devices  21.7 us (27%)
  waiting for transfers between devices  13.1 us (16%)
  blocking collectives  13 us (16%)
    pallas_call x3, Pallas kernels, encode(): call(functools.partial(encode_body, steps, last), [VM] * (6 + len(before)...  13.9 us
    all_to_all x1, blocking collectives, plane_sum(): lax.all_to_all(jnp.broadcast_to(x[None], (n, *x.shape)), DP, 0, 0)  13 us
    ppermute x3, starting transfers between devices, on_device(): lax.ppermute(packed, 'section', pairs)  9.97 us
    pallas_call x1, Pallas kernels, on_device(): call(functools.partial(start_body, 2), [HB] * 8, [v_kind, *kinds, ((C, 12...  6.71 us
    pallas_call x1, Pallas kernels, on_device(): call(functools.partial(more_body, 2, STEPS), [VM] * 4, [v_kind], blocks=3...  6.2 us
    ppermute x1, waiting for transfers between devices, on_device(): codes_b = lax.ppermute(codes, 'section', CROSS)  5.15 us
    ppermute x2, starting transfers between devices, around(): return lax.ppermute(x, DP, pairs)  4.62 us
    ppermute x1, waiting for transfers between devices, on_device(): mine = lax.ppermute(piece, 'section', PAIR)  4.51 us
  transfers between devices with their start and end apart: 14, of which 5 were waited for; matrix products, arithmetic and copies ran while one was open for 0% of the time, Pallas kernels for 31%

profile of v2, /device:TPU:1, one launch (start us, length us, event | category | flops | bytes accessed | tf_op | source)
XLA Modules:
  0.0 78.7 jit_solution(1677663761318843937)
XLA Ops:
  0.6 1.2 %shard_map.104 = (bf16[1040,128]{1,0:T(8,128)(2,1)S(1)}, bf16[1024,128]{1,0:T(8,128)(2,1)S(1)}) custom-call(bf16[1536,512]{1,0:T(8,128)(2,1)} %bitcast.9, bf16[512,512]{1,0:T(8,128)(2,1)} %bitcast.11, bf16[1,512]{1,0:T(2,128)(2,1)} %gain_hbm.1), custom_call_target="tpu_custom_call" | custom-call | tf_op jit(solution)/shard_map/pallas_call | solution.py:421
  1.8 2.1 %collective-permute-start.3 = (bf16[1024,128]{1,0:T(8,128)(2,1)S(1)}, bf16[1024,128]{1,0:T(8,128)(2,1)S(1)}, u32[]{:S(2)}, u32[]{:S(2)}) collective-permute-start(bf16[1024,128]{1,0:T(8,128)(2,1)S(1)} %get-tuple-element.48), channel_id=1, source_target_pairs={{0,32},{32,0},{64,96},{96,64},{1,33},{33,1},{65,97},{97,65},{2,34}... | collective-permute-start | bytes 786440 | tf_op jit(solution)/shard_map/ppermute | solution.py:428
  3.9 0.1 collective-permute-start
  4.0 6.7 %shard_map.105 = (bf16[5,4,256,512]{3,2,1,0:T(8,128)(2,1)S(1)}, bf16[2,1536,512]{2,1,0:T(8,128)(2,1)S(1)}, bf16[2,512,512]{2,1,0:T(8,128)(2,1)S(1)}, f32[2,8,512...) custom-call(bf16[32,256,512]{2,1,0:T(8,128)(2,1)} %pool.1, ...), custom_call_target="tpu_custom_call" | custom-call | flops 4294967296 | tf_op jit(solution)/shard_map/pallas_call | solution.py:430
  10.7 4.5 %collective-permute-done.refs_0_ = bf16[1040,128]{1,0:T(8,128)(2,1)S(1)} collective-permute-done((bf16[1040,128]{1,0:T(8,128)(2,1)S(1)}, bf16[1040,128]{1,0:T(8,128)(2,1)S(1)}, u32[]{:S(2)}, u32[]{:S(2)}) %collective-permute-start) | collective-permute-done | bytes 266272 | tf_op jit(solution)/shard_map/ppermute | solution.py:427
  15.2 1.7 %collective-permute-start.4 = (bf16[1040,128]{1,0:T(8,128)(2,1)S(1)}, bf16[1040,128]{1,0:T(8,128)(2,1)S(1)}, u32[]{:S(2)}, u32[]{:S(2)}) collective-permute-start(bf16[1040,128]{1,0:T(8,128)(2,1)S(1)} %collective-permute-done.refs_0_), channel_id=1, source_target_pairs={{0,1},{1,0},{2,3},{3,2},{4,5},{5,4},{6,7},{7,6},{8,9},{9,8},{10,11... | collective-permute-start | bytes 798728 | tf_op jit(solution)/shard_map/ppermute | solution.py:381
  16.9 3.0 %collective-permute-start.2 = (bf16[1040,128]{1,0:T(8,128)(2,1)S(1)}, bf16[1040,128]{1,0:T(8,128)(2,1)S(1)}, u32[]{:S(2)}, u32[]{:S(2)}) collective-permute-start(bf16[1040,128]{1,0:T(8,128)(2,1)S(1)} %collective-permute-done.refs_0_), channel_id=1, source_target_pairs={{0,6},{1,25},{2,0},{3,27},{4,2},{5,29},{6,4},{7,31},{8,14},{9,1},{... | collective-permute-start | bytes 798728 | tf_op jit(solution)/shard_map/ppermute | solution.py:394
  19.9 1.6 %collective-permute-start.1 = (bf16[1040,128]{1,0:T(8,128)(2,1)S(1)}, bf16[1040,128]{1,0:T(8,128)(2,1)S(1)}, u32[]{:S(2)}, u32[]{:S(2)}) collective-permute-start(bf16[1040,128]{1,0:T(8,128)(2,1)S(1)} %collective-permute-done.refs_0_), channel_id=1, source_target_pairs={{0,8},{1,3},{2,10},{3,5},{4,12},{5,7},{6,14},{7,1},{8,16},{9,11},{... | collective-permute-start | bytes 798728 | tf_op jit(solution)/shard_map/ppermute | solution.py:394
  21.5 6.2 %shard_map.106.v = bf16[5,4,256,512]{3,2,1,0:T(8,128)(2,1)S(1)} custom-call(bf16[5,4,256,512]{3,2,1,0:T(8,128)(2,1)S(1)} %get-tuple-element.49.before, bf16[2,1536,512]{2,1,0:T(8,128)(2,1)S(1)} %get-tuple-element.50.all_taps.refs_8_, bf16[2,512,512]{2,1,0:T(8,128)(2,1)S(1)} %get-tuple-element.51.all_out.refs_9_, ...), custom_call_target="tpu_custom_call", output_to_operand_aliasing={{}: (0, {})} | custom-call | flops 6442450944 | tf_op jit(solution)/shard_map/pallas_call | solution.py:448
  27.7 0.0 collective-permute-done.3.refs_1_
  27.7 0.0 collective-permute-done.4.refs_4_
  27.7 0.0 collective-permute-done.2.refs_3_
  27.8 0.0 collective-permute-done.1.refs_2_
  27.8 1.3 %collective-permute-start.6 = (bf16[1040,128]{1,0:T(8,128)(2,1)S(1)}, bf16[1040,128]{1,0:T(8,128)(2,1)S(1)}, u32[]{:S(2)}, u32[]{:S(2)}) collective-permute-start(bf16[1040,128]{1,0:T(8,128)(2,1)S(1)} %collective-permute-done.1.refs_2_), channel_id=1, source_target_pairs={{0,1},{1,0},{2,3},{3,2},{4,5},{5,4},{6,7},{7,6},{8,9},{9,8},{10,11... | collective-permute-start | bytes 798728 | tf_op jit(solution)/shard_map/ppermute | solution.py:381
  29.1 0.1 collective-permute-start.7
  29.2 0.4 collective-permute-start.5
  29.6 1.4 %collective-permute-done.5.refs_5_ = bf16[1024,128]{1,0:T(8,128)(2,1)S(1)} collective-permute-done((bf16[1024,128]{1,0:T(8,128)(2,1)S(1)}, bf16[1024,128]{1,0:T(8,128)(2,1)S(1)}, u32[]{:S(2)}, u32[]{:S(2)}) %collective-permute-start.5) | collective-permute-done | bytes 262176 | tf_op jit(solution)/shard_map/ppermute | solution.py:381
  31.0 0.0 collective-permute-done.6.refs_6_
  31.0 0.0 collective-permute-done.7.refs_7_
  31.0 0.6 shard_map.107
  31.7 2.7 %shard_map.108 = (bf16[1,24,1024]{2,1,0:T(8,128)(2,1)S(1)}, f32[24,128]{1,0:T(8,128)S(1)}) custom-call(bf16[5,4,256,512]{3,2,1,0:T(8,128)(2,1)S(1)} %shard_map.106.v, bf16[2,1536,512]{2,1,0:T(8,128)(2,1)S(1)} %get-tuple-element.58.all_taps, bf16[2,512,512]{2,1,0:T(8,128)(2,1)S(1)} %get-tuple-element.59.all_out, f32[2,8,512]{2,1,0:T(8,128)S(1)} %get-tuple-element.60.all_gain, ...), custom_call_target="tpu_custom_call" | custom-call | flops 4294967296 | tf_op jit(solution)/shard_map/pallas_call | solution.py:459
  34.4 0.1 collective-permute-start.8
  34.5 5.6 %shard_map.109 = (bf16[2,24,1024]{2,1,0:T(8,128)(2,1)S(1)}, f32[24,128]{1,0:T(8,128)S(1)}) custom-call(bf16[5,4,256,512]{3,2,1,0:T(8,128)(2,1)S(1)} %shard_map.106.v, bf16[2,1536,512]{2,1,0:T(8,128)(2,1)S(1)} %get-tuple-element.58.all_taps, bf16[2,512,512]{2,1,0:T(8,128)(2,1)S(1)} %get-tuple-element.59.all_out, f32[2,8,512]{2,1,0:T(8,128)S(1)} %get-tuple-element.60.all_gain, ...), custom_call_target="tpu_custom_call" | custom-call | flops 8589934592 | tf_op jit(solution)/shard_map/pallas_call | solution.py:459
  40.2 5.5 %shard_map.110 = (bf16[2,24,1024]{2,1,0:T(8,128)(2,1)S(1)}, f32[8,128]{1,0:T(8,128)S(1)}) custom-call(bf16[5,4,256,512]{3,2,1,0:T(8,128)(2,1)S(1)} %shard_map.106.v, bf16[2,1536,512]{2,1,0:T(8,128)(2,1)S(1)} %get-tuple-element.58.all_taps, bf16[2,512,512]{2,1,0:T(8,128)(2,1)S(1)} %get-tuple-element.59.all_out, f32[2,8,512]{2,1,0:T(8,128)S(1)} %get-tuple-element.60.all_gain, ...), custom_call_target="tpu_custom_call" | custom-call | flops 8589934592 | tf_op jit(solution)/shard_map/pallas_call | solution.py:459
  45.7 1.3 %collective-permute-start.9 = (bf16[2,24,1024]{2,1,0:T(8,128)(2,1)S(1)}, bf16[2,24,1024]{2,1,0:T(8,128)(2,1)S(1)}, u32[]{:S(2)}, u32[]{:S(2)}) collective-permute-start(bf16[2,24,1024]{2,1,0:T(8,128)(2,1)S(1)} %get-tuple-element.68), channel_id=1, source_target_pairs={{0,96},{32,64},{1,97},{33,65},{2,98},{34,66},{3,99},{35,67},{4,100... | collective-permute-start | bytes 294920 | tf_op jit(solution)/shard_map/ppermute | solution.py:482
  47.0 0.1 collective-permute-start.10
  47.1 0.0 collective-permute-done.8.codes
  47.1 5.1 %collective-permute-done.10.codes = bf16[2,24,1024]{2,1,0:T(8,128)(2,1)S(1)} collective-permute-done((bf16[2,24,1024]{2,1,0:T(8,128)(2,1)S(1)}, bf16[2,24,1024]{2,1,0:T(8,128)(2,1)S(1)}, u32[]{:S(2)}, u32[]{:S(2)}) %collective-permute-start.10) | collective-permute-done | bytes 98336 | tf_op jit(solution)/shard_map/ppermute | solution.py:480
  52.3 0.0 copy-start
  52.3 0.0 collective-permute-done.9.codes
  52.3 13.1 %conditional.1 = (f32[8,128]{1,0:T(8,128)S(1)}) conditional(s32[]{:T(128)} %convert_element_type.7, f32[8,128]{1,0:T(8,128)S(1)} %get-tuple-element.77, f32[8,128]{1,0:T(8,128)S(1)} %get-tuple-element.77), branch_computations={%region_0.0_spmd, %region_1.0_spmd} | conditional | flops 31744 | bytes 532492 | solution.py:490
  52.3 13.0 %all_to_all.4 = f32[32,8,128]{2,1,0:T(8,128)S(1)} all-to-all(f32[32,8,128]{2,1,0:T(8,128)S(1)} %broadcast_in_dim.0), channel_id=1, replica_groups=mesh['section'=4,'dp_0'=4,'dp_1'=4,'dp_2'=2] {'dp_0','dp_1','dp_2'}, dimensions={0} | all-to-all | bytes 262144 | tf_op jit(solution)/shard_map/cond/branch_1_fun/all_to_all | solution.py:399
  65.4 7.3 %collective-permute-start.13 = (f32[24,128]{1,0:T(8,128)S(1)}, f32[24,128]{1,0:T(8,128)S(1)}, u32[]{:S(2)}, u32[]{:S(2)}) collective-permute-start(f32[24,128]{1,0:T(8,128)S(1)} %pad_maximum_fusion.mine), channel_id=1, source_target_pairs={{0,64},{64,0},{32,96},{96,32},{1,65},{65,1},{33,97},{97,33},{2,66}... | collective-permute-start | bytes 36872 | tf_op jit(solution)/shard_map/ppermute | solution.py:492
  72.7 2.2 %collective-permute-start.12 = (f32[24,128]{1,0:T(8,128)S(1)}, f32[24,128]{1,0:T(8,128)S(1)}, u32[]{:S(2)}, u32[]{:S(2)}) collective-permute-start(f32[24,128]{1,0:T(8,128)S(1)} %pad_maximum_fusion.mine), channel_id=1, source_target_pairs={{0,96},{96,0},{32,64},{64,32},{1,97},{97,1},{33,65},{65,33},{2,98}... | collective-permute-start | bytes 36872 | tf_op jit(solution)/shard_map/ppermute | solution.py:492
  74.9 0.5 collective-permute-start.11
  75.4 0.0 collective-permute-done.13.far
  75.4 1.1 %collective-permute-done.12.cross = f32[24,128]{1,0:T(8,128)S(1)} collective-permute-done((f32[24,128]{1,0:T(8,128)S(1)}, f32[24,128]{1,0:T(8,128)S(1)}, u32[]{:S(2)}, u32[]{:S(2)}) %collective-permute-start.12) | collective-permute-done | bytes 12320 | tf_op jit(solution)/shard_map/ppermute | solution.py:492
  76.4 1.0 %collective-permute-done.11.next_ = f32[24,128]{1,0:T(8,128)S(1)} collective-permute-done((f32[24,128]{1,0:T(8,128)S(1)}, f32[24,128]{1,0:T(8,128)S(1)}, u32[]{:S(2)}, u32[]{:S(2)}) %collective-permute-start.11) | collective-permute-done | bytes 12320 | tf_op jit(solution)/shard_map/ppermute | solution.py:492
  77.4 0.0 copy-done
  77.4 1.3 %shard_map.114 = (f32[2,4,256]{2,1,0:T(4,128)}, f32[8]{0:T(128)}) custom-call(s32[8]{0:T(128)S(1)} %copy-done, f32[24,128]{1,0:T(8,128)S(1)} %pad_maximum_fusion.mine, f32[24,128]{1,0:T(8,128)S(1)} %collective-permute-done.11.next_, f32[24,128]{1,0:T(8,128)S(1)} %collective-permute-done.12.cross, f32[24,128]{1,0:T(8,128)S(1)} %collective-permute-done.13.far, ...), custom_call_target="tpu_custom_call" | custom-call | tf_op jit(solution)/shard_map/pallas_call | solution.py:494
  (7 shorter events, 0.1 us)
Async XLA Ops:
  1.8 25.9 %collective-permute-start.3 = (bf16[1024,128]{1,0:T(8,128)(2,1)S(1)}, bf16[1024,128]{1,0:T(8,128)(2,1)S(1)}, u32[]{:S(2)}, u32[]{:S(2)}) collective-permute-start(bf16[1024,128]{1,0:T(8,128)(2,1)S(1)} %get-tuple-element.48), channel_id=1, source_target_pairs={{0,32},{32,0},{64,96},{96,64},{1,33},{33,1},{65,97},{97,65},{2,34}... | collective-permute-start | bytes 786440 | tf_op jit(solution)/shard_map/ppermute | solution.py:428
  3.9 11.3 %collective-permute-start = (bf16[1040,128]{1,0:T(8,128)(2,1)S(1)}, bf16[1040,128]{1,0:T(8,128)(2,1)S(1)}, u32[]{:S(2)}, u32[]{:S(2)}) collective-permute-start(bf16[1040,128]{1,0:T(8,128)(2,1)S(1)} %get-tuple-element.45), channel_id=1, source_target_pairs={{0,32},{32,0},{64,96},{96,64},{1,33},{33,1},{65,97},{97,65},{2,34}... | collective-permute-start | bytes 798728 | tf_op jit(solution)/shard_map/ppermute | solution.py:427
  15.2 12.5 %collective-permute-start.4 = (bf16[1040,128]{1,0:T(8,128)(2,1)S(1)}, bf16[1040,128]{1,0:T(8,128)(2,1)S(1)}, u32[]{:S(2)}, u32[]{:S(2)}) collective-permute-start(bf16[1040,128]{1,0:T(8,128)(2,1)S(1)} %collective-permute-done.refs_0_), channel_id=1, source_target_pairs={{0,1},{1,0},{2,3},{3,2},{4,5},{5,4},{6,7},{7,6},{8,9},{9,8},{10,11... | collective-permute-start | bytes 798728 | tf_op jit(solution)/shard_map/ppermute | solution.py:381
  16.9 10.8 %collective-permute-start.2 = (bf16[1040,128]{1,0:T(8,128)(2,1)S(1)}, bf16[1040,128]{1,0:T(8,128)(2,1)S(1)}, u32[]{:S(2)}, u32[]{:S(2)}) collective-permute-start(bf16[1040,128]{1,0:T(8,128)(2,1)S(1)} %collective-permute-done.refs_0_), channel_id=1, source_target_pairs={{0,6},{1,25},{2,0},{3,27},{4,2},{5,29},{6,4},{7,31},{8,14},{9,1},{... | collective-permute-start | bytes 798728 | tf_op jit(solution)/shard_map/ppermute | solution.py:394
  19.9 7.9 %collective-permute-start.1 = (bf16[1040,128]{1,0:T(8,128)(2,1)S(1)}, bf16[1040,128]{1,0:T(8,128)(2,1)S(1)}, u32[]{:S(2)}, u32[]{:S(2)}) collective-permute-start(bf16[1040,128]{1,0:T(8,128)(2,1)S(1)} %collective-permute-done.refs_0_), channel_id=1, source_target_pairs={{0,8},{1,3},{2,10},{3,5},{4,12},{5,7},{6,14},{7,1},{8,16},{9,11},{... | collective-permute-start | bytes 798728 | tf_op jit(solution)/shard_map/ppermute | solution.py:394
  27.8 3.3 %collective-permute-start.6 = (bf16[1040,128]{1,0:T(8,128)(2,1)S(1)}, bf16[1040,128]{1,0:T(8,128)(2,1)S(1)}, u32[]{:S(2)}, u32[]{:S(2)}) collective-permute-start(bf16[1040,128]{1,0:T(8,128)(2,1)S(1)} %collective-permute-done.1.refs_2_), channel_id=1, source_target_pairs={{0,1},{1,0},{2,3},{3,2},{4,5},{5,4},{6,7},{7,6},{8,9},{9,8},{10,11... | collective-permute-start | bytes 798728 | tf_op jit(solution)/shard_map/ppermute | solution.py:381
  29.1 1.9 %collective-permute-start.7 = (bf16[1040,128]{1,0:T(8,128)(2,1)S(1)}, bf16[1040,128]{1,0:T(8,128)(2,1)S(1)}, u32[]{:S(2)}, u32[]{:S(2)}) collective-permute-start(bf16[1040,128]{1,0:T(8,128)(2,1)S(1)} %collective-permute-done.2.refs_3_), channel_id=1, source_target_pairs={{0,1},{1,0},{2,3},{3,2},{4,5},{5,4},{6,7},{7,6},{8,9},{9,8},{10,11... | collective-permute-start | bytes 798728 | tf_op jit(solution)/shard_map/ppermute | solution.py:381
  29.2 1.8 %collective-permute-start.5 = (bf16[1024,128]{1,0:T(8,128)(2,1)S(1)}, bf16[1024,128]{1,0:T(8,128)(2,1)S(1)}, u32[]{:S(2)}, u32[]{:S(2)}) collective-permute-start(bf16[1024,128]{1,0:T(8,128)(2,1)S(1)} %collective-permute-done.3.refs_1_), channel_id=1, source_target_pairs={{0,1},{1,0},{2,3},{3,2},{4,5},{5,4},{6,7},{7,6},{8,9},{9,8},{10,11... | collective-permute-start | bytes 786440 | tf_op jit(solution)/shard_map/ppermute | solution.py:381
  34.4 12.7 %collective-permute-start.8 = (bf16[1,24,1024]{2,1,0:T(8,128)(2,1)S(1)}, bf16[1,24,1024]{2,1,0:T(8,128)(2,1)S(1)}, u32[]{:S(2)}, u32[]{:S(2)}) collective-permute-start(bf16[1,24,1024]{2,1,0:T(8,128)(2,1)S(1)} %get-tuple-element.63), channel_id=1, source_target_pairs={{0,64},{64,0},{32,96},{96,32},{1,65},{65,1},{33,97},{97,33},{2,66}... | collective-permute-start | bytes 147464 | tf_op jit(solution)/shard_map/ppermute | solution.py:478
  45.7 6.6 %collective-permute-start.9 = (bf16[2,24,1024]{2,1,0:T(8,128)(2,1)S(1)}, bf16[2,24,1024]{2,1,0:T(8,128)(2,1)S(1)}, u32[]{:S(2)}, u32[]{:S(2)}) collective-permute-start(bf16[2,24,1024]{2,1,0:T(8,128)(2,1)S(1)} %get-tuple-element.68), channel_id=1, source_target_pairs={{0,96},{32,64},{1,97},{33,65},{2,98},{34,66},{3,99},{35,67},{4,100... | collective-permute-start | bytes 294920 | tf_op jit(solution)/shard_map/ppermute | solution.py:482
  47.0 5.3 %collective-permute-start.10 = (bf16[2,24,1024]{2,1,0:T(8,128)(2,1)S(1)}, bf16[2,24,1024]{2,1,0:T(8,128)(2,1)S(1)}, u32[]{:S(2)}, u32[]{:S(2)}) collective-permute-start(bf16[2,24,1024]{2,1,0:T(8,128)(2,1)S(1)} %get-tuple-element.70), channel_id=1, source_target_pairs={{0,96},{96,0},{32,64},{64,32},{1,97},{97,1},{33,65},{65,33},{2,98}... | collective-permute-start | bytes 294920 | tf_op jit(solution)/shard_map/ppermute | solution.py:480
  52.3 25.2 %copy-start = (s32[8]{0:T(128)S(1)}, s32[8]{0:T(128)}, u32[]{:S(2)}) copy-start(s32[8]{0:T(128)} %order.1) | copy-start | bytes 100
  65.4 10.0 %collective-permute-start.13 = (f32[24,128]{1,0:T(8,128)S(1)}, f32[24,128]{1,0:T(8,128)S(1)}, u32[]{:S(2)}, u32[]{:S(2)}) collective-permute-start(f32[24,128]{1,0:T(8,128)S(1)} %pad_maximum_fusion.mine), channel_id=1, source_target_pairs={{0,64},{64,0},{32,96},{96,32},{1,65},{65,1},{33,97},{97,33},{2,66}... | collective-permute-start | bytes 36872 | tf_op jit(solution)/shard_map/ppermute | solution.py:492
  72.7 3.8 %collective-permute-start.12 = (f32[24,128]{1,0:T(8,128)S(1)}, f32[24,128]{1,0:T(8,128)S(1)}, u32[]{:S(2)}, u32[]{:S(2)}) collective-permute-start(f32[24,128]{1,0:T(8,128)S(1)} %pad_maximum_fusion.mine), channel_id=1, source_target_pairs={{0,96},{96,0},{32,64},{64,32},{1,97},{97,1},{33,65},{65,33},{2,98}... | collective-permute-start | bytes 36872 | tf_op jit(solution)/shard_map/ppermute | solution.py:492
  74.9 2.5 %collective-permute-start.11 = (f32[24,128]{1,0:T(8,128)S(1)}, f32[24,128]{1,0:T(8,128)S(1)}, u32[]{:S(2)}, u32[]{:S(2)}) collective-permute-start(f32[24,128]{1,0:T(8,128)S(1)} %pad_maximum_fusion.mine), channel_id=1, source_target_pairs={{0,32},{32,0},{64,96},{96,64},{1,33},{33,1},{65,97},{97,65},{2,34}... | collective-permute-start | bytes 36872 | tf_op jit(solution)/shard_map/ppermute | solution.py:492

commit v3 on v2

--- a/solution.py
+++ b/solution.py
@@ -83,8 +83,9 @@
     gain_copy = pltpu.make_async_copy(gain_hbm, gain, sems.at[10])
     gain_copy.start()
 
-    def copies(target, on, at):
-        colour = lax.rem(lax.axis_index("dp_0") + lax.axis_index("dp_1") + on, 4)
+    own = 2 * lax.rem(lax.axis_index("dp_0"), 2) + lax.rem(lax.axis_index("dp_1"), 2)
+
+    def copies(target, colour, at):
         lanes = pl.ds(pl.multiple_of(colour * 128, 128), 128)
         lower = [
             pltpu.make_async_copy(
@@ -106,7 +107,7 @@
             )
         return lower, upper
 
-    sets = [copies(piece, 0, 0), copies(second, 2, 5)]
+    sets = [copies(piece, own, 0), copies(second, 3 - own, 5)]
     for side in range(2):
 
         @pl.when(core == side)
@@ -381,16 +382,14 @@
     return lax.ppermute(x, axis, [(i, (i + by) % n) for i in range(n)])
 
 
-def around(x, by):
+def within_corner(x, first):
     n, m = lax.axis_size("dp_0"), lax.axis_size("dp_1")
     pairs = []
     for i in range(n):
         for j in range(m):
-            along_0 = (((i + by) % n) * m + j) * 2
-            along_1 = (i * m + (j + by) % m) * 2
-            targets = (along_0, along_1) if by == 1 else (along_1, along_0)
-            pairs.append(((i * m + j) * 2, targets[0]))
-            pairs.append(((i * m + j) * 2 + 1, targets[1] + 1))
+            for core in range(2):
+                to = (i ^ 1, j) if (core == 0) == first else (i, j ^ 1)
+                pairs.append(((i * m + j) * 2 + core, (to[0] * m + to[1]) * 2 + core))
     return lax.ppermute(x, DP, pairs)
 
 
@@ -442,14 +441,14 @@
         blocks=2,
     )(pool, index, taps, out_weight, gain, qwt, qbias, post_weight)
     mine, v = lax.optimization_barrier((mine, v))
-    up = around(mine, 1)
-    down = around(mine, -1)
+    up = within_corner(mine, True)
+    down = within_corner(mine, False)
     mine_s = shifted(mine, "dp_2", 1)
     (v,) = call(
         functools.partial(more_body, 2, STEPS), [VM] * 4, [v_kind], blocks=3, aliases={0: 0}
     )(v, *weights)
     up, down, second, mine_s, v = lax.optimization_barrier((up, down, second, mine_s, v))
-    swapped = [mine_s] + [shifted(x, "dp_2", 1) for x in (second, up, down)]
+    swapped = [mine_s] + [shifted(x, "dp_2", 1) for x in (second, down, up)]
     weights = call(
         join_body, [VM] + [ANY] * 7 + [VM] * 3, kinds, [dma((24,))], aliases={8: 0, 9: 1, 10: 2}
     )(mine, second, up, down, *swapped, *weights)
@@ -477,12 +476,12 @@
     codes, stats = encode((0,), (), False)
     codes_a = lax.ppermute(codes, "section", FAR)
     codes, stats = encode((1, 2), (stats,), False)
+    e0 = decode((0,), codes_a)
+    codes, e0 = lax.optimization_barrier((codes, e0))
     codes_b = lax.ppermute(codes, "section", CROSS)
     codes, stats = encode((3, 4), (stats,), True)
     codes_c = lax.ppermute(codes, "section", ((0, 3), (1, 2)))
-    codes_a, stats = lax.optimization_barrier((codes_a, stats))
-    e0 = decode((0,), codes_a)
-    codes_b, e0 = lax.optimization_barrier((codes_b, e0))
+    codes_b, stats = lax.optimization_barrier((codes_b, stats))
     e12 = decode((1, 2), codes_b)
     codes_c, e12 = lax.optimization_barrier((codes_c, e12))
     e34 = decode((3, 4), codes_c)

time: 79.9 us -> 73.9 us (0.925)
  starting transfers between devices: 21.7 us -> 16 us
  blocking collectives: 13 us -> 15.8 us
  waiting for transfers between devices: 13.1 us -> 10.5 us
    ppermute x1, waiting for transfers between devices: 5.15 us -> 0.01 us  [on_device(): codes_b = lax.ppermute(codes, 'section', CROSS)]
    ppermute x3, starting transfers between devices: 9.97 us -> 6.3 us  [on_device(): lax.ppermute(packed, 'section', pairs)]
    all_to_all x1, blocking collectives: 13 us -> 15.8 us  [plane_sum(): lax.all_to_all(jnp.broadcast_to(x[None], (n, *x.shape)), DP, 0, 0)]
    ppermute x1, waiting for transfers between devices: 0.01 us -> 2 us  [on_device(): codes_c = lax.ppermute(codes, 'section', ((0, 3), (1, 2)))]
    ppermute x2, starting transfers between devices: 4.62 us -> 3.18 us  [within_corner(): return lax.ppermute(x, DP, pairs)]
  transfers between devices with their start and end apart: 14 -> 14, of which waited for: 5 -> 5; matrix products, arithmetic and copies ran while one was open for 0% -> 0% of each run, Pallas kernels for 31% -> 33%
where the time goes in v3:
time: 73.9 us; the launch traced here: 73 us
  Pallas kernels  30 us (41%)
  starting transfers between devices  16 us (22%)
  blocking collectives  15.8 us (21%)
  waiting for transfers between devices  10.5 us (14%)
  between operations  0.79 us (1%)
    all_to_all x1, blocking collectives, plane_sum(): lax.all_to_all(jnp.broadcast_to(x[None], (n, *x.shape)), DP, 0, 0)  15.8 us
    pallas_call x3, Pallas kernels, encode(): call(functools.partial(encode_body, steps, last), [VM] * (6 + len(before)...  13.9 us
    pallas_call x1, Pallas kernels, on_device(): call(functools.partial(start_body, 2), [HB] * 8, [v_kind, *kinds, ((C, 12...  6.71 us
    ppermute x3, starting transfers between devices, on_device(): lax.ppermute(packed, 'section', pairs)  6.3 us
    pallas_call x1, Pallas kernels, on_device(): call(functools.partial(more_body, 2, STEPS), [VM] * 4, [v_kind], blocks=3...  6.19 us
    ppermute x1, waiting for transfers between devices, on_device(): mine = lax.ppermute(piece, 'section', PAIR)  4.51 us
    ppermute x2, starting transfers between devices, within_corner(): return lax.ppermute(x, DP, pairs)  3.18 us
    ppermute x4, starting transfers between devices, shifted(): return lax.ppermute(x, axis, [(i, (i + by) % n) for i in range(n)])  2.81 us
  transfers between devices with their start and end apart: 14, of which 5 were waited for; matrix products, arithmetic and copies ran while one was open for 0% of the time, Pallas kernels for 33%

profile of v3, /device:TPU:1, one launch (start us, length us, event | category | flops | bytes accessed | tf_op | source)
XLA Modules:
  0.0 73.0 jit_solution(10733689124751442640)
XLA Ops:
  0.6 1.2 %shard_map.104 = (bf16[1040,128]{1,0:T(8,128)(2,1)S(1)}, bf16[1024,128]{1,0:T(8,128)(2,1)S(1)}) custom-call(bf16[1536,512]{1,0:T(8,128)(2,1)} %bitcast.9, bf16[512,512]{1,0:T(8,128)(2,1)} %bitcast.11, bf16[1,512]{1,0:T(2,128)(2,1)} %gain_hbm.1), custom_call_target="tpu_custom_call" | custom-call | tf_op jit(solution)/shard_map/pallas_call | solution.py:420
  1.8 2.1 %collective-permute-start.3 = (bf16[1024,128]{1,0:T(8,128)(2,1)S(1)}, bf16[1024,128]{1,0:T(8,128)(2,1)S(1)}, u32[]{:S(2)}, u32[]{:S(2)}) collective-permute-start(bf16[1024,128]{1,0:T(8,128)(2,1)S(1)} %get-tuple-element.48), channel_id=1, source_target_pairs={{0,32},{32,0},{64,96},{96,64},{1,33},{33,1},{65,97},{97,65},{2,34}... | collective-permute-start | bytes 786440 | tf_op jit(solution)/shard_map/ppermute | solution.py:427
  3.9 0.1 collective-permute-start
  4.0 6.7 %shard_map.105 = (bf16[5,4,256,512]{3,2,1,0:T(8,128)(2,1)S(1)}, bf16[2,1536,512]{2,1,0:T(8,128)(2,1)S(1)}, bf16[2,512,512]{2,1,0:T(8,128)(2,1)S(1)}, f32[2,8,512...) custom-call(bf16[32,256,512]{2,1,0:T(8,128)(2,1)} %pool.1, ...), custom_call_target="tpu_custom_call" | custom-call | flops 4294967296 | tf_op jit(solution)/shard_map/pallas_call | solution.py:429
  10.7 4.5 %collective-permute-done.refs_0_ = bf16[1040,128]{1,0:T(8,128)(2,1)S(1)} collective-permute-done((bf16[1040,128]{1,0:T(8,128)(2,1)S(1)}, bf16[1040,128]{1,0:T(8,128)(2,1)S(1)}, u32[]{:S(2)}, u32[]{:S(2)}) %collective-permute-start) | collective-permute-done | bytes 266272 | tf_op jit(solution)/shard_map/ppermute | solution.py:426
  15.2 1.7 %collective-permute-start.4 = (bf16[1040,128]{1,0:T(8,128)(2,1)S(1)}, bf16[1040,128]{1,0:T(8,128)(2,1)S(1)}, u32[]{:S(2)}, u32[]{:S(2)}) collective-permute-start(bf16[1040,128]{1,0:T(8,128)(2,1)S(1)} %collective-permute-done.refs_0_), channel_id=1, source_target_pairs={{0,1},{1,0},{2,3},{3,2},{4,5},{5,4},{6,7},{7,6},{8,9},{9,8},{10,11... | collective-permute-start | bytes 798728 | tf_op jit(solution)/shard_map/ppermute | solution.py:382
  16.9 1.5 %collective-permute-start.2 = (bf16[1040,128]{1,0:T(8,128)(2,1)S(1)}, bf16[1040,128]{1,0:T(8,128)(2,1)S(1)}, u32[]{:S(2)}, u32[]{:S(2)}) collective-permute-start(bf16[1040,128]{1,0:T(8,128)(2,1)S(1)} %collective-permute-done.refs_0_), channel_id=1, source_target_pairs={{0,2},{1,9},{2,0},{3,11},{4,6},{5,13},{6,4},{7,15},{8,10},{9,1},{1... | collective-permute-start | bytes 798728 | tf_op jit(solution)/shard_map/ppermute | solution.py:393
  18.4 1.6 %collective-permute-start.1 = (bf16[1040,128]{1,0:T(8,128)(2,1)S(1)}, bf16[1040,128]{1,0:T(8,128)(2,1)S(1)}, u32[]{:S(2)}, u32[]{:S(2)}) collective-permute-start(bf16[1040,128]{1,0:T(8,128)(2,1)S(1)} %collective-permute-done.refs_0_), channel_id=1, source_target_pairs={{0,8},{1,3},{2,10},{3,1},{4,12},{5,7},{6,14},{7,5},{8,0},{9,11},{1... | collective-permute-start | bytes 798728 | tf_op jit(solution)/shard_map/ppermute | solution.py:393
  20.1 6.2 %shard_map.106.v = bf16[5,4,256,512]{3,2,1,0:T(8,128)(2,1)S(1)} custom-call(bf16[5,4,256,512]{3,2,1,0:T(8,128)(2,1)S(1)} %get-tuple-element.49.before, bf16[2,1536,512]{2,1,0:T(8,128)(2,1)S(1)} %get-tuple-element.50.all_taps.refs_8_, bf16[2,512,512]{2,1,0:T(8,128)(2,1)S(1)} %get-tuple-element.51.all_out.refs_9_, ...), custom_call_target="tpu_custom_call", output_to_operand_aliasing={{}: (0, {})} | custom-call | flops 6442450944 | tf_op jit(solution)/shard_map/pallas_call | solution.py:447
  26.3 0.0 collective-permute-done.3.refs_1_
  26.3 0.0 collective-permute-done.4.refs_4_
  26.3 0.0 collective-permute-done.2.refs_3_
  26.3 0.0 collective-permute-done.1.refs_2_
  26.3 0.6 collective-permute-start.7
  27.0 0.1 collective-permute-start.6
  27.1 0.4 collective-permute-start.5
  27.5 1.4 %collective-permute-done.5.refs_5_ = bf16[1024,128]{1,0:T(8,128)(2,1)S(1)} collective-permute-done((bf16[1024,128]{1,0:T(8,128)(2,1)S(1)}, bf16[1024,128]{1,0:T(8,128)(2,1)S(1)}, u32[]{:S(2)}, u32[]{:S(2)}) %collective-permute-start.5) | collective-permute-done | bytes 262176 | tf_op jit(solution)/shard_map/ppermute | solution.py:382
  28.9 0.0 collective-permute-done.7.refs_7_
  28.9 0.0 collective-permute-done.6.refs_6_
  28.9 0.6 shard_map.107
  29.5 2.7 %shard_map.108 = (bf16[1,24,1024]{2,1,0:T(8,128)(2,1)S(1)}, f32[24,128]{1,0:T(8,128)S(1)}) custom-call(bf16[5,4,256,512]{3,2,1,0:T(8,128)(2,1)S(1)} %shard_map.106.v, bf16[2,1536,512]{2,1,0:T(8,128)(2,1)S(1)} %get-tuple-element.58.all_taps, bf16[2,512,512]{2,1,0:T(8,128)(2,1)S(1)} %get-tuple-element.59.all_out, f32[2,8,512]{2,1,0:T(8,128)S(1)} %get-tuple-element.60.all_gain, ...), custom_call_target="tpu_custom_call" | custom-call | flops 4294967296 | tf_op jit(solution)/shard_map/pallas_call | solution.py:458
  32.3 0.1 collective-permute-start.8
  32.4 5.6 %shard_map.109 = (bf16[2,24,1024]{2,1,0:T(8,128)(2,1)S(1)}, f32[24,128]{1,0:T(8,128)S(1)}) custom-call(bf16[5,4,256,512]{3,2,1,0:T(8,128)(2,1)S(1)} %shard_map.106.v, bf16[2,1536,512]{2,1,0:T(8,128)(2,1)S(1)} %get-tuple-element.58.all_taps, bf16[2,512,512]{2,1,0:T(8,128)(2,1)S(1)} %get-tuple-element.59.all_out, f32[2,8,512]{2,1,0:T(8,128)S(1)} %get-tuple-element.60.all_gain, ...), custom_call_target="tpu_custom_call" | custom-call | flops 8589934592 | tf_op jit(solution)/shard_map/pallas_call | solution.py:458
  38.0 0.0 collective-permute-done.8.codes
  38.1 0.1 collective-permute-start.9
  38.2 5.5 %shard_map.111 = (bf16[2,24,1024]{2,1,0:T(8,128)(2,1)S(1)}, f32[8,128]{1,0:T(8,128)S(1)}) custom-call(bf16[5,4,256,512]{3,2,1,0:T(8,128)(2,1)S(1)} %shard_map.106.v, bf16[2,1536,512]{2,1,0:T(8,128)(2,1)S(1)} %get-tuple-element.58.all_taps, bf16[2,512,512]{2,1,0:T(8,128)(2,1)S(1)} %get-tuple-element.59.all_out, f32[2,8,512]{2,1,0:T(8,128)S(1)} %get-tuple-element.60.all_gain, ...), custom_call_target="tpu_custom_call" | custom-call | flops 8589934592 | tf_op jit(solution)/shard_map/pallas_call | solution.py:458
  43.7 1.3 %collective-permute-start.10 = (bf16[2,24,1024]{2,1,0:T(8,128)(2,1)S(1)}, bf16[2,24,1024]{2,1,0:T(8,128)(2,1)S(1)}, u32[]{:S(2)}, u32[]{:S(2)}) collective-permute-start(bf16[2,24,1024]{2,1,0:T(8,128)(2,1)S(1)} %get-tuple-element.71), channel_id=1, source_target_pairs={{0,96},{32,64},{1,97},{33,65},{2,98},{34,66},{3,99},{35,67},{4,100... | collective-permute-start | bytes 294920 | tf_op jit(solution)/shard_map/ppermute | solution.py:483
  45.0 0.0 collective-permute-done.9.codes
  45.0 0.0 copy-start
  45.1 2.0 %collective-permute-done.10.codes = bf16[2,24,1024]{2,1,0:T(8,128)(2,1)S(1)} collective-permute-done((bf16[2,24,1024]{2,1,0:T(8,128)(2,1)S(1)}, bf16[2,24,1024]{2,1,0:T(8,128)(2,1)S(1)}, u32[]{:S(2)}, u32[]{:S(2)}) %collective-permute-start.10) | collective-permute-done | bytes 98336 | tf_op jit(solution)/shard_map/ppermute | solution.py:483
  47.1 15.8 %conditional.1 = (f32[8,128]{1,0:T(8,128)S(1)}) conditional(s32[]{:T(128)} %convert_element_type.7, f32[8,128]{1,0:T(8,128)S(1)} %get-tuple-element.77, f32[8,128]{1,0:T(8,128)S(1)} %get-tuple-element.77), branch_computations={%region_0.0_spmd, %region_1.0_spmd} | conditional | flops 31744 | bytes 532492 | solution.py:489
  47.1 15.8 %all_to_all.4 = f32[32,8,128]{2,1,0:T(8,128)S(1)} all-to-all(f32[32,8,128]{2,1,0:T(8,128)S(1)} %broadcast_in_dim.0), channel_id=1, replica_groups=mesh['section'=4,'dp_0'=4,'dp_1'=4,'dp_2'=2] {'dp_0','dp_1','dp_2'}, dimensions={0} | all-to-all | bytes 262144 | tf_op jit(solution)/shard_map/cond/branch_1_fun/all_to_all | solution.py:398
  62.9 0.1 collective-permute-start.13
  63.0 6.2 %collective-permute-start.12 = (f32[24,128]{1,0:T(8,128)S(1)}, f32[24,128]{1,0:T(8,128)S(1)}, u32[]{:S(2)}, u32[]{:S(2)}) collective-permute-start(f32[24,128]{1,0:T(8,128)S(1)} %pad_maximum_fusion.mine), channel_id=1, source_target_pairs={{0,96},{96,0},{32,64},{64,32},{1,97},{97,1},{33,65},{65,33},{2,98}... | collective-permute-start | bytes 36872 | tf_op jit(solution)/shard_map/ppermute | solution.py:491
  69.2 0.0 collective-permute-start.11
  69.2 0.0 collective-permute-done.13.far
  69.2 1.1 %collective-permute-done.12.cross = f32[24,128]{1,0:T(8,128)S(1)} collective-permute-done((f32[24,128]{1,0:T(8,128)S(1)}, f32[24,128]{1,0:T(8,128)S(1)}, u32[]{:S(2)}, u32[]{:S(2)}) %collective-permute-start.12) | collective-permute-done | bytes 12320 | tf_op jit(solution)/shard_map/ppermute | solution.py:491
  70.3 1.5 %collective-permute-done.11.next_ = f32[24,128]{1,0:T(8,128)S(1)} collective-permute-done((f32[24,128]{1,0:T(8,128)S(1)}, f32[24,128]{1,0:T(8,128)S(1)}, u32[]{:S(2)}, u32[]{:S(2)}) %collective-permute-start.11) | collective-permute-done | bytes 12320 | tf_op jit(solution)/shard_map/ppermute | solution.py:491
  71.7 0.0 copy-done
  71.7 1.3 %shard_map.114 = (f32[2,4,256]{2,1,0:T(4,128)}, f32[8]{0:T(128)}) custom-call(s32[8]{0:T(128)S(1)} %copy-done, f32[24,128]{1,0:T(8,128)S(1)} %pad_maximum_fusion.mine, f32[24,128]{1,0:T(8,128)S(1)} %collective-permute-done.11.next_, f32[24,128]{1,0:T(8,128)S(1)} %collective-permute-done.12.cross, f32[24,128]{1,0:T(8,128)S(1)} %collective-permute-done.13.far, ...), custom_call_target="tpu_custom_call" | custom-call | tf_op jit(solution)/shard_map/pallas_call | solution.py:493
  (7 shorter events, 0.1 us)
Async XLA Ops:
  1.8 24.5 %collective-permute-start.3 = (bf16[1024,128]{1,0:T(8,128)(2,1)S(1)}, bf16[1024,128]{1,0:T(8,128)(2,1)S(1)}, u32[]{:S(2)}, u32[]{:S(2)}) collective-permute-start(bf16[1024,128]{1,0:T(8,128)(2,1)S(1)} %get-tuple-element.48), channel_id=1, source_target_pairs={{0,32},{32,0},{64,96},{96,64},{1,33},{33,1},{65,97},{97,65},{2,34}... | collective-permute-start | bytes 786440 | tf_op jit(solution)/shard_map/ppermute | solution.py:427
  3.9 11.3 %collective-permute-start = (bf16[1040,128]{1,0:T(8,128)(2,1)S(1)}, bf16[1040,128]{1,0:T(8,128)(2,1)S(1)}, u32[]{:S(2)}, u32[]{:S(2)}) collective-permute-start(bf16[1040,128]{1,0:T(8,128)(2,1)S(1)} %get-tuple-element.45), channel_id=1, source_target_pairs={{0,32},{32,0},{64,96},{96,64},{1,33},{33,1},{65,97},{97,65},{2,34}... | collective-permute-start | bytes 798728 | tf_op jit(solution)/shard_map/ppermute | solution.py:426
  15.2 11.0 %collective-permute-start.4 = (bf16[1040,128]{1,0:T(8,128)(2,1)S(1)}, bf16[1040,128]{1,0:T(8,128)(2,1)S(1)}, u32[]{:S(2)}, u32[]{:S(2)}) collective-permute-start(bf16[1040,128]{1,0:T(8,128)(2,1)S(1)} %collective-permute-done.refs_0_), channel_id=1, source_target_pairs={{0,1},{1,0},{2,3},{3,2},{4,5},{5,4},{6,7},{7,6},{8,9},{9,8},{10,11... | collective-permute-start | bytes 798728 | tf_op jit(solution)/shard_map/ppermute | solution.py:382
  16.9 9.4 %collective-permute-start.2 = (bf16[1040,128]{1,0:T(8,128)(2,1)S(1)}, bf16[1040,128]{1,0:T(8,128)(2,1)S(1)}, u32[]{:S(2)}, u32[]{:S(2)}) collective-permute-start(bf16[1040,128]{1,0:T(8,128)(2,1)S(1)} %collective-permute-done.refs_0_), channel_id=1, source_target_pairs={{0,2},{1,9},{2,0},{3,11},{4,6},{5,13},{6,4},{7,15},{8,10},{9,1},{1... | collective-permute-start | bytes 798728 | tf_op jit(solution)/shard_map/ppermute | solution.py:393
  18.4 7.9 %collective-permute-start.1 = (bf16[1040,128]{1,0:T(8,128)(2,1)S(1)}, bf16[1040,128]{1,0:T(8,128)(2,1)S(1)}, u32[]{:S(2)}, u32[]{:S(2)}) collective-permute-start(bf16[1040,128]{1,0:T(8,128)(2,1)S(1)} %collective-permute-done.refs_0_), channel_id=1, source_target_pairs={{0,8},{1,3},{2,10},{3,1},{4,12},{5,7},{6,14},{7,5},{8,0},{9,11},{1... | collective-permute-start | bytes 798728 | tf_op jit(solution)/shard_map/ppermute | solution.py:393
  26.3 2.6 %collective-permute-start.7 = (bf16[1040,128]{1,0:T(8,128)(2,1)S(1)}, bf16[1040,128]{1,0:T(8,128)(2,1)S(1)}, u32[]{:S(2)}, u32[]{:S(2)}) collective-permute-start(bf16[1040,128]{1,0:T(8,128)(2,1)S(1)} %collective-permute-done.1.refs_2_), channel_id=1, source_target_pairs={{0,1},{1,0},{2,3},{3,2},{4,5},{5,4},{6,7},{7,6},{8,9},{9,8},{10,11... | collective-permute-start | bytes 798728 | tf_op jit(solution)/shard_map/ppermute | solution.py:382
  27.0 1.9 %collective-permute-start.6 = (bf16[1040,128]{1,0:T(8,128)(2,1)S(1)}, bf16[1040,128]{1,0:T(8,128)(2,1)S(1)}, u32[]{:S(2)}, u32[]{:S(2)}) collective-permute-start(bf16[1040,128]{1,0:T(8,128)(2,1)S(1)} %collective-permute-done.2.refs_3_), channel_id=1, source_target_pairs={{0,1},{1,0},{2,3},{3,2},{4,5},{5,4},{6,7},{7,6},{8,9},{9,8},{10,11... | collective-permute-start | bytes 798728 | tf_op jit(solution)/shard_map/ppermute | solution.py:382
  27.1 1.8 %collective-permute-start.5 = (bf16[1024,128]{1,0:T(8,128)(2,1)S(1)}, bf16[1024,128]{1,0:T(8,128)(2,1)S(1)}, u32[]{:S(2)}, u32[]{:S(2)}) collective-permute-start(bf16[1024,128]{1,0:T(8,128)(2,1)S(1)} %collective-permute-done.3.refs_1_), channel_id=1, source_target_pairs={{0,1},{1,0},{2,3},{3,2},{4,5},{5,4},{6,7},{7,6},{8,9},{9,8},{10,11... | collective-permute-start | bytes 786440 | tf_op jit(solution)/shard_map/ppermute | solution.py:382
  32.3 5.7 %collective-permute-start.8 = (bf16[1,24,1024]{2,1,0:T(8,128)(2,1)S(1)}, bf16[1,24,1024]{2,1,0:T(8,128)(2,1)S(1)}, u32[]{:S(2)}, u32[]{:S(2)}) collective-permute-start(bf16[1,24,1024]{2,1,0:T(8,128)(2,1)S(1)} %get-tuple-element.66), channel_id=1, source_target_pairs={{0,64},{64,0},{32,96},{96,32},{1,65},{65,1},{33,97},{97,33},{2,66}... | collective-permute-start | bytes 147464 | tf_op jit(solution)/shard_map/ppermute | solution.py:477
  38.1 6.9 %collective-permute-start.9 = (bf16[2,24,1024]{2,1,0:T(8,128)(2,1)S(1)}, bf16[2,24,1024]{2,1,0:T(8,128)(2,1)S(1)}, u32[]{:S(2)}, u32[]{:S(2)}) collective-permute-start(bf16[2,24,1024]{2,1,0:T(8,128)(2,1)S(1)} %get-tuple-element.67), channel_id=1, source_target_pairs={{0,96},{96,0},{32,64},{64,32},{1,97},{97,1},{33,65},{65,33},{2,98}... | collective-permute-start | bytes 294920 | tf_op jit(solution)/shard_map/ppermute | solution.py:481
  43.7 3.3 %collective-permute-start.10 = (bf16[2,24,1024]{2,1,0:T(8,128)(2,1)S(1)}, bf16[2,24,1024]{2,1,0:T(8,128)(2,1)S(1)}, u32[]{:S(2)}, u32[]{:S(2)}) collective-permute-start(bf16[2,24,1024]{2,1,0:T(8,128)(2,1)S(1)} %get-tuple-element.71), channel_id=1, source_target_pairs={{0,96},{32,64},{1,97},{33,65},{2,98},{34,66},{3,99},{35,67},{4,100... | collective-permute-start | bytes 294920 | tf_op jit(solution)/shard_map/ppermute | solution.py:483
  45.0 26.7 %copy-start = (s32[8]{0:T(128)S(1)}, s32[8]{0:T(128)}, u32[]{:S(2)}) copy-start(s32[8]{0:T(128)} %order.1) | copy-start | bytes 100
  62.9 6.3 %collective-permute-start.13 = (f32[24,128]{1,0:T(8,128)S(1)}, f32[24,128]{1,0:T(8,128)S(1)}, u32[]{:S(2)}, u32[]{:S(2)}) collective-permute-start(f32[24,128]{1,0:T(8,128)S(1)} %pad_maximum_fusion.mine), channel_id=1, source_target_pairs={{0,64},{64,0},{32,96},{96,32},{1,65},{65,1},{33,97},{97,33},{2,66}... | collective-permute-start | bytes 36872 | tf_op jit(solution)/shard_map/ppermute | solution.py:491
  63.0 7.3 %collective-permute-start.12 = (f32[24,128]{1,0:T(8,128)S(1)}, f32[24,128]{1,0:T(8,128)S(1)}, u32[]{:S(2)}, u32[]{:S(2)}) collective-permute-start(f32[24,128]{1,0:T(8,128)S(1)} %pad_maximum_fusion.mine), channel_id=1, source_target_pairs={{0,96},{96,0},{32,64},{64,32},{1,97},{97,1},{33,65},{65,33},{2,98}... | collective-permute-start | bytes 36872 | tf_op jit(solution)/shard_map/ppermute | solution.py:491
  69.2 2.5 %collective-permute-start.11 = (f32[24,128]{1,0:T(8,128)S(1)}, f32[24,128]{1,0:T(8,128)S(1)}, u32[]{:S(2)}, u32[]{:S(2)}) collective-permute-start(f32[24,128]{1,0:T(8,128)S(1)} %pad_maximum_fusion.mine), channel_id=1, source_target_pairs={{0,32},{32,0},{64,96},{96,64},{1,33},{33,1},{65,97},{97,65},{2,34}... | collective-permute-start | bytes 36872 | tf_op jit(solution)/shard_map/ppermute | solution.py:491

commit v4 on v3

--- a/solution.py
+++ b/solution.py
@@ -336,10 +336,9 @@
         target[c : c + 1, :] = jnp.concatenate([row[0:1], row[1:2]], axis=1)
 
 
-def final_body(rows_total, order, mine, next_, cross, far, e0, e34, error, loss):
+def final_body(rows_total, order, mine, cross, e0, e34, error, loss):
     section = lax.axis_index("section")
-    a, b, c, d = mine[0:8], next_[0:8], cross[0:8], far[0:8]
-    sums = (jnp.where(section <= 1, a + b, c + d)) * (1.0 / rows_total)
+    sums = jnp.where(section <= 1, mine[0:8], cross[0:8]) * (1.0 / rows_total)
     row = lax.broadcasted_iota(jnp.int32, sums.shape, 0)
     lane = lax.broadcasted_iota(jnp.int32, sums.shape, 1)
     averaged = jnp.zeros_like(sums)
@@ -393,8 +392,9 @@
     return lax.ppermute(x, DP, pairs)
 
 
-def plane_sum(x):
+def encoder_sum(x):
     n = lax.axis_size(DP)
+    x = x + lax.ppermute(x, "section", PAIR)
     return jnp.sum(lax.all_to_all(jnp.broadcast_to(x[None], (n, *x.shape)), DP, 0, 0), axis=0)
 
 
@@ -486,15 +486,15 @@
     codes_c, e12 = lax.optimization_barrier((codes_c, e12))
     e34 = decode((3, 4), codes_c)
     stats, e12, e34, encoder = lax.optimization_barrier((stats, e12, e34, encoder))
-    total = lax.cond(encoder == 1, plane_sum, lambda x: 0.0 * x, stats)
+    total = lax.cond(encoder == 1, encoder_sum, lambda x: 0.0 * x, stats)
     packed = jnp.concatenate([total, e12[0], e12[1]], axis=0)
-    near, cross, far = (lax.ppermute(packed, "section", pairs) for pairs in (PAIR, CROSS, FAR))
+    cross = lax.ppermute(packed, "section", CROSS)
     rows_total = float(CLIPS * lax.axis_size(DP) * ROWS)
     error, loss = call(
         functools.partial(final_body, rows_total),
-        [SM] + [VM] * 6,
+        [SM] + [VM] * 4,
         [((2, CLIPS, ROWS), f32), ((8,), f32)],
-    )(order, packed, near, cross, far, e0, e34)
+    )(order, packed, cross, e0, e34)
     return error, loss
 
 

time: 73.9 us -> 74.1 us (level)
  starting transfers between devices: 16 us -> 12.3 us
  blocking collectives: 15.8 us -> 18 us
  waiting for transfers between devices: 10.5 us -> 12.7 us
    ppermute x3 -> x2, starting transfers between devices: 6.3 us -> 2.6 us  [the longest x1 2.51 us: encoder_sum(): x = x + lax.ppermute(x, 'section', PAIR)]
    ppermute x3 -> x2, waiting for transfers between devices: 2.54 us -> 4.74 us  [the longest x1 3.74 us: on_device(): cross = lax.ppermute(packed, 'section', CROSS)]
    all_to_all x1, blocking collectives: 15.8 us -> 18 us  [encoder_sum(): lax.all_to_all(jnp.broadcast_to(x[None], (n, *x.shape)), DP, 0, 0)]
  transfers between devices with their start and end apart: 14 -> 13, of which waited for: 5 -> 5; matrix products, arithmetic and copies ran while one was open for 0% -> 0% of each run, Pallas kernels for 33% -> 33%
where the time goes in v4:
time: 74.1 us; the launch traced here: 73.7 us
  Pallas kernels  30 us (40%)
  blocking collectives  18 us (24%)
  waiting for transfers between devices  12.7 us (17%)
  starting transfers between devices  12.3 us (17%)
  between operations  0.79 us (1%)
    all_to_all x1, blocking collectives, encoder_sum(): lax.all_to_all(jnp.broadcast_to(x[None], (n, *x.shape)), DP, 0, 0)  18 us
    pallas_call x3, Pallas kernels, encode(): call(functools.partial(encode_body, steps, last), [VM] * (6 + len(before)...  13.9 us
    pallas_call x1, Pallas kernels, on_device(): call(functools.partial(start_body, 2), [HB] * 8, [v_kind, *kinds, ((C, 12...  6.71 us
    pallas_call x1, Pallas kernels, on_device(): call(functools.partial(more_body, 2, STEPS), [VM] * 4, [v_kind], blocks=3...  6.19 us
    ppermute x1, waiting for transfers between devices, on_device(): mine = lax.ppermute(piece, 'section', PAIR)  4.51 us
    ppermute x1, waiting for transfers between devices, on_device(): cross = lax.ppermute(packed, 'section', CROSS)  3.74 us
    ppermute x2, starting transfers between devices, within_corner(): return lax.ppermute(x, DP, pairs)  3.18 us
    ppermute x4, starting transfers between devices, shifted(): return lax.ppermute(x, axis, [(i, (i + by) % n) for i in range(n)])  2.81 us
  transfers between devices with their start and end apart: 13, of which 5 were waited for; matrix products, arithmetic and copies ran while one was open for 0% of the time, Pallas kernels for 33%

profile of v4, /device:TPU:1, one launch (start us, length us, event | category | flops | bytes accessed | tf_op | source)
XLA Modules:
  0.0 73.7 jit_solution(13074202795922320466)
XLA Ops:
  0.6 1.2 %shard_map.104 = (bf16[1040,128]{1,0:T(8,128)(2,1)S(1)}, bf16[1024,128]{1,0:T(8,128)(2,1)S(1)}) custom-call(bf16[1536,512]{1,0:T(8,128)(2,1)} %bitcast.9, bf16[512,512]{1,0:T(8,128)(2,1)} %bitcast.11, bf16[1,512]{1,0:T(2,128)(2,1)} %gain_hbm.1), custom_call_target="tpu_custom_call" | custom-call | tf_op jit(solution)/shard_map/pallas_call | solution.py:420
  1.8 2.1 %collective-permute-start.4 = (bf16[1024,128]{1,0:T(8,128)(2,1)S(1)}, bf16[1024,128]{1,0:T(8,128)(2,1)S(1)}, u32[]{:S(2)}, u32[]{:S(2)}) collective-permute-start(bf16[1024,128]{1,0:T(8,128)(2,1)S(1)} %get-tuple-element.48), channel_id=1, source_target_pairs={{0,32},{32,0},{64,96},{96,64},{1,33},{33,1},{65,97},{97,65},{2,34}... | collective-permute-start | bytes 786440 | tf_op jit(solution)/shard_map/ppermute | solution.py:427
  3.9 0.1 collective-permute-start.1
  4.0 6.7 %shard_map.105 = (bf16[5,4,256,512]{3,2,1,0:T(8,128)(2,1)S(1)}, bf16[2,1536,512]{2,1,0:T(8,128)(2,1)S(1)}, bf16[2,512,512]{2,1,0:T(8,128)(2,1)S(1)}, f32[2,8,512...) custom-call(bf16[32,256,512]{2,1,0:T(8,128)(2,1)} %pool.1, ...), custom_call_target="tpu_custom_call" | custom-call | flops 4294967296 | tf_op jit(solution)/shard_map/pallas_call | solution.py:429
  10.7 4.5 %collective-permute-done.1.refs_0_ = bf16[1040,128]{1,0:T(8,128)(2,1)S(1)} collective-permute-done((bf16[1040,128]{1,0:T(8,128)(2,1)S(1)}, bf16[1040,128]{1,0:T(8,128)(2,1)S(1)}, u32[]{:S(2)}, u32[]{:S(2)}) %collective-permute-start.1) | collective-permute-done | bytes 266272 | tf_op jit(solution)/shard_map/ppermute | solution.py:426
  15.2 1.7 %collective-permute-start.5 = (bf16[1040,128]{1,0:T(8,128)(2,1)S(1)}, bf16[1040,128]{1,0:T(8,128)(2,1)S(1)}, u32[]{:S(2)}, u32[]{:S(2)}) collective-permute-start(bf16[1040,128]{1,0:T(8,128)(2,1)S(1)} %collective-permute-done.1.refs_0_), channel_id=1, source_target_pairs={{0,1},{1,0},{2,3},{3,2},{4,5},{5,4},{6,7},{7,6},{8,9},{9,8},{10,11... | collective-permute-start | bytes 798728 | tf_op jit(solution)/shard_map/ppermute | solution.py:381
  16.9 1.5 %collective-permute-start.3 = (bf16[1040,128]{1,0:T(8,128)(2,1)S(1)}, bf16[1040,128]{1,0:T(8,128)(2,1)S(1)}, u32[]{:S(2)}, u32[]{:S(2)}) collective-permute-start(bf16[1040,128]{1,0:T(8,128)(2,1)S(1)} %collective-permute-done.1.refs_0_), channel_id=1, source_target_pairs={{0,2},{1,9},{2,0},{3,11},{4,6},{5,13},{6,4},{7,15},{8,10},{9,1},{1... | collective-permute-start | bytes 798728 | tf_op jit(solution)/shard_map/ppermute | solution.py:392
  18.4 1.6 %collective-permute-start.2 = (bf16[1040,128]{1,0:T(8,128)(2,1)S(1)}, bf16[1040,128]{1,0:T(8,128)(2,1)S(1)}, u32[]{:S(2)}, u32[]{:S(2)}) collective-permute-start(bf16[1040,128]{1,0:T(8,128)(2,1)S(1)} %collective-permute-done.1.refs_0_), channel_id=1, source_target_pairs={{0,8},{1,3},{2,10},{3,1},{4,12},{5,7},{6,14},{7,5},{8,0},{9,11},{1... | collective-permute-start | bytes 798728 | tf_op jit(solution)/shard_map/ppermute | solution.py:392
  20.1 6.2 %shard_map.106.v = bf16[5,4,256,512]{3,2,1,0:T(8,128)(2,1)S(1)} custom-call(bf16[5,4,256,512]{3,2,1,0:T(8,128)(2,1)S(1)} %get-tuple-element.49.before, bf16[2,1536,512]{2,1,0:T(8,128)(2,1)S(1)} %get-tuple-element.50.all_taps.refs_8_, bf16[2,512,512]{2,1,0:T(8,128)(2,1)S(1)} %get-tuple-element.51.all_out.refs_9_, ...), custom_call_target="tpu_custom_call", output_to_operand_aliasing={{}: (0, {})} | custom-call | flops 6442450944 | tf_op jit(solution)/shard_map/pallas_call | solution.py:447
  26.3 0.0 collective-permute-done.4.refs_1_
  26.3 0.0 collective-permute-done.5.refs_4_
  26.3 0.0 collective-permute-done.3.refs_3_
  26.3 0.0 collective-permute-done.2.refs_2_
  26.3 0.6 collective-permute-start.8
  27.0 0.1 collective-permute-start.7
  27.1 0.4 collective-permute-start.6
  27.5 1.4 %collective-permute-done.6.refs_5_ = bf16[1024,128]{1,0:T(8,128)(2,1)S(1)} collective-permute-done((bf16[1024,128]{1,0:T(8,128)(2,1)S(1)}, bf16[1024,128]{1,0:T(8,128)(2,1)S(1)}, u32[]{:S(2)}, u32[]{:S(2)}) %collective-permute-start.6) | collective-permute-done | bytes 262176 | tf_op jit(solution)/shard_map/ppermute | solution.py:381
  28.9 0.0 collective-permute-done.8.refs_7_
  28.9 0.0 collective-permute-done.7.refs_6_
  28.9 0.6 shard_map.107
  29.5 2.7 %shard_map.108 = (bf16[1,24,1024]{2,1,0:T(8,128)(2,1)S(1)}, f32[24,128]{1,0:T(8,128)S(1)}) custom-call(bf16[5,4,256,512]{3,2,1,0:T(8,128)(2,1)S(1)} %shard_map.106.v, bf16[2,1536,512]{2,1,0:T(8,128)(2,1)S(1)} %get-tuple-element.58.all_taps, bf16[2,512,512]{2,1,0:T(8,128)(2,1)S(1)} %get-tuple-element.59.all_out, f32[2,8,512]{2,1,0:T(8,128)S(1)} %get-tuple-element.60.all_gain, ...), custom_call_target="tpu_custom_call" | custom-call | flops 4294967296 | tf_op jit(solution)/shard_map/pallas_call | solution.py:458
  32.3 0.1 collective-permute-start.9
  32.4 5.6 %shard_map.109 = (bf16[2,24,1024]{2,1,0:T(8,128)(2,1)S(1)}, f32[24,128]{1,0:T(8,128)S(1)}) custom-call(bf16[5,4,256,512]{3,2,1,0:T(8,128)(2,1)S(1)} %shard_map.106.v, bf16[2,1536,512]{2,1,0:T(8,128)(2,1)S(1)} %get-tuple-element.58.all_taps, bf16[2,512,512]{2,1,0:T(8,128)(2,1)S(1)} %get-tuple-element.59.all_out, f32[2,8,512]{2,1,0:T(8,128)S(1)} %get-tuple-element.60.all_gain, ...), custom_call_target="tpu_custom_call" | custom-call | flops 8589934592 | tf_op jit(solution)/shard_map/pallas_call | solution.py:458
  38.0 0.0 collective-permute-done.9.codes
  38.1 0.1 collective-permute-start.10
  38.2 5.5 %shard_map.111 = (bf16[2,24,1024]{2,1,0:T(8,128)(2,1)S(1)}, f32[8,128]{1,0:T(8,128)S(1)}) custom-call(bf16[5,4,256,512]{3,2,1,0:T(8,128)(2,1)S(1)} %shard_map.106.v, bf16[2,1536,512]{2,1,0:T(8,128)(2,1)S(1)} %get-tuple-element.58.all_taps, bf16[2,512,512]{2,1,0:T(8,128)(2,1)S(1)} %get-tuple-element.59.all_out, f32[2,8,512]{2,1,0:T(8,128)S(1)} %get-tuple-element.60.all_gain, ...), custom_call_target="tpu_custom_call" | custom-call | flops 8589934592 | tf_op jit(solution)/shard_map/pallas_call | solution.py:458
  43.7 1.3 %collective-permute-start.11 = (bf16[2,24,1024]{2,1,0:T(8,128)(2,1)S(1)}, bf16[2,24,1024]{2,1,0:T(8,128)(2,1)S(1)}, u32[]{:S(2)}, u32[]{:S(2)}) collective-permute-start(bf16[2,24,1024]{2,1,0:T(8,128)(2,1)S(1)} %get-tuple-element.71), channel_id=1, source_target_pairs={{0,96},{32,64},{1,97},{33,65},{2,98},{34,66},{3,99},{35,67},{4,100... | collective-permute-start | bytes 294920 | tf_op jit(solution)/shard_map/ppermute | solution.py:483
  45.0 0.0 collective-permute-done.10.codes
  45.0 0.0 copy-start
  45.1 2.0 %collective-permute-done.11.codes = bf16[2,24,1024]{2,1,0:T(8,128)(2,1)S(1)} collective-permute-done((bf16[2,24,1024]{2,1,0:T(8,128)(2,1)S(1)}, bf16[2,24,1024]{2,1,0:T(8,128)(2,1)S(1)}, u32[]{:S(2)}, u32[]{:S(2)}) %collective-permute-start.11) | collective-permute-done | bytes 98336 | tf_op jit(solution)/shard_map/ppermute | solution.py:483
  47.1 21.5 %conditional.1 = (f32[8,128]{1,0:T(8,128)S(1)}) conditional(s32[]{:T(128)} %convert_element_type.7, f32[8,128]{1,0:T(8,128)S(1)} %get-tuple-element.77, f32[8,128]{1,0:T(8,128)S(1)} %get-tuple-element.77), branch_computations={%region_0.0_spmd, %region_1.0_spmd} | conditional | flops 32768 | bytes 561204 | solution.py:489
  47.1 2.5 %collective-permute-start = (f32[8,128]{1,0:T(8,128)S(1)}, f32[8,128]{1,0:T(8,128)S(1)}, u32[]{:S(2)}, u32[]{:S(2)}) collective-permute-start(f32[8,128]{1,0:T(8,128)S(1)} %param.1), channel_id=1, source_target_pairs={{0,32},{32,0},{64,96},{96,64},{1,33},{33,1},{65,97},{97,65},{2,34}... | collective-permute-start | bytes 12296 | tf_op jit(solution)/shard_map/cond/branch_1_fun/ppermute | solution.py:397
  49.6 1.0 %collective-permute-done = f32[8,128]{1,0:T(8,128)S(1)} collective-permute-done((f32[8,128]{1,0:T(8,128)S(1)}, f32[8,128]{1,0:T(8,128)S(1)}, u32[]{:S(2)}, u32[]{:S(2)}) %collective-permute-start) | collective-permute-done | bytes 4128 | tf_op jit(solution)/shard_map/cond/branch_1_fun/ppermute | solution.py:397
  50.6 18.0 %all_to_all.4 = f32[32,8,128]{2,1,0:T(8,128)S(1)} all-to-all(f32[32,8,128]{2,1,0:T(8,128)S(1)} %broadcast_in_dim.0), channel_id=1, replica_groups=mesh['section'=4,'dp_0'=4,'dp_1'=4,'dp_2'=2] {'dp_0','dp_1','dp_2'}, dimensions={0} | all-to-all | bytes 262144 | tf_op jit(solution)/shard_map/cond/branch_1_fun/all_to_all | solution.py:398
  68.6 0.1 collective-permute-start.12
  68.7 3.7 %collective-permute-done.12.cross = f32[24,128]{1,0:T(8,128)S(1)} collective-permute-done((f32[24,128]{1,0:T(8,128)S(1)}, f32[24,128]{1,0:T(8,128)S(1)}, u32[]{:S(2)}, u32[]{:S(2)}) %collective-permute-start.12) | collective-permute-done | bytes 12320 | tf_op jit(solution)/shard_map/ppermute | solution.py:491
  72.4 0.0 copy-done
  72.4 1.3 %shard_map.114 = (f32[2,4,256]{2,1,0:T(4,128)}, f32[8]{0:T(128)}) custom-call(s32[8]{0:T(128)S(1)} %copy-done, f32[24,128]{1,0:T(8,128)S(1)} %pad_maximum_fusion.mine, f32[24,128]{1,0:T(8,128)S(1)} %collective-permute-done.12.cross, f32[1,8,128]{2,1,0:T(8,128)S(1)} %shard_map.110.e0, f32[2,8,128]{2,1,0:T(8,128)S(1)} %shard_map.113.e34), custom_call_target="tpu_custom_call" | custom-call | tf_op jit(solution)/shard_map/pallas_call | solution.py:493
  (8 shorter events, 0.1 us)
Async XLA Ops:
  1.8 24.5 %collective-permute-start.4 = (bf16[1024,128]{1,0:T(8,128)(2,1)S(1)}, bf16[1024,128]{1,0:T(8,128)(2,1)S(1)}, u32[]{:S(2)}, u32[]{:S(2)}) collective-permute-start(bf16[1024,128]{1,0:T(8,128)(2,1)S(1)} %get-tuple-element.48), channel_id=1, source_target_pairs={{0,32},{32,0},{64,96},{96,64},{1,33},{33,1},{65,97},{97,65},{2,34}... | collective-permute-start | bytes 786440 | tf_op jit(solution)/shard_map/ppermute | solution.py:427
  3.9 11.3 %collective-permute-start.1 = (bf16[1040,128]{1,0:T(8,128)(2,1)S(1)}, bf16[1040,128]{1,0:T(8,128)(2,1)S(1)}, u32[]{:S(2)}, u32[]{:S(2)}) collective-permute-start(bf16[1040,128]{1,0:T(8,128)(2,1)S(1)} %get-tuple-element.45), channel_id=1, source_target_pairs={{0,32},{32,0},{64,96},{96,64},{1,33},{33,1},{65,97},{97,65},{2,34}... | collective-permute-start | bytes 798728 | tf_op jit(solution)/shard_map/ppermute | solution.py:426
  15.2 11.0 %collective-permute-start.5 = (bf16[1040,128]{1,0:T(8,128)(2,1)S(1)}, bf16[1040,128]{1,0:T(8,128)(2,1)S(1)}, u32[]{:S(2)}, u32[]{:S(2)}) collective-permute-start(bf16[1040,128]{1,0:T(8,128)(2,1)S(1)} %collective-permute-done.1.refs_0_), channel_id=1, source_target_pairs={{0,1},{1,0},{2,3},{3,2},{4,5},{5,4},{6,7},{7,6},{8,9},{9,8},{10,11... | collective-permute-start | bytes 798728 | tf_op jit(solution)/shard_map/ppermute | solution.py:381
  16.9 9.4 %collective-permute-start.3 = (bf16[1040,128]{1,0:T(8,128)(2,1)S(1)}, bf16[1040,128]{1,0:T(8,128)(2,1)S(1)}, u32[]{:S(2)}, u32[]{:S(2)}) collective-permute-start(bf16[1040,128]{1,0:T(8,128)(2,1)S(1)} %collective-permute-done.1.refs_0_), channel_id=1, source_target_pairs={{0,2},{1,9},{2,0},{3,11},{4,6},{5,13},{6,4},{7,15},{8,10},{9,1},{1... | collective-permute-start | bytes 798728 | tf_op jit(solution)/shard_map/ppermute | solution.py:392
  18.4 7.9 %collective-permute-start.2 = (bf16[1040,128]{1,0:T(8,128)(2,1)S(1)}, bf16[1040,128]{1,0:T(8,128)(2,1)S(1)}, u32[]{:S(2)}, u32[]{:S(2)}) collective-permute-start(bf16[1040,128]{1,0:T(8,128)(2,1)S(1)} %collective-permute-done.1.refs_0_), channel_id=1, source_target_pairs={{0,8},{1,3},{2,10},{3,1},{4,12},{5,7},{6,14},{7,5},{8,0},{9,11},{1... | collective-permute-start | bytes 798728 | tf_op jit(solution)/shard_map/ppermute | solution.py:392
  26.3 2.6 %collective-permute-start.8 = (bf16[1040,128]{1,0:T(8,128)(2,1)S(1)}, bf16[1040,128]{1,0:T(8,128)(2,1)S(1)}, u32[]{:S(2)}, u32[]{:S(2)}) collective-permute-start(bf16[1040,128]{1,0:T(8,128)(2,1)S(1)} %collective-permute-done.2.refs_2_), channel_id=1, source_target_pairs={{0,1},{1,0},{2,3},{3,2},{4,5},{5,4},{6,7},{7,6},{8,9},{9,8},{10,11... | collective-permute-start | bytes 798728 | tf_op jit(solution)/shard_map/ppermute | solution.py:381
  27.0 1.9 %collective-permute-start.7 = (bf16[1040,128]{1,0:T(8,128)(2,1)S(1)}, bf16[1040,128]{1,0:T(8,128)(2,1)S(1)}, u32[]{:S(2)}, u32[]{:S(2)}) collective-permute-start(bf16[1040,128]{1,0:T(8,128)(2,1)S(1)} %collective-permute-done.3.refs_3_), channel_id=1, source_target_pairs={{0,1},{1,0},{2,3},{3,2},{4,5},{5,4},{6,7},{7,6},{8,9},{9,8},{10,11... | collective-permute-start | bytes 798728 | tf_op jit(solution)/shard_map/ppermute | solution.py:381
  27.1 1.8 %collective-permute-start.6 = (bf16[1024,128]{1,0:T(8,128)(2,1)S(1)}, bf16[1024,128]{1,0:T(8,128)(2,1)S(1)}, u32[]{:S(2)}, u32[]{:S(2)}) collective-permute-start(bf16[1024,128]{1,0:T(8,128)(2,1)S(1)} %collective-permute-done.4.refs_1_), channel_id=1, source_target_pairs={{0,1},{1,0},{2,3},{3,2},{4,5},{5,4},{6,7},{7,6},{8,9},{9,8},{10,11... | collective-permute-start | bytes 786440 | tf_op jit(solution)/shard_map/ppermute | solution.py:381
  32.3 5.7 %collective-permute-start.9 = (bf16[1,24,1024]{2,1,0:T(8,128)(2,1)S(1)}, bf16[1,24,1024]{2,1,0:T(8,128)(2,1)S(1)}, u32[]{:S(2)}, u32[]{:S(2)}) collective-permute-start(bf16[1,24,1024]{2,1,0:T(8,128)(2,1)S(1)} %get-tuple-element.66), channel_id=1, source_target_pairs={{0,64},{64,0},{32,96},{96,32},{1,65},{65,1},{33,97},{97,33},{2,66}... | collective-permute-start | bytes 147464 | tf_op jit(solution)/shard_map/ppermute | solution.py:477
  38.1 6.9 %collective-permute-start.10 = (bf16[2,24,1024]{2,1,0:T(8,128)(2,1)S(1)}, bf16[2,24,1024]{2,1,0:T(8,128)(2,1)S(1)}, u32[]{:S(2)}, u32[]{:S(2)}) collective-permute-start(bf16[2,24,1024]{2,1,0:T(8,128)(2,1)S(1)} %get-tuple-element.67), channel_id=1, source_target_pairs={{0,96},{96,0},{32,64},{64,32},{1,97},{97,1},{33,65},{65,33},{2,98}... | collective-permute-start | bytes 294920 | tf_op jit(solution)/shard_map/ppermute | solution.py:481
  43.7 3.3 %collective-permute-start.11 = (bf16[2,24,1024]{2,1,0:T(8,128)(2,1)S(1)}, bf16[2,24,1024]{2,1,0:T(8,128)(2,1)S(1)}, u32[]{:S(2)}, u32[]{:S(2)}) collective-permute-start(bf16[2,24,1024]{2,1,0:T(8,128)(2,1)S(1)} %get-tuple-element.71), channel_id=1, source_target_pairs={{0,96},{32,64},{1,97},{33,65},{2,98},{34,66},{3,99},{35,67},{4,100... | collective-permute-start | bytes 294920 | tf_op jit(solution)/shard_map/ppermute | solution.py:483
  45.0 27.4 %copy-start = (s32[8]{0:T(128)S(1)}, s32[8]{0:T(128)}, u32[]{:S(2)}) copy-start(s32[8]{0:T(128)} %order.1) | copy-start | bytes 100
  47.1 3.5 %collective-permute-start = (f32[8,128]{1,0:T(8,128)S(1)}, f32[8,128]{1,0:T(8,128)S(1)}, u32[]{:S(2)}, u32[]{:S(2)}) collective-permute-start(f32[8,128]{1,0:T(8,128)S(1)} %param.1), channel_id=1, source_target_pairs={{0,32},{32,0},{64,96},{96,64},{1,33},{33,1},{65,97},{97,65},{2,34}... | collective-permute-start | bytes 12296 | tf_op jit(solution)/shard_map/cond/branch_1_fun/ppermute | solution.py:397
  68.6 3.8 %collective-permute-start.12 = (f32[24,128]{1,0:T(8,128)S(1)}, f32[24,128]{1,0:T(8,128)S(1)}, u32[]{:S(2)}, u32[]{:S(2)}) collective-permute-start(f32[24,128]{1,0:T(8,128)S(1)} %pad_maximum_fusion.mine), channel_id=1, source_target_pairs={{0,96},{96,0},{32,64},{64,32},{1,97},{97,1},{33,65},{65,33},{2,98}... | collective-permute-start | bytes 36872 | tf_op jit(solution)/shard_map/ppermute | solution.py:491

commit v5 on v4

--- a/solution.py
+++ b/solution.py
@@ -260,42 +260,51 @@
     )
 
 
-def encode_body(steps, last, v, all_taps, all_out, all_gain, qw, qb, *rest):
+def encode_body(steps, last, v_in, all_taps, all_out, all_gain, qw, qb, *rest):
     section = lax.axis_index("section")
-    codes, stats, buf, sums = rest[-4:]
+    v, codes, stats, sums = rest[-4:]
     sums[...] = rest[0][...] if len(rest) > 4 else jnp.zeros_like(sums)
-    row = lax.broadcasted_iota(jnp.int32, (CODE_ROWS, CLIPS * ROWS), 0)
-    top = lax.broadcasted_iota(jnp.int32, (CODE_ROWS, 128), 0)
-    lane = lax.broadcasted_iota(jnp.int32, (CODE_ROWS, 128), 1)
-
-    def chunk(i, t):
-        buf[...] = v[t]
-
+    n = len(steps)
+    span = CLIPS * ROWS
+
+    def blocks(t):
         def step(b, _):
-            block_at(b, buf, all_taps, all_out, all_gain)
+            block_at(b, v.at[t], all_taps, all_out, all_gain)
             return 0
 
         lax.fori_loop(1 - section, 2, step, 0)
-        logits = jnp.dot(
-            buf[...].reshape(CLIPS * ROWS, C), qw[...], preferred_element_type=jnp.float32
-        )
+
+    def quantize():
+        row = lax.broadcasted_iota(jnp.int32, (CODE_ROWS, n * span), 0)
+        top = lax.broadcasted_iota(jnp.int32, (CODE_ROWS, 128), 0)
+        lane = lax.broadcasted_iota(jnp.int32, (CODE_ROWS, 128), 1)
+        rows = v[steps[0] : steps[0] + n].reshape(n * span, C)
+        logits = jnp.dot(rows, qw[...], preferred_element_type=jnp.float32)
         z = (4.0 * (logits + qb[0:1, :])).T[:CODE_ROWS]
         size = jnp.abs(z)
         e = jnp.exp(-size)
         r = 1.0 / (1.0 + e)
-        p = jnp.where(z >= 0, r, e * r)
-        entropy = jnp.log1p(e) + size * (e * r)
         valid = row < BITS
-        codes[i] = jnp.where(valid, 2.0 * p - 1.0, 0.0).astype(jnp.bfloat16)
-        bit_sums = jnp.sum(jnp.where(valid, p, 0.0), axis=1, keepdims=True)
-        total = jnp.sum(
-            jnp.sum(jnp.where(valid, entropy, 0.0), axis=1, keepdims=True), axis=0, keepdims=True
-        )
-        column = jnp.where(top == BITS, total, bit_sums)
-        sums[...] += jnp.where(lane == batch_of(t), column, 0.0)
-
-    for i, t in enumerate(steps):
-        pl.when(has_chunk(t, (0, 1)))(functools.partial(chunk, i, t))
+        p = jnp.where(valid, jnp.where(z >= 0, r, e * r), 0.0)
+        entropy = jnp.where(valid, jnp.log1p(e) + size * (e * r), 0.0)
+        code = jnp.where(valid, 2.0 * p - 1.0, 0.0).astype(jnp.bfloat16)
+        added = jnp.zeros((CODE_ROWS, 128), jnp.float32)
+        for i, t in enumerate(steps):
+            at = slice(i * span, (i + 1) * span)
+            codes[i] = code[:, at]
+            bit_sums = jnp.sum(p[:, at], axis=1, keepdims=True)
+            total = jnp.sum(
+                jnp.sum(entropy[:, at], axis=0, keepdims=True), axis=1, keepdims=True
+            )
+            column = jnp.where(top == BITS, total, bit_sums)
+            batch = jnp.where(has_chunk(t, (0, 1)), batch_of(t), -1)
+            added = added + jnp.where(lane == batch, column, 0.0)
+        sums[...] += added
+
+    for t in steps:
+        pl.when(has_chunk(t, (0, 1)))(functools.partial(blocks, t))
+    active = functools.reduce(jnp.logical_or, [has_chunk(t, (0, 1)) for t in steps])
+    pl.when(active)(quantize)
 
     if last:
         full = jnp.concatenate([sums[...], jnp.zeros((128 - CODE_ROWS, 128), jnp.float32)], axis=0)
@@ -453,17 +462,22 @@
         join_body, [VM] + [ANY] * 7 + [VM] * 3, kinds, [dma((24,))], aliases={8: 0, 9: 1, 10: 2}
     )(mine, second, up, down, *swapped, *weights)
 
-    def encode(steps, before, last):
+    def encode(steps, v, before, last):
         n = len(steps)
         return call(
             functools.partial(encode_body, steps, last),
             [VM] * (6 + len(before)),
-            [((n, CODE_ROWS, CLIPS * ROWS), bf16), ((8 if last else CODE_ROWS, 128), f32)],
-            [pltpu.VMEM(chunk, bf16), pltpu.VMEM((CODE_ROWS, 128), f32)],
+            [
+                v_kind,
+                ((n, CODE_ROWS, CLIPS * ROWS), bf16),
+                ((8 if last else CODE_ROWS, 128), f32),
+            ],
+            [pltpu.VMEM((CODE_ROWS, 128), f32)],
             blocks=2 * n,
+            aliases={0: 0},
         )(v, *weights, qw, qb, *before)
 
-    def decode(steps, codes):
+    def decode(steps, v, codes):
         n = len(steps)
         return call(
             functools.partial(decode_body, steps),
@@ -473,18 +487,18 @@
             blocks=2 * n,
         )(v, *weights, post, codes)[0]
 
-    codes, stats = encode((0,), (), False)
+    v, codes, stats = encode((0,), v, (), False)
     codes_a = lax.ppermute(codes, "section", FAR)
-    codes, stats = encode((1, 2), (stats,), False)
-    e0 = decode((0,), codes_a)
-    codes, e0 = lax.optimization_barrier((codes, e0))
+    v, codes, stats = encode((1, 2), v, (stats,), False)
+    e0 = decode((0,), v, codes_a)
+    codes, e0, v = lax.optimization_barrier((codes, e0, v))
     codes_b = lax.ppermute(codes, "section", CROSS)
-    codes, stats = encode((3, 4), (stats,), True)
+    v, codes, stats = encode((3, 4), v, (stats,), True)
     codes_c = lax.ppermute(codes, "section", ((0, 3), (1, 2)))
     codes_b, stats = lax.optimization_barrier((codes_b, stats))
-    e12 = decode((1, 2), codes_b)
+    e12 = decode((1, 2), v, codes_b)
     codes_c, e12 = lax.optimization_barrier((codes_c, e12))
-    e34 = decode((3, 4), codes_c)
+    e34 = decode((3, 4), v, codes_c)
     stats, e12, e34, encoder = lax.optimization_barrier((stats, e12, e34, encoder))
     total = lax.cond(encoder == 1, encoder_sum, lambda x: 0.0 * x, stats)
     packed = jnp.concatenate([total, e12[0], e12[1]], axis=0)

time: 74.1 us -> 74.3 us (level)
  starting transfers between devices: 12.3 us -> 13.4 us
  Pallas kernels: 30 us -> 29 us
    ppermute x1, starting transfers between devices: 2.51 us -> 3.66 us  [encoder_sum(): x = x + lax.ppermute(x, 'section', PAIR)]
    pallas_call x3, Pallas kernels: 13.9 us -> 13 us  [encode(): call(functools.partial(encode_body, steps, last), [VM] * (6 + len(before)...]
  transfers between devices with their start and end apart: 13 -> 13, of which waited for: 5 -> 5; matrix products, arithmetic and copies ran while one was open for 0% -> 0% of each run, Pallas kernels for 33% -> 31%
where the time goes in v5:
time: 74.3 us; the launch traced here: 73.9 us
  Pallas kernels  29 us (39%)
  blocking collectives  18.2 us (24%)
  starting transfers between devices  13.4 us (18%)
  waiting for transfers between devices  12.5 us (17%)
  between operations  0.79 us (1%)
    all_to_all x1, blocking collectives, encoder_sum(): lax.all_to_all(jnp.broadcast_to(x[None], (n, *x.shape)), DP, 0, 0)  18.2 us
    pallas_call x3, Pallas kernels, encode(): call(functools.partial(encode_body, steps, last), [VM] * (6 + len(before)...  13 us
    pallas_call x1, Pallas kernels, on_device(): call(functools.partial(start_body, 2), [HB] * 8, [v_kind, *kinds, ((C, 12...  6.71 us
    pallas_call x1, Pallas kernels, on_device(): call(functools.partial(more_body, 2, STEPS), [VM] * 4, [v_kind], blocks=3...  6.19 us
    ppermute x1, waiting for transfers between devices, on_device(): mine = lax.ppermute(piece, 'section', PAIR)  4.51 us
    ppermute x1, waiting for transfers between devices, on_device(): cross = lax.ppermute(packed, 'section', CROSS)  3.74 us
    ppermute x1, starting transfers between devices, encoder_sum(): x = x + lax.ppermute(x, 'section', PAIR)  3.66 us
    ppermute x2, starting transfers between devices, within_corner(): return lax.ppermute(x, DP, pairs)  3.18 us
  transfers between devices with their start and end apart: 13, of which 5 were waited for; matrix products, arithmetic and copies ran while one was open for 0% of the time, Pallas kernels for 31%

profile of v5, /device:TPU:1, one launch (start us, length us, event | category | flops | bytes accessed | tf_op | source)
XLA Modules:
  0.0 73.9 jit_solution(16547762039974198179)
XLA Ops:
  0.6 1.2 %shard_map.104 = (bf16[1040,128]{1,0:T(8,128)(2,1)S(1)}, bf16[1024,128]{1,0:T(8,128)(2,1)S(1)}) custom-call(bf16[1536,512]{1,0:T(8,128)(2,1)} %bitcast.9, bf16[512,512]{1,0:T(8,128)(2,1)} %bitcast.11, bf16[1,512]{1,0:T(2,128)(2,1)} %gain_hbm.1), custom_call_target="tpu_custom_call" | custom-call | tf_op jit(solution)/shard_map/pallas_call | solution.py:429
  1.8 2.1 %collective-permute-start.4 = (bf16[1024,128]{1,0:T(8,128)(2,1)S(1)}, bf16[1024,128]{1,0:T(8,128)(2,1)S(1)}, u32[]{:S(2)}, u32[]{:S(2)}) collective-permute-start(bf16[1024,128]{1,0:T(8,128)(2,1)S(1)} %get-tuple-element.52), channel_id=1, source_target_pairs={{0,32},{32,0},{64,96},{96,64},{1,33},{33,1},{65,97},{97,65},{2,34}... | collective-permute-start | bytes 786440 | tf_op jit(solution)/shard_map/ppermute | solution.py:436
  3.9 0.1 collective-permute-start.1
  4.0 6.7 %shard_map.105 = (bf16[5,4,256,512]{3,2,1,0:T(8,128)(2,1)S(1)}, bf16[2,1536,512]{2,1,0:T(8,128)(2,1)S(1)}, bf16[2,512,512]{2,1,0:T(8,128)(2,1)S(1)}, f32[2,8,512...) custom-call(bf16[32,256,512]{2,1,0:T(8,128)(2,1)} %pool.1, ...), custom_call_target="tpu_custom_call" | custom-call | flops 4294967296 | tf_op jit(solution)/shard_map/pallas_call | solution.py:438
  10.7 4.5 %collective-permute-done.1.refs_0_ = bf16[1040,128]{1,0:T(8,128)(2,1)S(1)} collective-permute-done((bf16[1040,128]{1,0:T(8,128)(2,1)S(1)}, bf16[1040,128]{1,0:T(8,128)(2,1)S(1)}, u32[]{:S(2)}, u32[]{:S(2)}) %collective-permute-start.1) | collective-permute-done | bytes 266272 | tf_op jit(solution)/shard_map/ppermute | solution.py:435
  15.2 1.7 %collective-permute-start.5 = (bf16[1040,128]{1,0:T(8,128)(2,1)S(1)}, bf16[1040,128]{1,0:T(8,128)(2,1)S(1)}, u32[]{:S(2)}, u32[]{:S(2)}) collective-permute-start(bf16[1040,128]{1,0:T(8,128)(2,1)S(1)} %collective-permute-done.1.refs_0_), channel_id=1, source_target_pairs={{0,1},{1,0},{2,3},{3,2},{4,5},{5,4},{6,7},{7,6},{8,9},{9,8},{10,11... | collective-permute-start | bytes 798728 | tf_op jit(solution)/shard_map/ppermute | solution.py:390
  16.9 1.5 %collective-permute-start.3 = (bf16[1040,128]{1,0:T(8,128)(2,1)S(1)}, bf16[1040,128]{1,0:T(8,128)(2,1)S(1)}, u32[]{:S(2)}, u32[]{:S(2)}) collective-permute-start(bf16[1040,128]{1,0:T(8,128)(2,1)S(1)} %collective-permute-done.1.refs_0_), channel_id=1, source_target_pairs={{0,2},{1,9},{2,0},{3,11},{4,6},{5,13},{6,4},{7,15},{8,10},{9,1},{1... | collective-permute-start | bytes 798728 | tf_op jit(solution)/shard_map/ppermute | solution.py:401
  18.4 1.6 %collective-permute-start.2 = (bf16[1040,128]{1,0:T(8,128)(2,1)S(1)}, bf16[1040,128]{1,0:T(8,128)(2,1)S(1)}, u32[]{:S(2)}, u32[]{:S(2)}) collective-permute-start(bf16[1040,128]{1,0:T(8,128)(2,1)S(1)} %collective-permute-done.1.refs_0_), channel_id=1, source_target_pairs={{0,8},{1,3},{2,10},{3,1},{4,12},{5,7},{6,14},{7,5},{8,0},{9,11},{1... | collective-permute-start | bytes 798728 | tf_op jit(solution)/shard_map/ppermute | solution.py:401
  20.1 6.2 %shard_map.106.v_in = bf16[5,4,256,512]{3,2,1,0:T(8,128)(2,1)S(1)} custom-call(bf16[5,4,256,512]{3,2,1,0:T(8,128)(2,1)S(1)} %get-tuple-element.53.before, bf16[2,1536,512]{2,1,0:T(8,128)(2,1)S(1)} %get-tuple-element.54.all_taps.refs_8_, bf16[2,512,512]{2,1,0:T(8,128)(2,1)S(1)} %get-tuple-element.55.all_out.refs_9_, ...), custom_call_target="tpu_custom_call", output_to_operand_aliasing={{}: (0, {})} | custom-call | flops 6442450944 | tf_op jit(solution)/shard_map/pallas_call | solution.py:456
  26.3 0.0 collective-permute-done.4.refs_1_
  26.3 0.0 collective-permute-done.5.refs_4_
  26.3 0.0 collective-permute-done.3.refs_3_
  26.3 0.0 collective-permute-done.2.refs_2_
  26.3 0.6 collective-permute-start.8
  27.0 0.1 collective-permute-start.7
  27.1 0.4 collective-permute-start.6
  27.5 1.4 %collective-permute-done.6.refs_5_ = bf16[1024,128]{1,0:T(8,128)(2,1)S(1)} collective-permute-done((bf16[1024,128]{1,0:T(8,128)(2,1)S(1)}, bf16[1024,128]{1,0:T(8,128)(2,1)S(1)}, u32[]{:S(2)}, u32[]{:S(2)}) %collective-permute-start.6) | collective-permute-done | bytes 262176 | tf_op jit(solution)/shard_map/ppermute | solution.py:390
  28.9 0.0 collective-permute-done.8.refs_7_
  28.9 0.0 collective-permute-done.7.refs_6_
  28.9 0.6 shard_map.107
  29.5 2.7 %shard_map.108 = (bf16[5,4,256,512]{3,2,1,0:T(8,128)(2,1)S(1)}, bf16[1,24,1024]{2,1,0:T(8,128)(2,1)S(1)}, f32[24,128]{1,0:T(8,128)S(1)}) custom-call(bf16[5,4,256,512]{3,2,1,0:T(8,128)(2,1)S(1)} %shard_map.106.v_in, bf16[2,1536,512]{2,1,0:T(8,128)(2,1)S(1)} %get-tuple-element.62.all_taps, ...), custom_call_target="tpu_custom_call", output_to_operand_aliasing={{0}: (0, {})} | custom-call | flops 4294967296 | tf_op jit(solution)/shard_map/pallas_call | solution.py:467
  32.2 0.1 collective-permute-start.9
  32.3 5.2 %shard_map.109 = (bf16[5,4,256,512]{3,2,1,0:T(8,128)(2,1)S(1)}, bf16[2,24,1024]{2,1,0:T(8,128)(2,1)S(1)}, f32[24,128]{1,0:T(8,128)S(1)}) custom-call(bf16[5,4,256,512]{3,2,1,0:T(8,128)(2,1)S(1)} %get-tuple-element.67.v_in, bf16[2,1536,512]{2,1,0:T(8,128)(2,1)S(1)} %get-tuple-element.62.all_taps, ...), custom_call_target="tpu_custom_call", output_to_operand_aliasing={{0}: (0, {})} | custom-call | flops 8589934592 | tf_op jit(solution)/shard_map/pallas_call | solution.py:467
  37.5 0.0 collective-permute-done.9.codes
  37.6 0.1 collective-permute-start.10
  37.7 5.1 %shard_map.111 = (bf16[5,4,256,512]{3,2,1,0:T(8,128)(2,1)S(1)}, bf16[2,24,1024]{2,1,0:T(8,128)(2,1)S(1)}, f32[8,128]{1,0:T(8,128)S(1)}) custom-call(bf16[5,4,256,512]{3,2,1,0:T(8,128)(2,1)S(1)} %get-tuple-element.74.v.v_in, bf16[2,1536,512]{2,1,0:T(8,128)(2,1)S(1)} %get-tuple-element.62.all_taps, ...), custom_call_target="tpu_custom_call", output_to_operand_aliasing={{0}: (0, {})} | custom-call | flops 8589934592 | tf_op jit(solution)/shard_map/pallas_call | solution.py:467
  42.7 1.3 %collective-permute-start.11 = (bf16[2,24,1024]{2,1,0:T(8,128)(2,1)S(1)}, bf16[2,24,1024]{2,1,0:T(8,128)(2,1)S(1)}, u32[]{:S(2)}, u32[]{:S(2)}) collective-permute-start(bf16[2,24,1024]{2,1,0:T(8,128)(2,1)S(1)} %get-tuple-element.78), channel_id=1, source_target_pairs={{0,96},{32,64},{1,97},{33,65},{2,98},{34,66},{3,99},{35,67},{4,100... | collective-permute-start | bytes 294920 | tf_op jit(solution)/shard_map/ppermute | solution.py:497
  44.1 0.0 collective-permute-done.10.codes
  44.1 0.0 copy-start
  44.1 1.8 %collective-permute-done.11.codes = bf16[2,24,1024]{2,1,0:T(8,128)(2,1)S(1)} collective-permute-done((bf16[2,24,1024]{2,1,0:T(8,128)(2,1)S(1)}, bf16[2,24,1024]{2,1,0:T(8,128)(2,1)S(1)}, u32[]{:S(2)}, u32[]{:S(2)}) %collective-permute-start.11) | collective-permute-done | bytes 98336 | tf_op jit(solution)/shard_map/ppermute | solution.py:497
  45.9 22.9 %conditional.1 = (f32[8,128]{1,0:T(8,128)S(1)}) conditional(s32[]{:T(128)} %convert_element_type.7, f32[8,128]{1,0:T(8,128)S(1)} %get-tuple-element.85, f32[8,128]{1,0:T(8,128)S(1)} %get-tuple-element.85), branch_computations={%region_0.0_spmd, %region_1.0_spmd} | conditional | flops 32768 | bytes 561204 | solution.py:503
  45.9 3.7 %collective-permute-start = (f32[8,128]{1,0:T(8,128)S(1)}, f32[8,128]{1,0:T(8,128)S(1)}, u32[]{:S(2)}, u32[]{:S(2)}) collective-permute-start(f32[8,128]{1,0:T(8,128)S(1)} %param.1), channel_id=1, source_target_pairs={{0,32},{32,0},{64,96},{96,64},{1,33},{33,1},{65,97},{97,65},{2,34}... | collective-permute-start | bytes 12296 | tf_op jit(solution)/shard_map/cond/branch_1_fun/ppermute | solution.py:406
  49.5 1.0 %collective-permute-done = f32[8,128]{1,0:T(8,128)S(1)} collective-permute-done((f32[8,128]{1,0:T(8,128)S(1)}, f32[8,128]{1,0:T(8,128)S(1)}, u32[]{:S(2)}, u32[]{:S(2)}) %collective-permute-start) | collective-permute-done | bytes 4128 | tf_op jit(solution)/shard_map/cond/branch_1_fun/ppermute | solution.py:406
  50.6 18.2 %all_to_all.4 = f32[32,8,128]{2,1,0:T(8,128)S(1)} all-to-all(f32[32,8,128]{2,1,0:T(8,128)S(1)} %broadcast_in_dim.0), channel_id=1, replica_groups=mesh['section'=4,'dp_0'=4,'dp_1'=4,'dp_2'=2] {'dp_0','dp_1','dp_2'}, dimensions={0} | all-to-all | bytes 262144 | tf_op jit(solution)/shard_map/cond/branch_1_fun/all_to_all | solution.py:407
  68.8 0.1 collective-permute-start.12
  68.9 3.7 %collective-permute-done.12.cross = f32[24,128]{1,0:T(8,128)S(1)} collective-permute-done((f32[24,128]{1,0:T(8,128)S(1)}, f32[24,128]{1,0:T(8,128)S(1)}, u32[]{:S(2)}, u32[]{:S(2)}) %collective-permute-start.12) | collective-permute-done | bytes 12320 | tf_op jit(solution)/shard_map/ppermute | solution.py:505
  72.6 0.0 copy-done
  72.6 1.3 %shard_map.114 = (f32[2,4,256]{2,1,0:T(4,128)}, f32[8]{0:T(128)}) custom-call(s32[8]{0:T(128)S(1)} %copy-done, f32[24,128]{1,0:T(8,128)S(1)} %pad_maximum_fusion.mine, f32[24,128]{1,0:T(8,128)S(1)} %collective-permute-done.12.cross, f32[1,8,128]{2,1,0:T(8,128)S(1)} %shard_map.110.e0, f32[2,8,128]{2,1,0:T(8,128)S(1)} %shard_map.113.e34), custom_call_target="tpu_custom_call" | custom-call | tf_op jit(solution)/shard_map/pallas_call | solution.py:507
  (8 shorter events, 0.1 us)
Async XLA Ops:
  1.8 24.5 %collective-permute-start.4 = (bf16[1024,128]{1,0:T(8,128)(2,1)S(1)}, bf16[1024,128]{1,0:T(8,128)(2,1)S(1)}, u32[]{:S(2)}, u32[]{:S(2)}) collective-permute-start(bf16[1024,128]{1,0:T(8,128)(2,1)S(1)} %get-tuple-element.52), channel_id=1, source_target_pairs={{0,32},{32,0},{64,96},{96,64},{1,33},{33,1},{65,97},{97,65},{2,34}... | collective-permute-start | bytes 786440 | tf_op jit(solution)/shard_map/ppermute | solution.py:436
  3.9 11.3 %collective-permute-start.1 = (bf16[1040,128]{1,0:T(8,128)(2,1)S(1)}, bf16[1040,128]{1,0:T(8,128)(2,1)S(1)}, u32[]{:S(2)}, u32[]{:S(2)}) collective-permute-start(bf16[1040,128]{1,0:T(8,128)(2,1)S(1)} %get-tuple-element.49), channel_id=1, source_target_pairs={{0,32},{32,0},{64,96},{96,64},{1,33},{33,1},{65,97},{97,65},{2,34}... | collective-permute-start | bytes 798728 | tf_op jit(solution)/shard_map/ppermute | solution.py:435
  15.2 11.0 %collective-permute-start.5 = (bf16[1040,128]{1,0:T(8,128)(2,1)S(1)}, bf16[1040,128]{1,0:T(8,128)(2,1)S(1)}, u32[]{:S(2)}, u32[]{:S(2)}) collective-permute-start(bf16[1040,128]{1,0:T(8,128)(2,1)S(1)} %collective-permute-done.1.refs_0_), channel_id=1, source_target_pairs={{0,1},{1,0},{2,3},{3,2},{4,5},{5,4},{6,7},{7,6},{8,9},{9,8},{10,11... | collective-permute-start | bytes 798728 | tf_op jit(solution)/shard_map/ppermute | solution.py:390
  16.9 9.4 %collective-permute-start.3 = (bf16[1040,128]{1,0:T(8,128)(2,1)S(1)}, bf16[1040,128]{1,0:T(8,128)(2,1)S(1)}, u32[]{:S(2)}, u32[]{:S(2)}) collective-permute-start(bf16[1040,128]{1,0:T(8,128)(2,1)S(1)} %collective-permute-done.1.refs_0_), channel_id=1, source_target_pairs={{0,2},{1,9},{2,0},{3,11},{4,6},{5,13},{6,4},{7,15},{8,10},{9,1},{1... | collective-permute-start | bytes 798728 | tf_op jit(solution)/shard_map/ppermute | solution.py:401
  18.4 7.9 %collective-permute-start.2 = (bf16[1040,128]{1,0:T(8,128)(2,1)S(1)}, bf16[1040,128]{1,0:T(8,128)(2,1)S(1)}, u32[]{:S(2)}, u32[]{:S(2)}) collective-permute-start(bf16[1040,128]{1,0:T(8,128)(2,1)S(1)} %collective-permute-done.1.refs_0_), channel_id=1, source_target_pairs={{0,8},{1,3},{2,10},{3,1},{4,12},{5,7},{6,14},{7,5},{8,0},{9,11},{1... | collective-permute-start | bytes 798728 | tf_op jit(solution)/shard_map/ppermute | solution.py:401
  26.3 2.6 %collective-permute-start.8 = (bf16[1040,128]{1,0:T(8,128)(2,1)S(1)}, bf16[1040,128]{1,0:T(8,128)(2,1)S(1)}, u32[]{:S(2)}, u32[]{:S(2)}) collective-permute-start(bf16[1040,128]{1,0:T(8,128)(2,1)S(1)} %collective-permute-done.2.refs_2_), channel_id=1, source_target_pairs={{0,1},{1,0},{2,3},{3,2},{4,5},{5,4},{6,7},{7,6},{8,9},{9,8},{10,11... | collective-permute-start | bytes 798728 | tf_op jit(solution)/shard_map/ppermute | solution.py:390
  27.0 1.9 %collective-permute-start.7 = (bf16[1040,128]{1,0:T(8,128)(2,1)S(1)}, bf16[1040,128]{1,0:T(8,128)(2,1)S(1)}, u32[]{:S(2)}, u32[]{:S(2)}) collective-permute-start(bf16[1040,128]{1,0:T(8,128)(2,1)S(1)} %collective-permute-done.3.refs_3_), channel_id=1, source_target_pairs={{0,1},{1,0},{2,3},{3,2},{4,5},{5,4},{6,7},{7,6},{8,9},{9,8},{10,11... | collective-permute-start | bytes 798728 | tf_op jit(solution)/shard_map/ppermute | solution.py:390
  27.1 1.8 %collective-permute-start.6 = (bf16[1024,128]{1,0:T(8,128)(2,1)S(1)}, bf16[1024,128]{1,0:T(8,128)(2,1)S(1)}, u32[]{:S(2)}, u32[]{:S(2)}) collective-permute-start(bf16[1024,128]{1,0:T(8,128)(2,1)S(1)} %collective-permute-done.4.refs_1_), channel_id=1, source_target_pairs={{0,1},{1,0},{2,3},{3,2},{4,5},{5,4},{6,7},{7,6},{8,9},{9,8},{10,11... | collective-permute-start | bytes 786440 | tf_op jit(solution)/shard_map/ppermute | solution.py:390
  32.2 5.3 %collective-permute-start.9 = (bf16[1,24,1024]{2,1,0:T(8,128)(2,1)S(1)}, bf16[1,24,1024]{2,1,0:T(8,128)(2,1)S(1)}, u32[]{:S(2)}, u32[]{:S(2)}) collective-permute-start(bf16[1,24,1024]{2,1,0:T(8,128)(2,1)S(1)} %get-tuple-element.72), channel_id=1, source_target_pairs={{0,64},{64,0},{32,96},{96,32},{1,65},{65,1},{33,97},{97,33},{2,66}... | collective-permute-start | bytes 147464 | tf_op jit(solution)/shard_map/ppermute | solution.py:491
  37.6 6.5 %collective-permute-start.10 = (bf16[2,24,1024]{2,1,0:T(8,128)(2,1)S(1)}, bf16[2,24,1024]{2,1,0:T(8,128)(2,1)S(1)}, u32[]{:S(2)}, u32[]{:S(2)}) collective-permute-start(bf16[2,24,1024]{2,1,0:T(8,128)(2,1)S(1)} %get-tuple-element.73), channel_id=1, source_target_pairs={{0,96},{96,0},{32,64},{64,32},{1,97},{97,1},{33,65},{65,33},{2,98}... | collective-permute-start | bytes 294920 | tf_op jit(solution)/shard_map/ppermute | solution.py:495
  42.7 3.1 %collective-permute-start.11 = (bf16[2,24,1024]{2,1,0:T(8,128)(2,1)S(1)}, bf16[2,24,1024]{2,1,0:T(8,128)(2,1)S(1)}, u32[]{:S(2)}, u32[]{:S(2)}) collective-permute-start(bf16[2,24,1024]{2,1,0:T(8,128)(2,1)S(1)} %get-tuple-element.78), channel_id=1, source_target_pairs={{0,96},{32,64},{1,97},{33,65},{2,98},{34,66},{3,99},{35,67},{4,100... | collective-permute-start | bytes 294920 | tf_op jit(solution)/shard_map/ppermute | solution.py:497
  44.1 28.5 %copy-start = (s32[8]{0:T(128)S(1)}, s32[8]{0:T(128)}, u32[]{:S(2)}) copy-start(s32[8]{0:T(128)} %order.1) | copy-start | bytes 100
  45.9 4.7 %collective-permute-start = (f32[8,128]{1,0:T(8,128)S(1)}, f32[8,128]{1,0:T(8,128)S(1)}, u32[]{:S(2)}, u32[]{:S(2)}) collective-permute-start(f32[8,128]{1,0:T(8,128)S(1)} %param.1), channel_id=1, source_target_pairs={{0,32},{32,0},{64,96},{96,64},{1,33},{33,1},{65,97},{97,65},{2,34}... | collective-permute-start | bytes 12296 | tf_op jit(solution)/shard_map/cond/branch_1_fun/ppermute | solution.py:406
  68.8 3.8 %collective-permute-start.12 = (f32[24,128]{1,0:T(8,128)S(1)}, f32[24,128]{1,0:T(8,128)S(1)}, u32[]{:S(2)}, u32[]{:S(2)}) collective-permute-start(f32[24,128]{1,0:T(8,128)S(1)} %pad_maximum_fusion.mine), channel_id=1, source_target_pairs={{0,96},{96,0},{32,64},{64,32},{1,97},{97,1},{33,65},{65,33},{2,98}... | collective-permute-start | bytes 36872 | tf_op jit(solution)/shard_map/ppermute | solution.py:505

commit v6 on v5

--- a/solution.py
+++ b/solution.py
@@ -345,9 +345,9 @@
         target[c : c + 1, :] = jnp.concatenate([row[0:1], row[1:2]], axis=1)
 
 
-def final_body(rows_total, order, mine, cross, e0, e34, error, loss):
+def final_body(rows_total, order, mine, cross, given, e0, e34, error, loss):
     section = lax.axis_index("section")
-    sums = jnp.where(section <= 1, mine[0:8], cross[0:8]) * (1.0 / rows_total)
+    sums = jnp.where(section <= 1, mine[...], cross[...]) * (1.0 / rows_total)
     row = lax.broadcasted_iota(jnp.int32, sums.shape, 0)
     lane = lax.broadcasted_iota(jnp.int32, sums.shape, 1)
     averaged = jnp.zeros_like(sums)
@@ -366,8 +366,8 @@
 
     @pl.when(section <= 1)
     def _():
-        unpack(error.at[0], cross.at[pl.ds(8, 8)])
-        unpack(error.at[1], cross.at[pl.ds(16, 8)])
+        unpack(error.at[0], given.at[0])
+        unpack(error.at[1], given.at[1])
 
     @pl.when(section == 2)
     def _():
@@ -382,7 +382,6 @@
 
 PAIR = ((0, 1), (1, 0), (2, 3), (3, 2))
 CROSS = ((0, 3), (3, 0), (1, 2), (2, 1))
-FAR = ((0, 2), (2, 0), (1, 3), (3, 1))
 
 
 def shifted(x, axis, by):
@@ -488,27 +487,26 @@
         )(v, *weights, post, codes)[0]
 
     v, codes, stats = encode((0,), v, (), False)
-    codes_a = lax.ppermute(codes, "section", FAR)
+    codes_a = lax.ppermute(codes, "section", ((0, 2),))
     v, codes, stats = encode((1, 2), v, (stats,), False)
-    e0 = decode((0,), v, codes_a)
-    codes, e0, v = lax.optimization_barrier((codes, e0, v))
     codes_b = lax.ppermute(codes, "section", CROSS)
     v, codes, stats = encode((3, 4), v, (stats,), True)
     codes_c = lax.ppermute(codes, "section", ((0, 3), (1, 2)))
-    codes_b, stats = lax.optimization_barrier((codes_b, stats))
+    codes_a, stats = lax.optimization_barrier((codes_a, stats))
+    e0 = decode((0,), v, codes_a)
+    codes_b, e0 = lax.optimization_barrier((codes_b, e0))
     e12 = decode((1, 2), v, codes_b)
-    codes_c, e12 = lax.optimization_barrier((codes_c, e12))
+    given = lax.ppermute(e12, "section", ((3, 0), (2, 1)))
     e34 = decode((3, 4), v, codes_c)
-    stats, e12, e34, encoder = lax.optimization_barrier((stats, e12, e34, encoder))
+    stats, e34, encoder = lax.optimization_barrier((stats, e34, encoder))
     total = lax.cond(encoder == 1, encoder_sum, lambda x: 0.0 * x, stats)
-    packed = jnp.concatenate([total, e12[0], e12[1]], axis=0)
-    cross = lax.ppermute(packed, "section", CROSS)
+    cross = lax.ppermute(total, "section", ((0, 3), (1, 2)))
     rows_total = float(CLIPS * lax.axis_size(DP) * ROWS)
     error, loss = call(
         functools.partial(final_body, rows_total),
-        [SM] + [VM] * 4,
+        [SM] + [VM] * 5,
         [((2, CLIPS, ROWS), f32), ((8,), f32)],
-    )(order, packed, cross, e0, e34)
+    )(order, total, cross, given, e0, e34)
     return error, loss
 
 

time: 74.3 us -> 79.5 us (1.070); the launches traced: 73.9 us -> 78 us
  starting transfers between devices: 13.4 us -> 15.9 us
  waiting for transfers between devices: 12.5 us -> 14 us
    ppermute x2 -> x3, starting transfers between devices: 0.17 us -> 6 us  [the longest x1 3.3 us: on_device(): cross = lax.ppermute(total, 'section', ((0, 3), (1, 2)))]
    ppermute x1, waiting for transfers between devices: 0.01 us -> 5.14 us  [on_device(): codes_b = lax.ppermute(codes, 'section', CROSS)]
    ppermute x1, starting transfers between devices: 3.66 us -> 0.31 us  [encoder_sum(): x = x + lax.ppermute(x, 'section', PAIR)]
    ppermute x2 -> x3, waiting for transfers between devices: 3.75 us -> 0.74 us  [the longest x1 0.74 us: on_device(): cross = lax.ppermute(total, 'section', ((0, 3), (1, 2)))]
    ppermute x1, waiting for transfers between devices: 1.78 us -> 0.01 us  [on_device(): codes_c = lax.ppermute(codes, 'section', ((0, 3), (1, 2)))]
    ppermute x1, waiting for transfers between devices: 0.99 us -> 2.22 us  [encoder_sum(): x = x + lax.ppermute(x, 'section', PAIR)]
  transfers between devices with their start and end apart: 13 -> 14, of which waited for: 5 -> 5; matrix products, arithmetic and copies ran while one was open for 0% -> 0% of each run, Pallas kernels for 31% -> 30%
where the time goes in v6:
time: 79.5 us; the launch traced here: 78 us
  Pallas kernels  29.2 us (37%)
  blocking collectives  18 us (23%)
  starting transfers between devices  15.9 us (20%)
  waiting for transfers between devices  14 us (18%)
    all_to_all x1, blocking collectives, encoder_sum(): lax.all_to_all(jnp.broadcast_to(x[None], (n, *x.shape)), DP, 0, 0)  18 us
    pallas_call x3, Pallas kernels, encode(): call(functools.partial(encode_body, steps, last), [VM] * (6 + len(before)...  13 us
    pallas_call x1, Pallas kernels, on_device(): call(functools.partial(start_body, 2), [HB] * 8, [v_kind, *kinds, ((C, 12...  6.71 us
    pallas_call x1, Pallas kernels, on_device(): call(functools.partial(more_body, 2, STEPS), [VM] * 4, [v_kind], blocks=3...  6.19 us
    ppermute x1, waiting for transfers between devices, on_device(): codes_b = lax.ppermute(codes, 'section', CROSS)  5.14 us
    ppermute x1, waiting for transfers between devices, on_device(): mine = lax.ppermute(piece, 'section', PAIR)  4.51 us
    ppermute x1, starting transfers between devices, on_device(): cross = lax.ppermute(total, 'section', ((0, 3), (1, 2)))  3.3 us
    ppermute x2, starting transfers between devices, within_corner(): return lax.ppermute(x, DP, pairs)  3.18 us
  transfers between devices with their start and end apart: 14, of which 5 were waited for; matrix products, arithmetic and copies ran while one was open for 0% of the time, Pallas kernels for 30%

profile of v6, /device:TPU:1, one launch (start us, length us, event | category | flops | bytes accessed | tf_op | source)
XLA Modules:
  0.0 78.0 jit_solution(6397781326162285953)
XLA Ops:
  0.6 1.2 %shard_map.104 = (bf16[1040,128]{1,0:T(8,128)(2,1)S(1)}, bf16[1024,128]{1,0:T(8,128)(2,1)S(1)}) custom-call(bf16[1536,512]{1,0:T(8,128)(2,1)} %bitcast.5, bf16[512,512]{1,0:T(8,128)(2,1)} %bitcast.7, bf16[1,512]{1,0:T(2,128)(2,1)} %gain_hbm.1), custom_call_target="tpu_custom_call" | custom-call | tf_op jit(solution)/shard_map/pallas_call | solution.py:428
  1.8 2.1 %collective-permute-start.4 = (bf16[1024,128]{1,0:T(8,128)(2,1)S(1)}, bf16[1024,128]{1,0:T(8,128)(2,1)S(1)}, u32[]{:S(2)}, u32[]{:S(2)}) collective-permute-start(bf16[1024,128]{1,0:T(8,128)(2,1)S(1)} %get-tuple-element.48), channel_id=1, source_target_pairs={{0,32},{32,0},{64,96},{96,64},{1,33},{33,1},{65,97},{97,65},{2,34}... | collective-permute-start | bytes 786440 | tf_op jit(solution)/shard_map/ppermute | solution.py:435
  3.9 0.1 collective-permute-start.1
  4.0 6.7 %shard_map.105 = (bf16[5,4,256,512]{3,2,1,0:T(8,128)(2,1)S(1)}, bf16[2,1536,512]{2,1,0:T(8,128)(2,1)S(1)}, bf16[2,512,512]{2,1,0:T(8,128)(2,1)S(1)}, f32[2,8,512...) custom-call(bf16[32,256,512]{2,1,0:T(8,128)(2,1)} %pool.1, ...), custom_call_target="tpu_custom_call" | custom-call | flops 4294967296 | tf_op jit(solution)/shard_map/pallas_call | solution.py:437
  10.7 4.5 %collective-permute-done.1.refs_0_ = bf16[1040,128]{1,0:T(8,128)(2,1)S(1)} collective-permute-done((bf16[1040,128]{1,0:T(8,128)(2,1)S(1)}, bf16[1040,128]{1,0:T(8,128)(2,1)S(1)}, u32[]{:S(2)}, u32[]{:S(2)}) %collective-permute-start.1) | collective-permute-done | bytes 266272 | tf_op jit(solution)/shard_map/ppermute | solution.py:434
  15.2 1.7 %collective-permute-start.5 = (bf16[1040,128]{1,0:T(8,128)(2,1)S(1)}, bf16[1040,128]{1,0:T(8,128)(2,1)S(1)}, u32[]{:S(2)}, u32[]{:S(2)}) collective-permute-start(bf16[1040,128]{1,0:T(8,128)(2,1)S(1)} %collective-permute-done.1.refs_0_), channel_id=1, source_target_pairs={{0,1},{1,0},{2,3},{3,2},{4,5},{5,4},{6,7},{7,6},{8,9},{9,8},{10,11... | collective-permute-start | bytes 798728 | tf_op jit(solution)/shard_map/ppermute | solution.py:389
  16.9 1.5 %collective-permute-start.3 = (bf16[1040,128]{1,0:T(8,128)(2,1)S(1)}, bf16[1040,128]{1,0:T(8,128)(2,1)S(1)}, u32[]{:S(2)}, u32[]{:S(2)}) collective-permute-start(bf16[1040,128]{1,0:T(8,128)(2,1)S(1)} %collective-permute-done.1.refs_0_), channel_id=1, source_target_pairs={{0,2},{1,9},{2,0},{3,11},{4,6},{5,13},{6,4},{7,15},{8,10},{9,1},{1... | collective-permute-start | bytes 798728 | tf_op jit(solution)/shard_map/ppermute | solution.py:400
  18.4 1.6 %collective-permute-start.2 = (bf16[1040,128]{1,0:T(8,128)(2,1)S(1)}, bf16[1040,128]{1,0:T(8,128)(2,1)S(1)}, u32[]{:S(2)}, u32[]{:S(2)}) collective-permute-start(bf16[1040,128]{1,0:T(8,128)(2,1)S(1)} %collective-permute-done.1.refs_0_), channel_id=1, source_target_pairs={{0,8},{1,3},{2,10},{3,1},{4,12},{5,7},{6,14},{7,5},{8,0},{9,11},{1... | collective-permute-start | bytes 798728 | tf_op jit(solution)/shard_map/ppermute | solution.py:400
  20.1 6.2 %shard_map.106.v_in = bf16[5,4,256,512]{3,2,1,0:T(8,128)(2,1)S(1)} custom-call(bf16[5,4,256,512]{3,2,1,0:T(8,128)(2,1)S(1)} %get-tuple-element.49.before, bf16[2,1536,512]{2,1,0:T(8,128)(2,1)S(1)} %get-tuple-element.50.all_taps.refs_8_, bf16[2,512,512]{2,1,0:T(8,128)(2,1)S(1)} %get-tuple-element.51.all_out.refs_9_, ...), custom_call_target="tpu_custom_call", output_to_operand_aliasing={{}: (0, {})} | custom-call | flops 6442450944 | tf_op jit(solution)/shard_map/pallas_call | solution.py:455
  26.3 0.0 collective-permute-done.4.refs_1_
  26.3 0.0 collective-permute-done.5.refs_4_
  26.3 0.0 collective-permute-done.3.refs_3_
  26.3 0.0 collective-permute-done.2.refs_2_
  26.3 0.6 collective-permute-start.8
  27.0 0.1 collective-permute-start.7
  27.1 0.4 collective-permute-start.6
  27.5 1.4 %collective-permute-done.6.refs_5_ = bf16[1024,128]{1,0:T(8,128)(2,1)S(1)} collective-permute-done((bf16[1024,128]{1,0:T(8,128)(2,1)S(1)}, bf16[1024,128]{1,0:T(8,128)(2,1)S(1)}, u32[]{:S(2)}, u32[]{:S(2)}) %collective-permute-start.6) | collective-permute-done | bytes 262176 | tf_op jit(solution)/shard_map/ppermute | solution.py:389
  28.9 0.0 collective-permute-done.8.refs_7_
  28.9 0.0 collective-permute-done.7.refs_6_
  28.9 0.6 shard_map.107
  29.5 2.7 %shard_map.108 = (bf16[5,4,256,512]{3,2,1,0:T(8,128)(2,1)S(1)}, bf16[1,24,1024]{2,1,0:T(8,128)(2,1)S(1)}, f32[24,128]{1,0:T(8,128)S(1)}) custom-call(bf16[5,4,256,512]{3,2,1,0:T(8,128)(2,1)S(1)} %shard_map.106.v_in, bf16[2,1536,512]{2,1,0:T(8,128)(2,1)S(1)} %get-tuple-element.58.all_taps, ...), custom_call_target="tpu_custom_call", output_to_operand_aliasing={{0}: (0, {})} | custom-call | flops 4294967296 | tf_op jit(solution)/shard_map/pallas_call | solution.py:466
  32.2 1.3 %collective-permute-start.9 = (bf16[1,24,1024]{2,1,0:T(8,128)(2,1)S(1)}, bf16[1,24,1024]{2,1,0:T(8,128)(2,1)S(1)}, u32[]{:S(2)}, u32[]{:S(2)}) collective-permute-start(bf16[1,24,1024]{2,1,0:T(8,128)(2,1)S(1)} %get-tuple-element.63), channel_id=1, source_target_pairs={{0,64},{1,65},{2,66},{3,67},{4,68},{5,69},{6,70},{7,71},{8,72},{9,... | collective-permute-start | bytes 147464 | tf_op jit(solution)/shard_map/ppermute | solution.py:490
  33.5 5.0 %shard_map.109 = (bf16[5,4,256,512]{3,2,1,0:T(8,128)(2,1)S(1)}, bf16[2,24,1024]{2,1,0:T(8,128)(2,1)S(1)}, f32[24,128]{1,0:T(8,128)S(1)}) custom-call(bf16[5,4,256,512]{3,2,1,0:T(8,128)(2,1)S(1)} %get-tuple-element.64.v_in, bf16[2,1536,512]{2,1,0:T(8,128)(2,1)S(1)} %get-tuple-element.58.all_taps, ...), custom_call_target="tpu_custom_call", output_to_operand_aliasing={{0}: (0, {})} | custom-call | flops 8589934592 | tf_op jit(solution)/shard_map/pallas_call | solution.py:466
  38.6 5.3 %shard_map.110 = (bf16[5,4,256,512]{3,2,1,0:T(8,128)(2,1)S(1)}, bf16[2,24,1024]{2,1,0:T(8,128)(2,1)S(1)}, f32[8,128]{1,0:T(8,128)S(1)}) custom-call(bf16[5,4,256,512]{3,2,1,0:T(8,128)(2,1)S(1)} %get-tuple-element.66.v_in, bf16[2,1536,512]{2,1,0:T(8,128)(2,1)S(1)} %get-tuple-element.58.all_taps, ...), custom_call_target="tpu_custom_call", output_to_operand_aliasing={{0}: (0, {})} | custom-call | flops 8589934592 | tf_op jit(solution)/shard_map/pallas_call | solution.py:466
  43.8 1.3 %collective-permute-start.10 = (bf16[2,24,1024]{2,1,0:T(8,128)(2,1)S(1)}, bf16[2,24,1024]{2,1,0:T(8,128)(2,1)S(1)}, u32[]{:S(2)}, u32[]{:S(2)}) collective-permute-start(bf16[2,24,1024]{2,1,0:T(8,128)(2,1)S(1)} %get-tuple-element.72), channel_id=1, source_target_pairs={{0,96},{32,64},{1,97},{33,65},{2,98},{34,66},{3,99},{35,67},{4,100... | collective-permute-start | bytes 294920 | tf_op jit(solution)/shard_map/ppermute | solution.py:494
  45.1 0.1 collective-permute-start.12
  45.2 0.0 collective-permute-done.9.codes
  45.3 5.1 %collective-permute-done.12.codes = bf16[2,24,1024]{2,1,0:T(8,128)(2,1)S(1)} collective-permute-done((bf16[2,24,1024]{2,1,0:T(8,128)(2,1)S(1)}, bf16[2,24,1024]{2,1,0:T(8,128)(2,1)S(1)}, u32[]{:S(2)}, u32[]{:S(2)}) %collective-permute-start.12) | collective-permute-done | bytes 98336 | tf_op jit(solution)/shard_map/ppermute | solution.py:492
  50.4 0.0 copy-start
  50.4 1.4 %collective-permute-start.13 = (f32[2,8,128]{2,1,0:T(8,128)S(1)}, f32[2,8,128]{2,1,0:T(8,128)S(1)}, u32[]{:S(2)}, u32[]{:S(2)}) collective-permute-start(f32[2,8,128]{2,1,0:T(8,128)S(1)} %shard_map.113), channel_id=1, source_target_pairs={{96,0},{64,32},{97,1},{65,33},{98,2},{66,34},{99,3},{67,35},{100,4... | collective-permute-start | bytes 24584 | tf_op jit(solution)/shard_map/ppermute | solution.py:499
  51.8 0.0 collective-permute-done.10.codes
  51.8 0.2 shard_map.111.e34
  52.1 20.6 %conditional.1 = (f32[8,128]{1,0:T(8,128)S(1)}) conditional(s32[]{:T(128)} %convert_element_type.7, f32[8,128]{1,0:T(8,128)S(1)} %get-tuple-element.75, f32[8,128]{1,0:T(8,128)S(1)} %get-tuple-element.75), branch_computations={%region_0.0_spmd, %region_1.0_spmd} | conditional | flops 32768 | bytes 561204 | solution.py:502
  52.1 0.3 collective-permute-start
  52.4 2.2 %collective-permute-done = f32[8,128]{1,0:T(8,128)S(1)} collective-permute-done((f32[8,128]{1,0:T(8,128)S(1)}, f32[8,128]{1,0:T(8,128)S(1)}, u32[]{:S(2)}, u32[]{:S(2)}) %collective-permute-start) | collective-permute-done | bytes 4128 | tf_op jit(solution)/shard_map/cond/branch_1_fun/ppermute | solution.py:405
  54.7 18.0 %all_to_all.4 = f32[32,8,128]{2,1,0:T(8,128)S(1)} all-to-all(f32[32,8,128]{2,1,0:T(8,128)S(1)} %broadcast_in_dim.0), channel_id=1, replica_groups=mesh['section'=4,'dp_0'=4,'dp_1'=4,'dp_2'=2] {'dp_0','dp_1','dp_2'}, dimensions={0} | all-to-all | bytes 262144 | tf_op jit(solution)/shard_map/cond/branch_1_fun/all_to_all | solution.py:406
  72.7 3.3 %collective-permute-start.11 = (f32[8,128]{1,0:T(8,128)S(1)}, f32[8,128]{1,0:T(8,128)S(1)}, u32[]{:S(2)}, u32[]{:S(2)}) collective-permute-start(f32[8,128]{1,0:T(8,128)S(1)} %get-tuple-element.81.mine), channel_id=1, source_target_pairs={{0,96},{32,64},{1,97},{33,65},{2,98},{34,66},{3,99},{35,67},{4,100... | collective-permute-start | bytes 12296 | tf_op jit(solution)/shard_map/ppermute | solution.py:503
  76.0 0.7 collective-permute-done.11.cross
  76.8 0.0 collective-permute-done.13.given
  76.8 0.0 copy-done
  76.8 1.3 %shard_map.114 = (f32[2,4,256]{2,1,0:T(4,128)}, f32[8]{0:T(128)}) custom-call(s32[8]{0:T(128)S(1)} %copy-done, f32[8,128]{1,0:T(8,128)S(1)} %get-tuple-element.81.mine, f32[8,128]{1,0:T(8,128)S(1)} %collective-permute-done.11.cross, f32[2,8,128]{2,1,0:T(8,128)S(1)} %collective-permute-done.13.given, f32[1,8,128]{2,1,0:T(8,128)S(1)} %shard_map.112.e0, ...), custom_call_target="tpu_custom_call" | custom-call | tf_op jit(solution)/shard_map/pallas_call | solution.py:505
  (5 shorter events, 0.1 us)
Async XLA Ops:
  1.8 24.5 %collective-permute-start.4 = (bf16[1024,128]{1,0:T(8,128)(2,1)S(1)}, bf16[1024,128]{1,0:T(8,128)(2,1)S(1)}, u32[]{:S(2)}, u32[]{:S(2)}) collective-permute-start(bf16[1024,128]{1,0:T(8,128)(2,1)S(1)} %get-tuple-element.48), channel_id=1, source_target_pairs={{0,32},{32,0},{64,96},{96,64},{1,33},{33,1},{65,97},{97,65},{2,34}... | collective-permute-start | bytes 786440 | tf_op jit(solution)/shard_map/ppermute | solution.py:435
  3.9 11.3 %collective-permute-start.1 = (bf16[1040,128]{1,0:T(8,128)(2,1)S(1)}, bf16[1040,128]{1,0:T(8,128)(2,1)S(1)}, u32[]{:S(2)}, u32[]{:S(2)}) collective-permute-start(bf16[1040,128]{1,0:T(8,128)(2,1)S(1)} %get-tuple-element.45), channel_id=1, source_target_pairs={{0,32},{32,0},{64,96},{96,64},{1,33},{33,1},{65,97},{97,65},{2,34}... | collective-permute-start | bytes 798728 | tf_op jit(solution)/shard_map/ppermute | solution.py:434
  15.2 11.0 %collective-permute-start.5 = (bf16[1040,128]{1,0:T(8,128)(2,1)S(1)}, bf16[1040,128]{1,0:T(8,128)(2,1)S(1)}, u32[]{:S(2)}, u32[]{:S(2)}) collective-permute-start(bf16[1040,128]{1,0:T(8,128)(2,1)S(1)} %collective-permute-done.1.refs_0_), channel_id=1, source_target_pairs={{0,1},{1,0},{2,3},{3,2},{4,5},{5,4},{6,7},{7,6},{8,9},{9,8},{10,11... | collective-permute-start | bytes 798728 | tf_op jit(solution)/shard_map/ppermute | solution.py:389
  16.9 9.4 %collective-permute-start.3 = (bf16[1040,128]{1,0:T(8,128)(2,1)S(1)}, bf16[1040,128]{1,0:T(8,128)(2,1)S(1)}, u32[]{:S(2)}, u32[]{:S(2)}) collective-permute-start(bf16[1040,128]{1,0:T(8,128)(2,1)S(1)} %collective-permute-done.1.refs_0_), channel_id=1, source_target_pairs={{0,2},{1,9},{2,0},{3,11},{4,6},{5,13},{6,4},{7,15},{8,10},{9,1},{1... | collective-permute-start | bytes 798728 | tf_op jit(solution)/shard_map/ppermute | solution.py:400
  18.4 7.9 %collective-permute-start.2 = (bf16[1040,128]{1,0:T(8,128)(2,1)S(1)}, bf16[1040,128]{1,0:T(8,128)(2,1)S(1)}, u32[]{:S(2)}, u32[]{:S(2)}) collective-permute-start(bf16[1040,128]{1,0:T(8,128)(2,1)S(1)} %collective-permute-done.1.refs_0_), channel_id=1, source_target_pairs={{0,8},{1,3},{2,10},{3,1},{4,12},{5,7},{6,14},{7,5},{8,0},{9,11},{1... | collective-permute-start | bytes 798728 | tf_op jit(solution)/shard_map/ppermute | solution.py:400
  26.3 2.6 %collective-permute-start.8 = (bf16[1040,128]{1,0:T(8,128)(2,1)S(1)}, bf16[1040,128]{1,0:T(8,128)(2,1)S(1)}, u32[]{:S(2)}, u32[]{:S(2)}) collective-permute-start(bf16[1040,128]{1,0:T(8,128)(2,1)S(1)} %collective-permute-done.2.refs_2_), channel_id=1, source_target_pairs={{0,1},{1,0},{2,3},{3,2},{4,5},{5,4},{6,7},{7,6},{8,9},{9,8},{10,11... | collective-permute-start | bytes 798728 | tf_op jit(solution)/shard_map/ppermute | solution.py:389
  27.0 1.9 %collective-permute-start.7 = (bf16[1040,128]{1,0:T(8,128)(2,1)S(1)}, bf16[1040,128]{1,0:T(8,128)(2,1)S(1)}, u32[]{:S(2)}, u32[]{:S(2)}) collective-permute-start(bf16[1040,128]{1,0:T(8,128)(2,1)S(1)} %collective-permute-done.3.refs_3_), channel_id=1, source_target_pairs={{0,1},{1,0},{2,3},{3,2},{4,5},{5,4},{6,7},{7,6},{8,9},{9,8},{10,11... | collective-permute-start | bytes 798728 | tf_op jit(solution)/shard_map/ppermute | solution.py:389
  27.1 1.8 %collective-permute-start.6 = (bf16[1024,128]{1,0:T(8,128)(2,1)S(1)}, bf16[1024,128]{1,0:T(8,128)(2,1)S(1)}, u32[]{:S(2)}, u32[]{:S(2)}) collective-permute-start(bf16[1024,128]{1,0:T(8,128)(2,1)S(1)} %collective-permute-done.4.refs_1_), channel_id=1, source_target_pairs={{0,1},{1,0},{2,3},{3,2},{4,5},{5,4},{6,7},{7,6},{8,9},{9,8},{10,11... | collective-permute-start | bytes 786440 | tf_op jit(solution)/shard_map/ppermute | solution.py:389
  32.2 13.0 %collective-permute-start.9 = (bf16[1,24,1024]{2,1,0:T(8,128)(2,1)S(1)}, bf16[1,24,1024]{2,1,0:T(8,128)(2,1)S(1)}, u32[]{:S(2)}, u32[]{:S(2)}) collective-permute-start(bf16[1,24,1024]{2,1,0:T(8,128)(2,1)S(1)} %get-tuple-element.63), channel_id=1, source_target_pairs={{0,64},{1,65},{2,66},{3,67},{4,68},{5,69},{6,70},{7,71},{8,72},{9,... | collective-permute-start | bytes 147464 | tf_op jit(solution)/shard_map/ppermute | solution.py:490
  43.8 8.0 %collective-permute-start.10 = (bf16[2,24,1024]{2,1,0:T(8,128)(2,1)S(1)}, bf16[2,24,1024]{2,1,0:T(8,128)(2,1)S(1)}, u32[]{:S(2)}, u32[]{:S(2)}) collective-permute-start(bf16[2,24,1024]{2,1,0:T(8,128)(2,1)S(1)} %get-tuple-element.72), channel_id=1, source_target_pairs={{0,96},{32,64},{1,97},{33,65},{2,98},{34,66},{3,99},{35,67},{4,100... | collective-permute-start | bytes 294920 | tf_op jit(solution)/shard_map/ppermute | solution.py:494
  45.1 5.3 %collective-permute-start.12 = (bf16[2,24,1024]{2,1,0:T(8,128)(2,1)S(1)}, bf16[2,24,1024]{2,1,0:T(8,128)(2,1)S(1)}, u32[]{:S(2)}, u32[]{:S(2)}) collective-permute-start(bf16[2,24,1024]{2,1,0:T(8,128)(2,1)S(1)} %get-tuple-element.76), channel_id=1, source_target_pairs={{0,96},{96,0},{32,64},{64,32},{1,97},{97,1},{33,65},{65,33},{2,98}... | collective-permute-start | bytes 294920 | tf_op jit(solution)/shard_map/ppermute | solution.py:492
  50.4 26.4 %copy-start = (s32[8]{0:T(128)S(1)}, s32[8]{0:T(128)}, u32[]{:S(2)}) copy-start(s32[8]{0:T(128)} %order.1) | copy-start | bytes 100
  50.4 26.4 %collective-permute-start.13 = (f32[2,8,128]{2,1,0:T(8,128)S(1)}, f32[2,8,128]{2,1,0:T(8,128)S(1)}, u32[]{:S(2)}, u32[]{:S(2)}) collective-permute-start(f32[2,8,128]{2,1,0:T(8,128)S(1)} %shard_map.113), channel_id=1, source_target_pairs={{96,0},{64,32},{97,1},{65,33},{98,2},{66,34},{99,3},{67,35},{100,4... | collective-permute-start | bytes 24584 | tf_op jit(solution)/shard_map/ppermute | solution.py:499
  52.1 2.5 %collective-permute-start = (f32[8,128]{1,0:T(8,128)S(1)}, f32[8,128]{1,0:T(8,128)S(1)}, u32[]{:S(2)}, u32[]{:S(2)}) collective-permute-start(f32[8,128]{1,0:T(8,128)S(1)} %param.1), channel_id=1, source_target_pairs={{0,32},{32,0},{64,96},{96,64},{1,33},{33,1},{65,97},{97,65},{2,34}... | collective-permute-start | bytes 12296 | tf_op jit(solution)/shard_map/cond/branch_1_fun/ppermute | solution.py:405
  72.7 4.0 %collective-permute-start.11 = (f32[8,128]{1,0:T(8,128)S(1)}, f32[8,128]{1,0:T(8,128)S(1)}, u32[]{:S(2)}, u32[]{:S(2)}) collective-permute-start(f32[8,128]{1,0:T(8,128)S(1)} %get-tuple-element.81.mine), channel_id=1, source_target_pairs={{0,96},{32,64},{1,97},{33,65},{2,98},{34,66},{3,99},{35,67},{4,100... | collective-permute-start | bytes 12296 | tf_op jit(solution)/shard_map/ppermute | solution.py:503

commit v7 on v6

--- a/solution.py
+++ b/solution.py
@@ -486,19 +486,18 @@
             blocks=2 * n,
         )(v, *weights, post, codes)[0]
 
-    v, codes, stats = encode((0,), v, (), False)
-    codes_a = lax.ppermute(codes, "section", ((0, 2),))
+    v, first, stats = encode((0,), v, (), False)
     v, codes, stats = encode((1, 2), v, (stats,), False)
     codes_b = lax.ppermute(codes, "section", CROSS)
     v, codes, stats = encode((3, 4), v, (stats,), True)
     codes_c = lax.ppermute(codes, "section", ((0, 3), (1, 2)))
-    codes_a, stats = lax.optimization_barrier((codes_a, stats))
+    first, codes_b, stats = lax.optimization_barrier((first, codes_b, stats))
+    codes_a = lax.ppermute(first, "section", ((0, 2),))
+    e12 = decode((1, 2), v, codes_b)
     e0 = decode((0,), v, codes_a)
-    codes_b, e0 = lax.optimization_barrier((codes_b, e0))
-    e12 = decode((1, 2), v, codes_b)
     given = lax.ppermute(e12, "section", ((3, 0), (2, 1)))
     e34 = decode((3, 4), v, codes_c)
-    stats, e34, encoder = lax.optimization_barrier((stats, e34, encoder))
+    stats, e0, e34, encoder = lax.optimization_barrier((stats, e0, e34, encoder))
     total = lax.cond(encoder == 1, encoder_sum, lambda x: 0.0 * x, stats)
     cross = lax.ppermute(total, "section", ((0, 3), (1, 2)))
     rows_total = float(CLIPS * lax.axis_size(DP) * ROWS)

time: 79.5 us -> 83 us (1.044); the launches traced: 78 us -> 82.6 us
  starting transfers between devices: 15.9 us -> 24.1 us
  waiting for transfers between devices: 14 us -> 10.2 us
    ppermute x1, starting transfers between devices: 1.29 us -> 11.8 us  [on_device(): codes_a = lax.ppermute(first, 'section', ((0, 2),))]
    ppermute x1, waiting for transfers between devices: 5.14 us -> 0.01 us  [on_device(): codes_b = lax.ppermute(codes, 'section', CROSS)]
    ppermute x1, starting transfers between devices: 3.3 us -> 1.28 us  [on_device(): cross = lax.ppermute(total, 'section', ((0, 3), (1, 2)))]
    ppermute x1, waiting for transfers between devices: 0.01 us -> 1.1 us  [on_device(): codes_a = lax.ppermute(first, 'section', ((0, 2),))]
  transfers between devices with their start and end apart: 14 -> 14, of which waited for: 5 -> 5; matrix products, arithmetic and copies ran while one was open for 0% -> 0% of each run, Pallas kernels for 30% -> 22%
where the time goes in v7:
time: 83 us; the launch traced here: 82.6 us
  Pallas kernels  28.8 us (35%)
  starting transfers between devices  24.1 us (29%)
  blocking collectives  18.5 us (22%)
  waiting for transfers between devices  10.2 us (12%)
    all_to_all x1, blocking collectives, encoder_sum(): lax.all_to_all(jnp.broadcast_to(x[None], (n, *x.shape)), DP, 0, 0)  18.5 us
    pallas_call x3, Pallas kernels, encode(): call(functools.partial(encode_body, steps, last), [VM] * (6 + len(before)...  12.8 us
    ppermute x1, starting transfers between devices, on_device(): codes_a = lax.ppermute(first, 'section', ((0, 2),))  11.8 us
    pallas_call x1, Pallas kernels, on_device(): call(functools.partial(start_body, 2), [HB] * 8, [v_kind, *kinds, ((C, 12...  6.71 us
    pallas_call x1, Pallas kernels, on_device(): call(functools.partial(more_body, 2, STEPS), [VM] * 4, [v_kind], blocks=3...  6.19 us
    ppermute x1, waiting for transfers between devices, on_device(): mine = lax.ppermute(piece, 'section', PAIR)  4.51 us
    ppermute x2, starting transfers between devices, within_corner(): return lax.ppermute(x, DP, pairs)  3.18 us
    ppermute x4, starting transfers between devices, shifted(): return lax.ppermute(x, axis, [(i, (i + by) % n) for i in range(n)])  2.81 us
  transfers between devices with their start and end apart: 14, of which 5 were waited for; matrix products, arithmetic and copies ran while one was open for 0% of the time, Pallas kernels for 22%

profile of v7, /device:TPU:1, one launch (start us, length us, event | category | flops | bytes accessed | tf_op | source)
XLA Modules:
  0.0 82.6 jit_solution(728286478789406605)
XLA Ops:
  0.6 1.2 %shard_map.104 = (bf16[1040,128]{1,0:T(8,128)(2,1)S(1)}, bf16[1024,128]{1,0:T(8,128)(2,1)S(1)}) custom-call(bf16[1536,512]{1,0:T(8,128)(2,1)} %bitcast.5, bf16[512,512]{1,0:T(8,128)(2,1)} %bitcast.7, bf16[1,512]{1,0:T(2,128)(2,1)} %gain_hbm.1), custom_call_target="tpu_custom_call" | custom-call | tf_op jit(solution)/shard_map/pallas_call | solution.py:428
  1.8 2.1 %collective-permute-start.4 = (bf16[1024,128]{1,0:T(8,128)(2,1)S(1)}, bf16[1024,128]{1,0:T(8,128)(2,1)S(1)}, u32[]{:S(2)}, u32[]{:S(2)}) collective-permute-start(bf16[1024,128]{1,0:T(8,128)(2,1)S(1)} %get-tuple-element.48), channel_id=1, source_target_pairs={{0,32},{32,0},{64,96},{96,64},{1,33},{33,1},{65,97},{97,65},{2,34}... | collective-permute-start | bytes 786440 | tf_op jit(solution)/shard_map/ppermute | solution.py:435
  3.9 0.1 collective-permute-start.1
  4.0 6.7 %shard_map.105 = (bf16[5,4,256,512]{3,2,1,0:T(8,128)(2,1)S(1)}, bf16[2,1536,512]{2,1,0:T(8,128)(2,1)S(1)}, bf16[2,512,512]{2,1,0:T(8,128)(2,1)S(1)}, f32[2,8,512...) custom-call(bf16[32,256,512]{2,1,0:T(8,128)(2,1)} %pool.1, ...), custom_call_target="tpu_custom_call" | custom-call | flops 4294967296 | tf_op jit(solution)/shard_map/pallas_call | solution.py:437
  10.7 4.5 %collective-permute-done.1.refs_0_ = bf16[1040,128]{1,0:T(8,128)(2,1)S(1)} collective-permute-done((bf16[1040,128]{1,0:T(8,128)(2,1)S(1)}, bf16[1040,128]{1,0:T(8,128)(2,1)S(1)}, u32[]{:S(2)}, u32[]{:S(2)}) %collective-permute-start.1) | collective-permute-done | bytes 266272 | tf_op jit(solution)/shard_map/ppermute | solution.py:434
  15.2 1.7 %collective-permute-start.5 = (bf16[1040,128]{1,0:T(8,128)(2,1)S(1)}, bf16[1040,128]{1,0:T(8,128)(2,1)S(1)}, u32[]{:S(2)}, u32[]{:S(2)}) collective-permute-start(bf16[1040,128]{1,0:T(8,128)(2,1)S(1)} %collective-permute-done.1.refs_0_), channel_id=1, source_target_pairs={{0,1},{1,0},{2,3},{3,2},{4,5},{5,4},{6,7},{7,6},{8,9},{9,8},{10,11... | collective-permute-start | bytes 798728 | tf_op jit(solution)/shard_map/ppermute | solution.py:389
  16.9 1.5 %collective-permute-start.3 = (bf16[1040,128]{1,0:T(8,128)(2,1)S(1)}, bf16[1040,128]{1,0:T(8,128)(2,1)S(1)}, u32[]{:S(2)}, u32[]{:S(2)}) collective-permute-start(bf16[1040,128]{1,0:T(8,128)(2,1)S(1)} %collective-permute-done.1.refs_0_), channel_id=1, source_target_pairs={{0,2},{1,9},{2,0},{3,11},{4,6},{5,13},{6,4},{7,15},{8,10},{9,1},{1... | collective-permute-start | bytes 798728 | tf_op jit(solution)/shard_map/ppermute | solution.py:400
  18.4 1.6 %collective-permute-start.2 = (bf16[1040,128]{1,0:T(8,128)(2,1)S(1)}, bf16[1040,128]{1,0:T(8,128)(2,1)S(1)}, u32[]{:S(2)}, u32[]{:S(2)}) collective-permute-start(bf16[1040,128]{1,0:T(8,128)(2,1)S(1)} %collective-permute-done.1.refs_0_), channel_id=1, source_target_pairs={{0,8},{1,3},{2,10},{3,1},{4,12},{5,7},{6,14},{7,5},{8,0},{9,11},{1... | collective-permute-start | bytes 798728 | tf_op jit(solution)/shard_map/ppermute | solution.py:400
  20.1 6.2 %shard_map.106.v_in = bf16[5,4,256,512]{3,2,1,0:T(8,128)(2,1)S(1)} custom-call(bf16[5,4,256,512]{3,2,1,0:T(8,128)(2,1)S(1)} %get-tuple-element.49.before, bf16[2,1536,512]{2,1,0:T(8,128)(2,1)S(1)} %get-tuple-element.50.all_taps.refs_8_, bf16[2,512,512]{2,1,0:T(8,128)(2,1)S(1)} %get-tuple-element.51.all_out.refs_9_, ...), custom_call_target="tpu_custom_call", output_to_operand_aliasing={{}: (0, {})} | custom-call | flops 6442450944 | tf_op jit(solution)/shard_map/pallas_call | solution.py:455
  26.3 0.0 collective-permute-done.4.refs_1_
  26.3 0.0 collective-permute-done.5.refs_4_
  26.3 0.0 collective-permute-done.3.refs_3_
  26.3 0.0 collective-permute-done.2.refs_2_
  26.3 0.6 collective-permute-start.8
  27.0 0.1 collective-permute-start.7
  27.1 0.4 collective-permute-start.6
  27.5 1.4 %collective-permute-done.6.refs_5_ = bf16[1024,128]{1,0:T(8,128)(2,1)S(1)} collective-permute-done((bf16[1024,128]{1,0:T(8,128)(2,1)S(1)}, bf16[1024,128]{1,0:T(8,128)(2,1)S(1)}, u32[]{:S(2)}, u32[]{:S(2)}) %collective-permute-start.6) | collective-permute-done | bytes 262176 | tf_op jit(solution)/shard_map/ppermute | solution.py:389
  28.9 0.0 collective-permute-done.8.refs_7_
  28.9 0.0 collective-permute-done.7.refs_6_
  28.9 0.6 shard_map.107
  29.5 2.7 %shard_map.108 = (bf16[5,4,256,512]{3,2,1,0:T(8,128)(2,1)S(1)}, bf16[1,24,1024]{2,1,0:T(8,128)(2,1)S(1)}, f32[24,128]{1,0:T(8,128)S(1)}) custom-call(bf16[5,4,256,512]{3,2,1,0:T(8,128)(2,1)S(1)} %shard_map.106.v_in, bf16[2,1536,512]{2,1,0:T(8,128)(2,1)S(1)} %get-tuple-element.58.all_taps, ...), custom_call_target="tpu_custom_call", output_to_operand_aliasing={{0}: (0, {})} | custom-call | flops 4294967296 | tf_op jit(solution)/shard_map/pallas_call | solution.py:466
  32.2 5.0 %shard_map.109 = (bf16[5,4,256,512]{3,2,1,0:T(8,128)(2,1)S(1)}, bf16[2,24,1024]{2,1,0:T(8,128)(2,1)S(1)}, f32[24,128]{1,0:T(8,128)S(1)}) custom-call(bf16[5,4,256,512]{3,2,1,0:T(8,128)(2,1)S(1)} %get-tuple-element.64.v_in, bf16[2,1536,512]{2,1,0:T(8,128)(2,1)S(1)} %get-tuple-element.58.all_taps, ...), custom_call_target="tpu_custom_call", output_to_operand_aliasing={{0}: (0, {})} | custom-call | flops 8589934592 | tf_op jit(solution)/shard_map/pallas_call | solution.py:466
  37.3 0.3 collective-permute-start.9
  37.5 5.1 %shard_map.110 = (bf16[5,4,256,512]{3,2,1,0:T(8,128)(2,1)S(1)}, bf16[2,24,1024]{2,1,0:T(8,128)(2,1)S(1)}, f32[8,128]{1,0:T(8,128)S(1)}) custom-call(bf16[5,4,256,512]{3,2,1,0:T(8,128)(2,1)S(1)} %get-tuple-element.67.v_in, bf16[2,1536,512]{2,1,0:T(8,128)(2,1)S(1)} %get-tuple-element.58.all_taps, ...), custom_call_target="tpu_custom_call", output_to_operand_aliasing={{0}: (0, {})} | custom-call | flops 8589934592 | tf_op jit(solution)/shard_map/pallas_call | solution.py:466
  42.6 1.3 %collective-permute-start.11 = (bf16[2,24,1024]{2,1,0:T(8,128)(2,1)S(1)}, bf16[2,24,1024]{2,1,0:T(8,128)(2,1)S(1)}, u32[]{:S(2)}, u32[]{:S(2)}) collective-permute-start(bf16[2,24,1024]{2,1,0:T(8,128)(2,1)S(1)} %get-tuple-element.74), channel_id=1, source_target_pairs={{0,96},{32,64},{1,97},{33,65},{2,98},{34,66},{3,99},{35,67},{4,100... | collective-permute-start | bytes 294920 | tf_op jit(solution)/shard_map/ppermute | solution.py:493
  43.9 0.0 collective-permute-done.9.codes
  44.0 1.3 %collective-permute-start.13 = (f32[2,8,128]{2,1,0:T(8,128)S(1)}, f32[2,8,128]{2,1,0:T(8,128)S(1)}, u32[]{:S(2)}, u32[]{:S(2)}) collective-permute-start(f32[2,8,128]{2,1,0:T(8,128)S(1)} %shard_map.113), channel_id=1, source_target_pairs={{96,0},{64,32},{97,1},{65,33},{98,2},{66,34},{99,3},{67,35},{100,4... | collective-permute-start | bytes 24584 | tf_op jit(solution)/shard_map/ppermute | solution.py:498
  45.3 11.8 %collective-permute-start.10 = (bf16[1,24,1024]{2,1,0:T(8,128)(2,1)S(1)}, bf16[1,24,1024]{2,1,0:T(8,128)(2,1)S(1)}, u32[]{:S(2)}, u32[]{:S(2)}) collective-permute-start(bf16[1,24,1024]{2,1,0:T(8,128)(2,1)S(1)} %get-tuple-element.73), channel_id=1, source_target_pairs={{0,64},{1,65},{2,66},{3,67},{4,68},{5,69},{6,70},{7,71},{8,72},{9,... | collective-permute-start | bytes 147464 | tf_op jit(solution)/shard_map/ppermute | solution.py:495
  57.1 0.0 collective-permute-done.11.codes
  57.1 0.0 copy-start
  57.1 1.1 %collective-permute-done.10.codes = bf16[1,24,1024]{2,1,0:T(8,128)(2,1)S(1)} collective-permute-done((bf16[1,24,1024]{2,1,0:T(8,128)(2,1)S(1)}, bf16[1,24,1024]{2,1,0:T(8,128)(2,1)S(1)}, u32[]{:S(2)}, u32[]{:S(2)}) %collective-permute-start.10) | collective-permute-done | bytes 49184 | tf_op jit(solution)/shard_map/ppermute | solution.py:495
  58.2 21.0 %conditional.1 = (f32[8,128]{1,0:T(8,128)S(1)}) conditional(s32[]{:T(128)} %convert_element_type.7, f32[8,128]{1,0:T(8,128)S(1)} %get-tuple-element.77, f32[8,128]{1,0:T(8,128)S(1)} %get-tuple-element.77), branch_computations={%region_0.0_spmd, %region_1.0_spmd} | conditional | flops 32768 | bytes 561204 | solution.py:501
  58.2 0.0 collective-permute-start
  58.2 2.5 %collective-permute-done = f32[8,128]{1,0:T(8,128)S(1)} collective-permute-done((f32[8,128]{1,0:T(8,128)S(1)}, f32[8,128]{1,0:T(8,128)S(1)}, u32[]{:S(2)}, u32[]{:S(2)}) %collective-permute-start) | collective-permute-done | bytes 4128 | tf_op jit(solution)/shard_map/cond/branch_1_fun/ppermute | solution.py:405
  60.7 18.5 %all_to_all.4 = f32[32,8,128]{2,1,0:T(8,128)S(1)} all-to-all(f32[32,8,128]{2,1,0:T(8,128)S(1)} %broadcast_in_dim.0), channel_id=1, replica_groups=mesh['section'=4,'dp_0'=4,'dp_1'=4,'dp_2'=2] {'dp_0','dp_1','dp_2'}, dimensions={0} | all-to-all | bytes 262144 | tf_op jit(solution)/shard_map/cond/branch_1_fun/all_to_all | solution.py:406
  79.3 1.3 %collective-permute-start.12 = (f32[8,128]{1,0:T(8,128)S(1)}, f32[8,128]{1,0:T(8,128)S(1)}, u32[]{:S(2)}, u32[]{:S(2)}) collective-permute-start(f32[8,128]{1,0:T(8,128)S(1)} %get-tuple-element.81.mine), channel_id=1, source_target_pairs={{0,96},{32,64},{1,97},{33,65},{2,98},{34,66},{3,99},{35,67},{4,100... | collective-permute-start | bytes 12296 | tf_op jit(solution)/shard_map/ppermute | solution.py:502
  80.6 0.0 collective-permute-done.13.given
  80.6 0.7 collective-permute-done.12.cross
  81.3 0.0 copy-done
  81.3 1.3 %shard_map.114 = (f32[2,4,256]{2,1,0:T(4,128)}, f32[8]{0:T(128)}) custom-call(s32[8]{0:T(128)S(1)} %copy-done, f32[8,128]{1,0:T(8,128)S(1)} %get-tuple-element.81.mine, f32[8,128]{1,0:T(8,128)S(1)} %collective-permute-done.12.cross, f32[2,8,128]{2,1,0:T(8,128)S(1)} %collective-permute-done.13.given, f32[1,8,128]{2,1,0:T(8,128)S(1)} %shard_map.111.e0, ...), custom_call_target="tpu_custom_call" | custom-call | tf_op jit(solution)/shard_map/pallas_call | solution.py:504
  (6 shorter events, 0.1 us)
Async XLA Ops:
  1.8 24.5 %collective-permute-start.4 = (bf16[1024,128]{1,0:T(8,128)(2,1)S(1)}, bf16[1024,128]{1,0:T(8,128)(2,1)S(1)}, u32[]{:S(2)}, u32[]{:S(2)}) collective-permute-start(bf16[1024,128]{1,0:T(8,128)(2,1)S(1)} %get-tuple-element.48), channel_id=1, source_target_pairs={{0,32},{32,0},{64,96},{96,64},{1,33},{33,1},{65,97},{97,65},{2,34}... | collective-permute-start | bytes 786440 | tf_op jit(solution)/shard_map/ppermute | solution.py:435
  3.9 11.3 %collective-permute-start.1 = (bf16[1040,128]{1,0:T(8,128)(2,1)S(1)}, bf16[1040,128]{1,0:T(8,128)(2,1)S(1)}, u32[]{:S(2)}, u32[]{:S(2)}) collective-permute-start(bf16[1040,128]{1,0:T(8,128)(2,1)S(1)} %get-tuple-element.45), channel_id=1, source_target_pairs={{0,32},{32,0},{64,96},{96,64},{1,33},{33,1},{65,97},{97,65},{2,34}... | collective-permute-start | bytes 798728 | tf_op jit(solution)/shard_map/ppermute | solution.py:434
  15.2 11.0 %collective-permute-start.5 = (bf16[1040,128]{1,0:T(8,128)(2,1)S(1)}, bf16[1040,128]{1,0:T(8,128)(2,1)S(1)}, u32[]{:S(2)}, u32[]{:S(2)}) collective-permute-start(bf16[1040,128]{1,0:T(8,128)(2,1)S(1)} %collective-permute-done.1.refs_0_), channel_id=1, source_target_pairs={{0,1},{1,0},{2,3},{3,2},{4,5},{5,4},{6,7},{7,6},{8,9},{9,8},{10,11... | collective-permute-start | bytes 798728 | tf_op jit(solution)/shard_map/ppermute | solution.py:389
  16.9 9.4 %collective-permute-start.3 = (bf16[1040,128]{1,0:T(8,128)(2,1)S(1)}, bf16[1040,128]{1,0:T(8,128)(2,1)S(1)}, u32[]{:S(2)}, u32[]{:S(2)}) collective-permute-start(bf16[1040,128]{1,0:T(8,128)(2,1)S(1)} %collective-permute-done.1.refs_0_), channel_id=1, source_target_pairs={{0,2},{1,9},{2,0},{3,11},{4,6},{5,13},{6,4},{7,15},{8,10},{9,1},{1... | collective-permute-start | bytes 798728 | tf_op jit(solution)/shard_map/ppermute | solution.py:400
  18.4 7.9 %collective-permute-start.2 = (bf16[1040,128]{1,0:T(8,128)(2,1)S(1)}, bf16[1040,128]{1,0:T(8,128)(2,1)S(1)}, u32[]{:S(2)}, u32[]{:S(2)}) collective-permute-start(bf16[1040,128]{1,0:T(8,128)(2,1)S(1)} %collective-permute-done.1.refs_0_), channel_id=1, source_target_pairs={{0,8},{1,3},{2,10},{3,1},{4,12},{5,7},{6,14},{7,5},{8,0},{9,11},{1... | collective-permute-start | bytes 798728 | tf_op jit(solution)/shard_map/ppermute | solution.py:400
  26.3 2.6 %collective-permute-start.8 = (bf16[1040,128]{1,0:T(8,128)(2,1)S(1)}, bf16[1040,128]{1,0:T(8,128)(2,1)S(1)}, u32[]{:S(2)}, u32[]{:S(2)}) collective-permute-start(bf16[1040,128]{1,0:T(8,128)(2,1)S(1)} %collective-permute-done.2.refs_2_), channel_id=1, source_target_pairs={{0,1},{1,0},{2,3},{3,2},{4,5},{5,4},{6,7},{7,6},{8,9},{9,8},{10,11... | collective-permute-start | bytes 798728 | tf_op jit(solution)/shard_map/ppermute | solution.py:389
  27.0 1.9 %collective-permute-start.7 = (bf16[1040,128]{1,0:T(8,128)(2,1)S(1)}, bf16[1040,128]{1,0:T(8,128)(2,1)S(1)}, u32[]{:S(2)}, u32[]{:S(2)}) collective-permute-start(bf16[1040,128]{1,0:T(8,128)(2,1)S(1)} %collective-permute-done.3.refs_3_), channel_id=1, source_target_pairs={{0,1},{1,0},{2,3},{3,2},{4,5},{5,4},{6,7},{7,6},{8,9},{9,8},{10,11... | collective-permute-start | bytes 798728 | tf_op jit(solution)/shard_map/ppermute | solution.py:389
  27.1 1.8 %collective-permute-start.6 = (bf16[1024,128]{1,0:T(8,128)(2,1)S(1)}, bf16[1024,128]{1,0:T(8,128)(2,1)S(1)}, u32[]{:S(2)}, u32[]{:S(2)}) collective-permute-start(bf16[1024,128]{1,0:T(8,128)(2,1)S(1)} %collective-permute-done.4.refs_1_), channel_id=1, source_target_pairs={{0,1},{1,0},{2,3},{3,2},{4,5},{5,4},{6,7},{7,6},{8,9},{9,8},{10,11... | collective-permute-start | bytes 786440 | tf_op jit(solution)/shard_map/ppermute | solution.py:389
  37.3 6.7 %collective-permute-start.9 = (bf16[2,24,1024]{2,1,0:T(8,128)(2,1)S(1)}, bf16[2,24,1024]{2,1,0:T(8,128)(2,1)S(1)}, u32[]{:S(2)}, u32[]{:S(2)}) collective-permute-start(bf16[2,24,1024]{2,1,0:T(8,128)(2,1)S(1)} %get-tuple-element.66), channel_id=1, source_target_pairs={{0,96},{96,0},{32,64},{64,32},{1,97},{97,1},{33,65},{65,33},{2,98}... | collective-permute-start | bytes 294920 | tf_op jit(solution)/shard_map/ppermute | solution.py:491
  42.6 14.5 %collective-permute-start.11 = (bf16[2,24,1024]{2,1,0:T(8,128)(2,1)S(1)}, bf16[2,24,1024]{2,1,0:T(8,128)(2,1)S(1)}, u32[]{:S(2)}, u32[]{:S(2)}) collective-permute-start(bf16[2,24,1024]{2,1,0:T(8,128)(2,1)S(1)} %get-tuple-element.74), channel_id=1, source_target_pairs={{0,96},{32,64},{1,97},{33,65},{2,98},{34,66},{3,99},{35,67},{4,100... | collective-permute-start | bytes 294920 | tf_op jit(solution)/shard_map/ppermute | solution.py:493
  44.0 36.6 %collective-permute-start.13 = (f32[2,8,128]{2,1,0:T(8,128)S(1)}, f32[2,8,128]{2,1,0:T(8,128)S(1)}, u32[]{:S(2)}, u32[]{:S(2)}) collective-permute-start(f32[2,8,128]{2,1,0:T(8,128)S(1)} %shard_map.113), channel_id=1, source_target_pairs={{96,0},{64,32},{97,1},{65,33},{98,2},{66,34},{99,3},{67,35},{100,4... | collective-permute-start | bytes 24584 | tf_op jit(solution)/shard_map/ppermute | solution.py:498
  45.3 13.0 %collective-permute-start.10 = (bf16[1,24,1024]{2,1,0:T(8,128)(2,1)S(1)}, bf16[1,24,1024]{2,1,0:T(8,128)(2,1)S(1)}, u32[]{:S(2)}, u32[]{:S(2)}) collective-permute-start(bf16[1,24,1024]{2,1,0:T(8,128)(2,1)S(1)} %get-tuple-element.73), channel_id=1, source_target_pairs={{0,64},{1,65},{2,66},{3,67},{4,68},{5,69},{6,70},{7,71},{8,72},{9,... | collective-permute-start | bytes 147464 | tf_op jit(solution)/shard_map/ppermute | solution.py:495
  57.1 24.2 %copy-start = (s32[8]{0:T(128)S(1)}, s32[8]{0:T(128)}, u32[]{:S(2)}) copy-start(s32[8]{0:T(128)} %order.1) | copy-start | bytes 100
  58.2 2.5 %collective-permute-start = (f32[8,128]{1,0:T(8,128)S(1)}, f32[8,128]{1,0:T(8,128)S(1)}, u32[]{:S(2)}, u32[]{:S(2)}) collective-permute-start(f32[8,128]{1,0:T(8,128)S(1)} %param.1), channel_id=1, source_target_pairs={{0,32},{32,0},{64,96},{96,64},{1,33},{33,1},{65,97},{97,65},{2,34}... | collective-permute-start | bytes 12296 | tf_op jit(solution)/shard_map/cond/branch_1_fun/ppermute | solution.py:405
  79.3 2.0 %collective-permute-start.12 = (f32[8,128]{1,0:T(8,128)S(1)}, f32[8,128]{1,0:T(8,128)S(1)}, u32[]{:S(2)}, u32[]{:S(2)}) collective-permute-start(f32[8,128]{1,0:T(8,128)S(1)} %get-tuple-element.81.mine), channel_id=1, source_target_pairs={{0,96},{32,64},{1,97},{33,65},{2,98},{34,66},{3,99},{35,67},{4,100... | collective-permute-start | bytes 12296 | tf_op jit(solution)/shard_map/ppermute | solution.py:502
